TPU v7x, 256 devices: a whole 4x4x8 slice. The times are simulated.
256 devices in a mesh: seq: 16 (over y, x), grp: 16 (over z, core).
Axes of the slice: x: 4, y: 4, z: 8, core: 2. Of those that a mesh axis runs over, the one named last changes fastest.
Arguments:
- actions: int32 [32, 7], P('grp'), may hold values from 0 to 255
- lengths: int32 [32], P('grp'), may hold values from 2048 to 4096
- embed: bfloat16 [256, 4096], replicated, may hold values from -6 to 6
- attn_gain: float32 [4096], replicated, may hold values from 0.1 to 1.9
- w_query: bfloat16 [4096, 4096], P('grp', 'seq'), may hold values from -0.09375 to 0.09375
- w_key: bfloat16 [4096, 4096], P('grp', 'seq'), may hold values from -0.140625 to 0.140625
- w_value: bfloat16 [4096, 4096], P('grp', 'seq'), may hold values from -0.09375 to 0.09375
- w_out: bfloat16 [4096, 4096], P('grp', 'seq'), may hold values from -0.09375 to 0.09375
- key_cache: bfloat16 [32, 4096, 4096], P('grp', 'seq'), may hold values from -136 to 136
- value_cache: bfloat16 [32, 4096, 4096], P('grp', 'seq'), may hold values from -6 to 6
- final_gain: float32 [4096], replicated, may hold values from 0.1 to 1.9
- head: bfloat16 [256, 4096], P('seq'), may hold values from -0.25 to 0.25
Outputs:
- logprob: float32 [32, 7, 256], P('grp', None, 'seq')
Inputs may be any that keep to these rules, and one draw needn't show every extreme that they name: Robot r's prompt occupies cache positions 0 to lengths[r] - 1.
All inputs are finite; a program needn't handle non-finite values.
Results may differ from a plain program's by a relative error of at most 0.008.
Values may be sent and summed in bfloat16 or wider, within the bound.
No kernel may reach another device: no remote copies, remote signals or barrier semaphores. Data moves between devices by JAX's collectives and lax.ppermute only.
A program may use at most 64 MiB of HBM per device.

v0:
```python
import jax
import jax.numpy as jnp
from jax import lax
from jax.sharding import Mesh
from jax.sharding import PartitionSpec as P

HEAD_DIM = 128
SEQ = ("seq_0", "seq_1")


def split_up(shard, dim, devices):
    before, after = (shard.shape[:dim], shard.shape[dim + 1 :])
    return jnp.moveaxis(shard.reshape(*before, devices, -1, *after), dim, 0)


def sum_at_owner(shard, axis, dim):
    pieces = split_up(shard, dim, lax.axis_size(axis))
    arrived = lax.all_to_all(pieces, axis, split_axis=0, concat_axis=0, tiled=True)
    return arrived.sum(axis=0)


def sent_together(arrays, axis, dim, along):
    widths = [a.shape[along] for a in arrays]
    both = jnp.concatenate(arrays, axis=along)
    out = lax.all_gather(both, axis, axis=dim, tiled=True)
    return tuple(jnp.split(out, [sum(widths[:k]) for k in range(1, len(widths))], axis=along))


def all_in_one(shard, axis):
    leaves = jax.tree.leaves(shard)
    order = sorted(range(len(leaves)), key=lambda k: -leaves[k].size)
    width = (1, *leaves[order[0]].shape)[-1]
    lines = [
        jnp.pad(leaves[k].reshape(-1), (0, -leaves[k].size % width)).reshape(-1, width)
        for k in order
    ]
    both, at, found = (lax.all_gather(jnp.concatenate(lines), axis), 0, {})
    for k, line in zip(order, lines):
        share = both[:, at : at + len(line)].reshape(len(both), -1)
        found[k] = share[:, : leaves[k].size].reshape(-1, *leaves[k].shape)
        at += len(line)
    numbers = iter(range(len(leaves)))
    return jax.tree.map(lambda _: found[next(numbers)], shard)


def merged_by_axis(shard, axes, combine):
    for axis in axes:
        pieces = all_in_one(shard, axis)
        shard = jax.tree.map(lambda part: part[0], pieces)
        for k in range(1, lax.axis_size(axis)):
            shard = combine(shard, jax.tree.map(lambda part: part[k], pieces))
    return shard


def sum_at_owner_2(shard, axis, dim):
    devices = lax.axis_size(axis)
    pieces = lax.all_to_all(split_up(shard, dim, devices), axis, 0, 0, tiled=True)
    return jnp.sum(pieces.astype(jnp.float32), axis=0)


def joined_along(pieces, dim):
    pieces = jnp.moveaxis(pieces, 0, dim)
    lengths = pieces.shape
    return pieces.reshape(*lengths[:dim], lengths[dim] * lengths[dim + 1], *lengths[dim + 2 :])


def copy_for_each(shard, axis):
    devices = lax.axis_size(axis)
    return lax.all_to_all(
        jnp.broadcast_to(shard[None], (devices, *shard.shape)), axis, 0, 0, tiled=True
    )


def collect(shard, axis, dim):
    return joined_along(copy_for_each(shard, axis), dim)


def gathered_once(shard, axis):
    leaves = jax.tree.leaves(shard)
    order = sorted(range(len(leaves)), key=lambda k: -leaves[k].size)
    width = (1, *leaves[order[0]].shape)[-1]
    lines = [
        jnp.pad(leaves[k].reshape(-1), (0, -leaves[k].size % width)).reshape(-1, width)
        for k in order
    ]
    both, at, found = (copy_for_each(jnp.concatenate(lines), axis), 0, {})
    for k, line in zip(order, lines):
        share = both[:, at : at + len(line)].reshape(len(both), -1)
        found[k] = share[:, : leaves[k].size].reshape(-1, *leaves[k].shape)
        at += len(line)
    numbers = iter(range(len(leaves)))
    return jax.tree.map(lambda _: found[next(numbers)], shard)


def combined_pairwise(pieces, combine):
    while len(jax.tree.leaves(pieces)[0]) > 1:
        pieces = jax.vmap(combine)(
            *(jax.tree.map(lambda part: part[side::2], pieces) for side in (0, 1))
        )
    return jax.tree.map(lambda part: part[0], pieces)


def combined_all(shard, axis, combine):
    pieces = gathered_once(shard, axis)
    return combined_pairwise(pieces, combine)


def rms_scale(values, gain):
    mean_square = jnp.mean(values * values, axis=-1, keepdims=True)
    return values * lax.rsqrt(mean_square + 1e-05) * gain


def rotate(values, places):
    half = values.shape[-1] // 2
    freq = 10000.0 ** (-(jnp.arange(half, dtype=jnp.float32) * 2.0 / values.shape[-1]))
    angle = places[..., None, None] * freq
    first = values[..., :half]
    second = values[..., half:]
    cosine = jnp.cos(angle)
    sine = jnp.sin(angle)
    return jnp.concatenate(
        [first * cosine - second * sine, second * cosine + first * sine], axis=-1
    )


def join_softmax(left, right):
    top = jnp.maximum(left[0], right[0])
    left_factor = jnp.exp(left[0] - top)
    right_factor = jnp.exp(right[0] - top)
    total = left[1] * left_factor + right[1] * right_factor
    acc = left[2] * left_factor[..., None] + right[2] * right_factor[..., None]
    return (top, total, acc)


def join_totals(left, right):
    top = jnp.maximum(left[0], right[0])
    return (top, left[1] * jnp.exp(left[0] - top) + right[1] * jnp.exp(right[0] - top))


def on_device(
    actions,
    lengths,
    embed,
    attn_gain,
    w_query,
    w_key,
    w_value,
    w_out,
    key_cache,
    value_cache,
    final_gain,
    head,
):
    seq_index = lax.axis_index(SEQ)
    seq_count = lax.axis_size(SEQ)
    robots, steps = actions.shape
    prompt_dev = key_cache.shape[1]
    width = key_cache.shape[2]
    col_block = w_query.shape[1]
    head_dim = HEAD_DIM
    heads = width // head_dim
    local_heads = col_block // head_dim
    scale = head_dim ** (-0.5)
    bins = jnp.arange(embed.shape[0], dtype=jnp.int32)
    onehot = (actions[:, :, None] == bins[None, None, :]).astype(jnp.bfloat16)
    inputs = jnp.einsum("rtb,bd->rtd", onehot, embed, preferred_element_type=jnp.float32)
    normed = rms_scale(inputs, attn_gain).astype(jnp.bfloat16)
    places = (lengths[:, None] + jnp.arange(steps, dtype=jnp.int32)[None, :]).astype(jnp.float32)
    prompt_places = seq_index * prompt_dev + jnp.arange(prompt_dev, dtype=jnp.int32)
    prompt_valid = prompt_places[None, :] < lengths[:, None]
    cache_keys = key_cache.reshape(robots, prompt_dev, heads, head_dim)
    cache_values = value_cache.reshape(robots, prompt_dev, heads, head_dim)
    empty = jnp.zeros((robots, 0, heads, head_dim), jnp.bfloat16)
    window_keys = empty
    window_values = empty
    rows = robots * steps
    block_norm = normed.reshape(rows, width)
    spread_rows = lax.all_to_all(block_norm, "grp", split_axis=1, concat_axis=0, tiled=True)
    terms = jnp.concatenate(
        [
            jnp.dot(spread_rows, w_query, preferred_element_type=jnp.float32),
            jnp.dot(spread_rows, w_key, preferred_element_type=jnp.float32),
            jnp.dot(spread_rows, w_value, preferred_element_type=jnp.float32),
        ],
        axis=1,
    )
    sums = sum_at_owner(terms, "grp", 0)

    def heads_of(flat):
        return flat.reshape(robots, steps, local_heads, head_dim)

    query = (
        rotate(heads_of(sums[:, :col_block]), places).astype(jnp.bfloat16).reshape(rows, col_block)
    )
    key = (
        rotate(heads_of(sums[:, col_block : 2 * col_block]), places)
        .astype(jnp.bfloat16)
        .reshape(rows, col_block)
    )
    value = sums[:, 2 * col_block :].astype(jnp.bfloat16)
    query, key, value = sent_together((query, key, value), SEQ, 1, 0)
    query = query.reshape(robots, steps, heads, head_dim)
    window_keys = jnp.concatenate(
        [window_keys, key.reshape(robots, steps, heads, head_dim)], axis=1
    )
    window_values = jnp.concatenate(
        [window_values, value.reshape(robots, steps, heads, head_dim)], axis=1
    )
    seen = 0 + steps
    window_index = jnp.arange(seen, dtype=jnp.int32)
    step_index = 0 + jnp.arange(steps, dtype=jnp.int32)
    window_valid = (window_index[None, :] <= step_index[:, None]) & (
        window_index % seq_count == seq_index
    )[None, :]
    prompt_mask = prompt_valid[:, None, None, :]
    window_mask = window_valid[None, :, None, :]
    prompt_scores = (
        jnp.einsum("rthd,rphd->rthp", query, cache_keys, preferred_element_type=jnp.float32) * scale
    )
    window_scores = (
        jnp.einsum("rthd,rjhd->rthj", query, window_keys, preferred_element_type=jnp.float32)
        * scale
    )
    prompt_scores = jnp.where(prompt_mask, prompt_scores, -1e30)
    window_scores = jnp.where(window_mask, window_scores, -1e30)
    local_max = jnp.maximum(jnp.max(prompt_scores, axis=-1), jnp.max(window_scores, axis=-1))
    prompt_e = jnp.where(prompt_mask, jnp.exp(prompt_scores - local_max[..., None]), 0.0)
    window_e = jnp.where(window_mask, jnp.exp(window_scores - local_max[..., None]), 0.0)
    total = jnp.sum(prompt_e, axis=-1) + jnp.sum(window_e, axis=-1)
    acc = jnp.einsum(
        "rthp,rphd->rthd",
        prompt_e.astype(jnp.bfloat16),
        cache_values,
        preferred_element_type=jnp.float32,
    )
    acc = acc + jnp.einsum(
        "rthj,rjhd->rthd",
        window_e.astype(jnp.bfloat16),
        window_values,
        preferred_element_type=jnp.float32,
    )
    total, acc = (total, acc)
    top, total, acc = merged_by_axis((local_max, total, acc), SEQ, join_softmax)
    attended = (acc / total[..., None]).astype(jnp.bfloat16).reshape(rows, width)
    spread_attended = lax.all_to_all(attended, "grp", split_axis=1, concat_axis=0, tiled=True)
    out_terms = jnp.dot(spread_attended, w_out, preferred_element_type=jnp.float32)
    out_part = sum_at_owner_2(out_terms.astype(jnp.bfloat16), "grp", 0)
    branch = collect(out_part, SEQ, 1)
    residual = inputs.reshape(rows, width) + branch
    final = rms_scale(residual, final_gain).astype(jnp.bfloat16)
    logits = lax.dot_general(
        final, head, (((1,), (1,)), ((), ())), preferred_element_type=jnp.float32
    )
    row_max = jnp.max(logits, axis=-1)
    local_total = jnp.sum(jnp.exp(logits - row_max[:, None]), axis=-1)
    top_logit, exp_total = combined_all((row_max, local_total), SEQ, join_totals)
    logprob = logits - top_logit[:, None] - jnp.log(exp_total)[:, None]
    result = logprob.reshape(robots, steps, logits.shape[1])
    return result


def solution(mesh):
    torus = Mesh(mesh.devices.reshape(4, 4, mesh.shape["grp"]), ("seq_0", "seq_1", "grp"))
    in_specs = (
        P("grp", None),
        P("grp"),
        P(),
        P(),
        P("grp", SEQ),
        P("grp", SEQ),
        P("grp", SEQ),
        P("grp", SEQ),
        P("grp", SEQ, None),
        P("grp", SEQ, None),
        P(),
        P(SEQ, None),
    )
    out_specs = P("grp", None, SEQ)
    return jax.shard_map(
        on_device, mesh=torus, in_specs=in_specs, out_specs=out_specs, check_vma=False
    )
```

profile of v0, /device:TPU:32, one launch (start us, length us, event | category | flops | bytes accessed | tf_op | source)
XLA Modules:
  0.0 184.0 jit_solution(1616942880006318692)
XLA Ops:
  0.0 1.6 copy-done
  1.6 1.2 multiply_reduce_fusion.1
  3.8 15.8 %all_to_all.55 = bf16[14,16,256]{2,0,1:T(8,128)(2,1)S(1)} all-to-all(bf16[14,16,256]{2,0,1:T(8,128)(2,1)S(1)} %copy.58), channel_id=1, replica_groups=mesh['seq_0'=4,'seq_1'=4,'grp'=16] {'grp'}, dimensions={1} | all-to-all | bytes 229376 | tf_op jit(solution)/shard_map/all_to_all | solution.py:178
  22.2 5.4 %all-to-all-start.1 = ((f32[16,14,768]{2,1,0:T(8,128)}), f32[16,14,768]{2,1,0:T(8,128)}, u32[]{:S(2)}, u32[]{:S(2)}) async-start(f32[16,14,768]{2,1,0:T(8,128)} %reshape.569), calls=%async_computation.1 | async-start | bytes 1572864 | tf_op jit(solution)/shard_map/all_to_all | solution.py:18
  27.9 18.9 %all-to-all-done.1 = f32[16,14,768]{2,1,0:T(8,128)} async-done(((f32[16,14,768]{2,1,0:T(8,128)}), f32[16,14,768]{2,1,0:T(8,128)}, u32[]{:S(2)}, u32[]{:S(2)}) %all-to-all-start.1) | async-done | bytes 688160 | tf_op jit(solution)/shard_map/all_to_all | solution.py:18
  46.7 1.2 reduce_sum.64
  48.3 25.1 %all_gather.15 = bf16[42,4096]{1,0:T(8,128)(2,1)S(1)} all-gather(bf16[42,256]{1,0:T(8,128)(2,1)S(1)} %pad_maximum_fusion.3), channel_id=1, replica_groups=mesh['seq_0'=4,'seq_1'=4,'grp'=16] {'seq_0','seq_1'}, dimensions={1}, use_global_device_ids=true | all-gather | bytes 365568 | tf_op jit(solution)/shard_map/all_gather | solution.py:25
  74.2 3.5 %fusion.63 = (f32[2,7,32]{1,2,0:T(8,128)S(1)}, f32[2,7,32,256]{3,1,2,0:T(8,128)S(1)}) fusion(bf16[2,7,32,128]{3,2,1,0:T(8,128)(2,1)S(1)} %bitcast.185, pred[2,256]{1,0:T(4,128)(4,1)S(1)} %broadcast_compare_fusion, bf16[2,256,4096]{2,1,0:T(8,128)(2,1)} %param.20), kind=kOutput, calls=%fused_computation.130 | convolution fusion | flops 29703744 | bytes 4770048 | tf_op jit(solution)/shard_map/rthd,rphd->rthp/dot_general | solution.py:218
  78.7 2.9 %fusion.20 = f32[2,7,32,128]{3,1,2,0:T(8,128)S(1)} fusion(f32[2,7,32,128]{3,1,2,0:T(8,128)S(1)} %convolution_bitcast_fusion, f32[2,7,32,256]{3,1,2,0:T(8,128)S(1)} %get-tuple-element.74, f32[2,7,32]{1,2,0:T(8,128)S(1)} %max.134, pred[2,256]{1,0:T(4,128)(4,1)S(1)} %broadcast_compare_fusion, bf16[2,256,4096]{2,1,0:T(8,128)(2,1)} %param.21), kind=kOutput, calls=%fused_computation.12 | convolution fusion | flops 29761536 | bytes 5114112 | tf_op jit(solution)/shard_map/rthp,rphd->rthd/dot_general | solution.py:230
  82.1 14.1 %all-gather = f32[1824,128]{1,0:T(8,128)S(1)} all-gather(f32[456,128]{1,0:T(8,128)S(1)} %pad_maximum_fusion.1), channel_id=2, replica_groups=mesh['seq_0'=4,'seq_1'=4,'grp'=16] {'seq_0'}, dimensions={0}, use_global_device_ids=true | all-gather | bytes 1167360 | tf_op jit(solution)/shard_map/all_gather | solution.py:37
  96.8 13.6 %all-gather.1 = f32[1824,128]{1,0:T(8,128)S(1)} all-gather(f32[456,128]{1,0:T(8,128)S(1)} %pad_maximum_fusion.2), channel_id=3, replica_groups=mesh['seq_0'=4,'seq_1'=4,'grp'=16] {'seq_1'}, dimensions={0}, use_global_device_ids=true | all-gather | bytes 1167360 | tf_op jit(solution)/shard_map/all_gather | solution.py:37
  114.1 1.7 mul.404
  116.6 1.7 mul.407
  119.1 1.7 mul.410
  121.6 1.7 mul.413
  124.1 1.7 mul.416
  126.6 1.7 mul.419
  128.3 1.7 divide_convert_fusion
  130.0 13.2 %all_to_all.56 = bf16[14,16,256]{2,0,1:T(8,128)(2,1)S(1)} all-to-all(bf16[14,16,256]{2,0,1:T(8,128)(2,1)S(1)} %copy.73), channel_id=1, replica_groups=mesh['seq_0'=4,'seq_1'=4,'grp'=16] {'grp'}, dimensions={1} | all-to-all | bytes 229376 | tf_op jit(solution)/shard_map/all_to_all | solution.py:245
  143.3 1.1 convolution_convert_fusion
  144.4 11.6 %all_to_all.57 = bf16[16,14,256]{2,1,0:T(8,128)(2,1)S(1)} all-to-all(bf16[16,14,256]{2,1,0:T(8,128)(2,1)S(1)} %reshape.586), channel_id=1, replica_groups=mesh['seq_0'=4,'seq_1'=4,'grp'=16] {'grp'}, dimensions={0} | all-to-all | bytes 229376 | tf_op jit(solution)/shard_map/all_to_all | solution.py:57
  156.7 5.1 %all-to-all-start.4 = ((f32[16,14,256]{2,1,0:T(8,128)}), f32[16,14,256]{2,1,0:T(8,128)S(1)}, u32[]{:S(2)}, u32[]{:S(2)}) async-start(f32[16,14,256]{2,1,0:T(8,128)} %broadcast_in_dim.49), calls=%async_computation.4 | async-start | bytes 524288 | tf_op jit(solution)/shard_map/all_to_all | solution.py:69
  161.9 9.3 %all-to-all-done.4 = f32[16,14,256]{2,1,0:T(8,128)S(1)} async-done(((f32[16,14,256]{2,1,0:T(8,128)}), f32[16,14,256]{2,1,0:T(8,128)S(1)}, u32[]{:S(2)}, u32[]{:S(2)}) %all-to-all-start.4) | async-done | bytes 229408 | tf_op jit(solution)/shard_map/all_to_all | solution.py:69
  172.5 10.5 %all_to_all.58 = f32[16,2,14]{2,1,0:T(2,128)S(1)} all-to-all(f32[16,2,14]{2,1,0:T(2,128)S(1)} %broadcast_in_dim.50), channel_id=1, replica_groups=mesh['seq_0'=4,'seq_1'=4,'grp'=16] {'seq_0','seq_1'}, dimensions={0} | all-to-all | bytes 3584 | tf_op jit(solution)/shard_map/all_to_all | solution.py:69
  (141 shorter events, 17.7 us)
Async XLA Ops:
  0.0 1.6 copy-start
  0.0 20.7 %copy-start.1 = (bf16[256,256]{1,0:T(8,128)(2,1)S(1)}, bf16[256,256]{1,0:T(8,128)(2,1)}, u32[]{:S(2)}) copy-start(bf16[256,256]{1,0:T(8,128)(2,1)} %param.17) | copy-start | bytes 393220
  0.0 20.9 %copy-start.2 = (bf16[256,256]{1,0:T(8,128)(2,1)S(1)}, bf16[256,256]{1,0:T(8,128)(2,1)}, u32[]{:S(2)}) copy-start(bf16[256,256]{1,0:T(8,128)(2,1)} %param.18) | copy-start | bytes 393220
  2.8 24.8 %copy-start.5 = (s32[2]{0:T(128)S(1)}, s32[2]{0:T(128)}, u32[]{:S(2)}) copy-start(s32[2]{0:T(128)} %param.13) | copy-start | bytes 28
  22.2 24.6 %all-to-all-start.1 = ((f32[16,14,768]{2,1,0:T(8,128)}), f32[16,14,768]{2,1,0:T(8,128)}, u32[]{:S(2)}, u32[]{:S(2)}) async-start(f32[16,14,768]{2,1,0:T(8,128)} %reshape.569), calls=%async_computation.1 | async-start | bytes 1572864 | tf_op jit(solution)/shard_map/all_to_all | solution.py:18
  128.3 43.6 %copy-start.4 = (f32[4096]{0:T(1024)S(1)}, f32[4096]{0:T(1024)}, u32[]{:S(2)}) copy-start(f32[4096]{0:T(1024)} %param.22) | copy-start | bytes 49156
  130.0 41.9 %copy-start.3 = (bf16[16,4096]{1,0:T(8,128)(2,1)S(1)}, bf16[16,4096]{1,0:T(8,128)(2,1)}, u32[]{:S(2)}) copy-start(bf16[16,4096]{1,0:T(8,128)(2,1)} %param.23) | copy-start | bytes 393220
  156.7 14.5 %all-to-all-start.4 = ((f32[16,14,256]{2,1,0:T(8,128)}), f32[16,14,256]{2,1,0:T(8,128)S(1)}, u32[]{:S(2)}, u32[]{:S(2)}) async-start(f32[16,14,256]{2,1,0:T(8,128)} %broadcast_in_dim.49), calls=%async_computation.4 | async-start | bytes 524288 | tf_op jit(solution)/shard_map/all_to_all | solution.py:69
where the time goes:
time: 185 us; the launch traced here: 184 us
  blocking collectives  104 us (56%)
  waiting for transfers between devices  28.2 us (15%)
  local copies, waits for them, and re-layouts  24.2 us (13%)
  matrix products  10.8 us (6%)
  starting transfers between devices  10.5 us (6%)
  other arithmetic  5.88 us (3%)
    all_gather x2, blocking collectives, all_in_one(): both, at, found = (lax.all_gather(jnp.concatenate(lines), axis), 0, {})  27.7 us
    all_gather x1, blocking collectives, sent_together(): out = lax.all_gather(both, axis, axis=dim, tiled=True)  25.1 us
    all_to_all x1, waiting for transfers between devices, sum_at_owner(): lax.all_to_all(pieces, axis, split_axis=0, concat_axis=0, tiled=True)  18.9 us
    all_to_all x1, blocking collectives, on_device(): lax.all_to_all(block_norm, 'grp', split_axis=1, concat_axis=0, tiled=True)  15.8 us
    mul x12, local copies, waits for them, and re-layouts, join_softmax(): acc = left[2] * left_factor[..., None] + right[2] * right_factor[..., None]  15 us
    all_to_all x1, blocking collectives, on_device(): lax.all_to_all(attended, 'grp', split_axis=1, concat_axis=0, tiled=True)  13.2 us
    all_to_all x1, blocking collectives, sum_at_owner_2(): lax.all_to_all(split_up(shard, dim, devices), axis, 0, 0, tiled=True)  11.6 us
    all_to_all x1, blocking collectives, copy_for_each(): lax.all_to_all(jnp.broadcast_to(shard[None], (devices, *shard.shape)), ax...  10.5 us
  transfers between devices with their start and end apart: 2, of which 2 were waited for; matrix products, arithmetic and copies ran while one was open for 0% of the time, Pallas kernels for 0%

commit v1 on v0

v1 whole, which is shorter than its diff:
```python
import jax
import jax.numpy as jnp
from jax import lax
from jax.sharding import Mesh
from jax.sharding import PartitionSpec as P

HEAD_DIM = 128
SEQ = ("seq_0", "seq_1")
GRP = ("z", "core")
NEG = -1e30


def exchange(pieces, axis):
    return lax.all_to_all(pieces, axis, split_axis=0, concat_axis=0, tiled=True)


def copy_for_each(shard, axis):
    return exchange(jnp.broadcast_to(shard[None], (lax.axis_size(axis), *shard.shape)), axis)


def rotate(values, places):
    half = values.shape[-1] // 2
    freq = 10000.0 ** (-(jnp.arange(half, dtype=jnp.float32) * 2.0 / values.shape[-1]))
    angle = places[..., None, None] * freq
    first = values[..., :half]
    second = values[..., half:]
    cosine = jnp.cos(angle)
    sine = jnp.sin(angle)
    return jnp.concatenate(
        [first * cosine - second * sine, second * cosine + first * sine], axis=-1
    )


def gathered_blocks(block):
    blocks = block[None]
    zs = [0]
    for bit in (4, 2, 1):
        pairs = [(i, i ^ bit) for i in range(lax.axis_size("z"))]
        blocks = jnp.concatenate([blocks, lax.ppermute(blocks, "z", pairs)], axis=0)
        zs = zs + [m ^ bit for m in zs]
    other = lax.ppermute(blocks, "core", [(0, 1), (1, 0)])
    return blocks, other, zs


def on_device(
    actions,
    lengths,
    embed,
    attn_gain,
    w_query,
    w_key,
    w_value,
    w_out,
    key_cache,
    value_cache,
    final_gain,
    head,
):
    s = lax.axis_index(SEQ)
    g = lax.axis_index(GRP)
    seqs = lax.axis_size(SEQ)
    groups = lax.axis_size(GRP)
    robots, steps = actions.shape
    rows = robots * steps
    prompt_dev, width = key_cache.shape[1:]
    cols = w_query.shape[1]
    feats = w_query.shape[0]
    bins = embed.shape[0]
    own_bins = head.shape[0]
    lh = cols // HEAD_DIM
    scale = HEAD_DIM ** (-0.5)
    bin_ids = jnp.arange(bins, dtype=jnp.int32)

    w_mine, w_other, zs = gathered_blocks(w_out)

    acts = copy_for_each(actions.reshape(rows), GRP).reshape(groups * rows)
    wide = embed.astype(jnp.float32)
    mean_square = jnp.mean(wide * wide, axis=-1, keepdims=True)
    part = lax.dynamic_slice(embed, (0, g * feats), (bins, feats)).astype(jnp.float32)
    part_gain = lax.dynamic_slice(attn_gain, (g * feats,), (feats,))
    table = (part * lax.rsqrt(mean_square + 1e-05) * part_gain).astype(jnp.bfloat16)
    onehot = (acts[:, None] == bin_ids[None, :]).astype(jnp.bfloat16)
    normed = jnp.dot(onehot, table, preferred_element_type=jnp.float32).astype(jnp.bfloat16)
    weights = jnp.concatenate([w_query, w_key, w_value], axis=1)
    terms = jnp.dot(normed, weights, preferred_element_type=jnp.float32).astype(jnp.bfloat16)
    sums = exchange(terms.reshape(groups, rows, 3 * cols), GRP)
    sums = jnp.sum(sums.astype(jnp.float32), axis=0)

    places = (lengths[:, None] + jnp.arange(steps, dtype=jnp.int32)[None, :]).astype(jnp.float32)
    heads_of = lambda flat: flat.reshape(robots, steps, lh, HEAD_DIM)
    query = rotate(heads_of(sums[:, :cols]), places).astype(jnp.bfloat16)
    key = rotate(heads_of(sums[:, cols : 2 * cols]), places).astype(jnp.bfloat16)
    value = heads_of(sums[:, 2 * cols :]).astype(jnp.bfloat16)

    head_parts = jnp.swapaxes(head.reshape(own_bins, seqs, cols), 0, 1)
    flat_query = jnp.broadcast_to(query.reshape(1, rows, cols), (seqs, rows, cols))
    spread = exchange(jnp.concatenate([flat_query, head_parts], axis=1), SEQ)
    all_query = spread[:, :rows].reshape(seqs, robots, steps, lh, HEAD_DIM)
    head_cols = spread[:, rows:].reshape(bins, cols)

    prompt_ids = s * prompt_dev + jnp.arange(prompt_dev, dtype=jnp.int32)
    mask = (prompt_ids[None, :] < lengths[:, None])[:, None, None, :]
    heads = seqs * lh
    q = jnp.moveaxis(all_query, 0, 2).reshape(robots, steps, heads, HEAD_DIM)
    cache_keys = key_cache.reshape(robots, prompt_dev, heads, HEAD_DIM)
    cache_values = value_cache.reshape(robots, prompt_dev, heads, HEAD_DIM)
    scores = jnp.einsum("rthd,rphd->rhtp", q, cache_keys, preferred_element_type=jnp.float32)
    scores = jnp.where(mask, scores * scale, NEG)
    top = jnp.max(scores, axis=-1)
    e = jnp.where(mask, jnp.exp(scores - top[..., None]), 0.0)
    total = jnp.sum(e, axis=-1)
    acc = jnp.einsum(
        "rhtp,rphd->rhtd", e.astype(jnp.bfloat16), cache_values, preferred_element_type=jnp.float32
    )

    def to_owner(x):
        x = x.reshape(robots, seqs, lh, steps, -1)
        return jnp.moveaxis(x, 1, 0).reshape(seqs, robots * lh * steps, -1)

    stats = jnp.concatenate([to_owner(top)[..., 0], to_owner(total)[..., 0]], axis=-1)
    stats = jnp.pad(stats, ((0, 0), (0, -stats.shape[-1] % HEAD_DIM))).reshape(seqs, -1, HEAD_DIM)
    packed = exchange(jnp.concatenate([to_owner(acc), stats], axis=1), SEQ)
    n = robots * lh * steps
    tops = packed[:, n:].reshape(seqs, -1)[:, :n]
    totals = packed[:, n:].reshape(seqs, -1)[:, n : 2 * n]
    accs = packed[:, :n]

    step_ids = jnp.arange(steps, dtype=jnp.int32)
    causal = step_ids[None, :] <= step_ids[:, None]
    w_scores = jnp.einsum("rthd,rjhd->rhtj", query, key, preferred_element_type=jnp.float32)
    w_scores = jnp.where(causal, w_scores * scale, NEG)
    w_top = jnp.max(w_scores, axis=-1)
    w_e = jnp.where(causal, jnp.exp(w_scores - w_top[..., None]), 0.0)
    w_total = jnp.sum(w_e, axis=-1).reshape(n)
    w_acc = jnp.einsum(
        "rhtj,rjhd->rhtd", w_e.astype(jnp.bfloat16), value, preferred_element_type=jnp.float32
    ).reshape(n, HEAD_DIM)
    w_top = w_top.reshape(n)

    best = jnp.maximum(jnp.max(tops, axis=0), w_top)
    factors = jnp.exp(tops - best[None])
    w_factor = jnp.exp(w_top - best)
    denom = jnp.sum(totals * factors, axis=0) + w_total * w_factor
    numer = jnp.sum(accs * factors[..., None], axis=0) + w_acc * w_factor[:, None]
    attended = (numer / denom[:, None]).astype(jnp.bfloat16)
    attended = attended.reshape(robots, lh, steps, HEAD_DIM).swapaxes(1, 2).reshape(rows, cols)

    blocks = copy_for_each(attended, SEQ)
    z = lax.axis_index("z")
    core = lax.axis_index("core")
    zc = lax.axis_size("core")
    order = (z ^ jnp.array(zs, jnp.int32)) * zc
    mine = jnp.moveaxis(jnp.take(blocks, order + core, axis=0), 0, 1).reshape(rows, -1)
    others = jnp.moveaxis(jnp.take(blocks, order + 1 - core, axis=0), 0, 1).reshape(rows, -1)
    branch = jnp.dot(mine, w_mine.reshape(-1, cols), preferred_element_type=jnp.float32)
    branch += jnp.dot(others, w_other.reshape(-1, cols), preferred_element_type=jnp.float32)

    own_hot = (actions.reshape(rows)[:, None] == bin_ids[None, :]).astype(jnp.bfloat16)
    own_embed = lax.dynamic_slice(embed, (0, s * cols), (bins, cols))
    inputs = jnp.dot(own_hot, own_embed, preferred_element_type=jnp.float32)
    residual = inputs + branch
    gained = (residual * lax.dynamic_slice(final_gain, (s * cols,), (cols,))).astype(jnp.bfloat16)
    part_logits = lax.dot_general(
        gained, head_cols, (((1,), (1,)), ((), ())), preferred_element_type=jnp.float32
    )
    squares = jnp.sum(residual * residual, axis=-1)
    squares = jnp.pad(squares, (0, bins - rows))[None]
    parts = jnp.concatenate([part_logits, squares, jnp.zeros((1, bins), jnp.float32)], axis=0)
    summed = jnp.sum(copy_for_each(parts, SEQ), axis=0)
    inverse = lax.rsqrt(summed[rows, :rows] / width + 1e-05)
    logits = summed[:rows] * inverse[:, None]
    top_logit = jnp.max(logits, axis=-1, keepdims=True)
    exp_total = jnp.sum(jnp.exp(logits - top_logit), axis=-1, keepdims=True)
    own = lax.dynamic_slice(logits, (0, s * own_bins), (rows, own_bins))
    logprob = own - top_logit - jnp.log(exp_total)
    return logprob.reshape(robots, steps, own_bins)


def solution(mesh):
    torus = Mesh(mesh.devices.reshape(4, 4, 8, 2), ("seq_0", "seq_1", "z", "core"))
    in_specs = (
        P(GRP, None),
        P(GRP),
        P(),
        P(),
        P(GRP, SEQ),
        P(GRP, SEQ),
        P(GRP, SEQ),
        P(GRP, SEQ),
        P(GRP, SEQ, None),
        P(GRP, SEQ, None),
        P(),
        P(SEQ, None),
    )
    out_specs = P(GRP, None, SEQ)
    return jax.shard_map(
        on_device, mesh=torus, in_specs=in_specs, out_specs=out_specs, check_vma=False
    )
```

time: 185 us -> 118 us (0.64)
  blocking collectives: 104 us -> 0 us
  starting transfers between devices: 10.5 us -> 41.7 us
  waiting for transfers between devices: 28.2 us -> 49.5 us
  local copies, waits for them, and re-layouts: 24.2 us -> 10.7 us
  matrix products: 10.8 us -> 8.16 us
    all_gather x3 -> x0, blocking collectives: 52.8 us -> none  [the longest x2 27.7 us: all_in_one(): both, at, found = (lax.all_gather(jnp.concatenate(lines), axis), 0, {})]
    all_to_all x4 -> x0, blocking collectives: 51 us -> none  [the longest x1 15.8 us: on_device(): lax.all_to_all(block_norm, 'grp', split_axis=1, concat_axis=0, tiled=True)]
    all_to_all x2 -> x6, starting transfers between devices: 10.5 us -> 31 us  [exchange(): return lax.all_to_all(pieces, axis, split_axis=0, concat_axis=0, tiled=True)]
    ppermute x0 -> x4, waiting for transfers between devices: none -> 16.7 us  [the longest x3 16.7 us: gathered_blocks(): blocks = jnp.concatenate([blocks, lax.ppermute(blocks, 'z', pairs)], axis=0)]
    mul x12 -> x0, local copies, waits for them, and re-layouts: 15 us -> none  [join_softmax(): acc = left[2] * left_factor[..., None] + right[2] * right_factor[..., None]]
    ppermute x0 -> x4, starting transfers between devices: none -> 10.7 us  [the longest x3 10.6 us: gathered_blocks(): blocks = jnp.concatenate([blocks, lax.ppermute(blocks, 'z', pairs)], axis=0)]
    all_to_all x2 -> x6, waiting for transfers between devices: 28.2 us -> 32.9 us  [exchange(): return lax.all_to_all(pieces, axis, split_axis=0, concat_axis=0, tiled=True)]
    dot_general x10 -> x9, matrix products: 10.8 us -> 8.16 us  [the longest x1 3.6 us: on_device(): jnp.einsum('rthd,rphd->rhtp', q, cache_keys, preferred_element_type=jnp.f...]
  transfers between devices with their start and end apart: 2 -> 10, of which waited for: 2 -> 5; matrix products, arithmetic and copies ran while one was open for 0% -> 18% of each run, Pallas kernels for 0% -> 0%
where the time goes in v1:
time: 118 us; the launch traced here: 117 us
  waiting for transfers between devices  49.5 us (42%)
  starting transfers between devices  41.7 us (35%)
  local copies, waits for them, and re-layouts  10.7 us (9%)
  matrix products  8.16 us (7%)
  other arithmetic  6.84 us (6%)
    all_to_all x6, waiting for transfers between devices, exchange(): return lax.all_to_all(pieces, axis, split_axis=0, concat_axis=0, tiled=True)  32.9 us
    all_to_all x6, starting transfers between devices, exchange(): return lax.all_to_all(pieces, axis, split_axis=0, concat_axis=0, tiled=True)  31 us
    ppermute x3, waiting for transfers between devices, gathered_blocks(): blocks = jnp.concatenate([blocks, lax.ppermute(blocks, 'z', pairs)], axis=0)  16.7 us
    ppermute x3, starting transfers between devices, gathered_blocks(): blocks = jnp.concatenate([blocks, lax.ppermute(blocks, 'z', pairs)], axis=0)  10.6 us
    dot_general x1, matrix products, on_device(): jnp.einsum('rthd,rphd->rhtp', q, cache_keys, preferred_element_type=jnp.f...  3.6 us
  transfers between devices with their start and end apart: 10, of which 5 were waited for; matrix products, arithmetic and copies ran while one was open for 18% of the time, Pallas kernels for 0%

profile of v1, /device:TPU:32, one launch (start us, length us, event | category | flops | bytes accessed | tf_op | source)
XLA Modules:
  0.0 117.3 jit_solution(17974327390225510978)
XLA Ops:
  0.0 0.8 eq.30
  1.4 8.6 %all-to-all-start = ((s32[16,1,14]{2,1,0:T(1,128)}), s32[16,1,14]{2,1,0:T(1,128)S(1)}, u32[]{:S(2)}, u32[]{:S(2)}) async-start(s32[16,1,14]{2,1,0:T(1,128)} %broadcast_in_dim.58), calls=%async_computation | async-start | bytes 16384 | tf_op jit(solution)/shard_map/all_to_all | solution.py:14
  10.0 4.5 %collective-permute-start = (bf16[1,256,256]{2,1,0:T(8,128)(2,1)}, bf16[1,256,256]{2,1,0:T(8,128)(2,1)S(1)}, u32[]{:S(2)}, u32[]{:S(2)}) collective-permute-start(bf16[1,256,256]{2,1,0:T(8,128)(2,1)} %bitcast.81), channel_id=1, source_target_pairs={{0,8},{2,10},{4,12},{6,14},{8,0},{10,2},{12,4},{14,6},{1,9},{3,11}... | collective-permute-start | bytes 393224 | tf_op jit(solution)/shard_map/ppermute | solution.py:39
  14.5 2.1 %multiply_reduce_fusion = f32[256]{0:T(256)S(1)} fusion(bf16[256,4096]{1,0:T(8,128)(2,1)} %param.17), kind=kLoop, calls=%fused_computation.8 | loop fusion | flops 3145472 | bytes 2098176 | tf_op jit(solution)/shard_map/reduce_sum | solution.py:78
  16.6 1.1 fusion.36
  19.8 0.8 dynamic_slice.17
  21.8 1.6 %convolution_convert_fusion = bf16[224,768]{1,0:T(8,128)(2,1)S(1)} fusion(bf16[256,256]{1,0:T(8,128)(2,1)} %param.21, bf16[256,256]{1,0:T(8,128)(2,1)} %param.20, bf16[256,256]{1,0:T(8,128)(2,1)} %param.19, f32[256]{0:T(256)S(1)} %dynamic_slice.17, f32[256]{0:T(256)S(1)} %add_rsqrt_fusion, bf16[256,4096]{1,0:T(8,128)(2,1)} %param.17, s32[]{:T(128)S(6)} %select_n.33, ...), kind=kOutput, calls=%fused_computation.11 | convolution fusion | flops 119169024 | bytes 871300 | tf_op jit(solution)/shard_map/dot_general | solution.py:85
  23.4 0.8 reshape.222
  24.2 4.8 %all-to-all-start.1 = ((bf16[16,14,768]{2,1,0:T(8,128)(2,1)}), bf16[16,14,768]{2,1,0:T(8,128)(2,1)S(1)}, u32[]{:S(2)}, u32[]{:S(2)}) async-start(bf16[16,14,768]{2,1,0:T(8,128)(2,1)} %reshape.222), calls=%async_computation.1 | async-start | bytes 786432 | tf_op jit(solution)/shard_map/all_to_all | solution.py:14
  29.1 2.5 %collective-permute-start.1 = (bf16[2,256,256]{2,1,0:T(8,128)(2,1)S(1)}, bf16[2,256,256]{2,1,0:T(8,128)(2,1)S(1)}, u32[]{:S(2)}, u32[]{:S(2)}) collective-permute-start(bf16[2,256,256]{2,1,0:T(8,128)(2,1)S(1)} %pad_maximum_fusion.2), channel_id=1, source_target_pairs={{0,4},{2,6},{4,0},{6,2},{8,12},{10,14},{12,8},{14,10},{1,5},{3,7},... | collective-permute-start | bytes 786440 | tf_op jit(solution)/shard_map/ppermute | solution.py:39
  31.6 0.8 dynamic_slice.18
  32.6 16.7 %collective-permute-done.1 = bf16[2,256,256]{2,1,0:T(8,128)(2,1)S(1)} collective-permute-done((bf16[2,256,256]{2,1,0:T(8,128)(2,1)S(1)}, bf16[2,256,256]{2,1,0:T(8,128)(2,1)S(1)}, u32[]{:S(2)}, u32[]{:S(2)}) %collective-permute-start.1) | collective-permute-done | bytes 262176 | tf_op jit(solution)/shard_map/ppermute | solution.py:39
  49.3 3.6 %collective-permute-start.2 = (bf16[4,256,256]{2,1,0:T(8,128)(2,1)S(1)}, bf16[4,256,256]{2,1,0:T(8,128)(2,1)S(1)}, u32[]{:S(2)}, u32[]{:S(2)}) collective-permute-start(bf16[4,256,256]{2,1,0:T(8,128)(2,1)S(1)} %pad_maximum_fusion.1), channel_id=1, source_target_pairs={{0,2},{2,0},{4,6},{6,4},{8,10},{10,8},{12,14},{14,12},{1,3},{3,1},... | collective-permute-start | bytes 1572872 | tf_op jit(solution)/shard_map/ppermute | solution.py:39
  53.4 0.8 copy.119
  54.2 7.0 %all-to-all-start.2 = ((bf16[16,30,256]{2,1,0:T(8,128)(2,1)}), bf16[16,30,256]{2,1,0:T(8,128)(2,1)S(1)}, u32[]{:S(2)}, u32[]{:S(2)}) async-start(bf16[16,30,256]{2,1,0:T(8,128)(2,1)} %copy.119), calls=%async_computation.2 | async-start | bytes 524288 | tf_op jit(solution)/shard_map/all_to_all | solution.py:14
  61.7 8.3 %all-to-all-done.2 = bf16[16,30,256]{2,1,0:T(8,128)(2,1)S(1)} async-done(((bf16[16,30,256]{2,1,0:T(8,128)(2,1)}), bf16[16,30,256]{2,1,0:T(8,128)(2,1)S(1)}, u32[]{:S(2)}, u32[]{:S(2)}) %all-to-all-start.2) | async-done | bytes 245792 | tf_op jit(solution)/shard_map/all_to_all | solution.py:14
  70.1 3.6 %fusion.84 = (f32[2,32,7]{2,1,0:T(8,128)S(1)}, f32[2,32,7,256]{3,2,1,0:T(8,128)S(1)}) fusion(bf16[2,7,32,128]{3,1,2,0:T(8,128)(2,1)S(1)} %bitcast.89, pred[2,256]{1,0:T(4,128)(4,1)S(1)} %broadcast_compare_fusion, bf16[2,256,4096]{2,1,0:T(8,128)(2,1)} %param.23), kind=kOutput, calls=%fused_computation.133 | convolution fusion | flops 29703744 | bytes 4770048 | tf_op jit(solution)/shard_map/rthd,rphd->rhtp/dot_general | solution.py:107
  75.1 0.8 copy.129
  75.9 3.5 %all-to-all-start.3 = ((f32[16,29,128]{2,1,0:T(8,128)}), f32[16,29,128]{2,1,0:T(8,128)S(1)}, u32[]{:S(2)}, u32[]{:S(2)}) async-start(f32[16,29,128]{2,1,0:T(8,128)} %copy.129), calls=%async_computation.3 | async-start | bytes 524288 | tf_op jit(solution)/shard_map/all_to_all | solution.py:14
  80.0 8.0 %all-to-all-done.3 = f32[16,29,128]{2,1,0:T(8,128)S(1)} async-done(((f32[16,29,128]{2,1,0:T(8,128)}), f32[16,29,128]{2,1,0:T(8,128)S(1)}, u32[]{:S(2)}, u32[]{:S(2)}) %all-to-all-start.3) | async-done | bytes 237600 | tf_op jit(solution)/shard_map/all_to_all | solution.py:14
  89.7 3.5 %all-to-all-start.4 = ((bf16[16,14,256]{2,1,0:T(8,128)(2,1)}), bf16[16,14,256]{2,1,0:T(8,128)(2,1)S(1)}, u32[]{:S(2)}, u32[]{:S(2)}) async-start(bf16[16,14,256]{2,1,0:T(8,128)(2,1)} %broadcast_in_dim.107), calls=%async_computation.4 | async-start | bytes 262144 | tf_op jit(solution)/shard_map/all_to_all | solution.py:14
  93.3 7.9 %all-to-all-done.4 = bf16[16,14,256]{2,1,0:T(8,128)(2,1)S(1)} async-done(((bf16[16,14,256]{2,1,0:T(8,128)(2,1)}), bf16[16,14,256]{2,1,0:T(8,128)(2,1)S(1)}, u32[]{:S(2)}, u32[]{:S(2)}) %all-to-all-start.4) | async-done | bytes 114720 | tf_op jit(solution)/shard_map/all_to_all | solution.py:14
  104.0 3.5 %all-to-all-start.5 = ((f32[16,16,256]{2,1,0:T(8,128)}), f32[16,16,256]{2,1,0:T(8,128)S(1)}, u32[]{:S(2)}, u32[]{:S(2)}) async-start(f32[16,16,256]{2,1,0:T(8,128)} %broadcast_in_dim.111), calls=%async_computation.5 | async-start | bytes 524288 | tf_op jit(solution)/shard_map/all_to_all | solution.py:14
  107.6 8.7 %all-to-all-done.5 = f32[16,16,256]{2,1,0:T(8,128)S(1)} async-done(((f32[16,16,256]{2,1,0:T(8,128)}), f32[16,16,256]{2,1,0:T(8,128)S(1)}, u32[]{:S(2)}, u32[]{:S(2)}) %all-to-all-start.5) | async-done | bytes 262176 | tf_op jit(solution)/shard_map/all_to_all | solution.py:14
  (99 shorter events, 12.8 us)
Async XLA Ops:
  0.0 29.1 %copy-start.1 = (bf16[256,256]{1,0:T(8,128)(2,1)S(1)}, bf16[256,256]{1,0:T(8,128)(2,1)}, u32[]{:S(2)}) copy-start(bf16[256,256]{1,0:T(8,128)(2,1)} %param.22) | copy-start | bytes 393220
  0.0 32.4 %copy-start.2 = (bf16[16,4096]{1,0:T(8,128)(2,1)S(1)}, bf16[16,4096]{1,0:T(8,128)(2,1)}, u32[]{:S(2)}) copy-start(bf16[16,4096]{1,0:T(8,128)(2,1)} %param.26) | copy-start | bytes 393220
  1.4 19.1 %all-to-all-start = ((s32[16,1,14]{2,1,0:T(1,128)}), s32[16,1,14]{2,1,0:T(1,128)S(1)}, u32[]{:S(2)}, u32[]{:S(2)}) async-start(s32[16,1,14]{2,1,0:T(1,128)} %broadcast_in_dim.58), calls=%async_computation | async-start | bytes 16384 | tf_op jit(solution)/shard_map/all_to_all | solution.py:14
  10.0 19.1 %collective-permute-start = (bf16[1,256,256]{2,1,0:T(8,128)(2,1)}, bf16[1,256,256]{2,1,0:T(8,128)(2,1)S(1)}, u32[]{:S(2)}, u32[]{:S(2)}) collective-permute-start(bf16[1,256,256]{2,1,0:T(8,128)(2,1)} %bitcast.81), channel_id=1, source_target_pairs={{0,8},{2,10},{4,12},{6,14},{8,0},{10,2},{12,4},{14,6},{1,9},{3,11}... | collective-permute-start | bytes 393224 | tf_op jit(solution)/shard_map/ppermute | solution.py:39
  24.2 28.7 %all-to-all-start.1 = ((bf16[16,14,768]{2,1,0:T(8,128)(2,1)}), bf16[16,14,768]{2,1,0:T(8,128)(2,1)S(1)}, u32[]{:S(2)}, u32[]{:S(2)}) async-start(bf16[16,14,768]{2,1,0:T(8,128)(2,1)} %reshape.222), calls=%async_computation.1 | async-start | bytes 786432 | tf_op jit(solution)/shard_map/all_to_all | solution.py:14
  29.1 20.2 %collective-permute-start.1 = (bf16[2,256,256]{2,1,0:T(8,128)(2,1)S(1)}, bf16[2,256,256]{2,1,0:T(8,128)(2,1)S(1)}, u32[]{:S(2)}, u32[]{:S(2)}) collective-permute-start(bf16[2,256,256]{2,1,0:T(8,128)(2,1)S(1)} %pad_maximum_fusion.2), channel_id=1, source_target_pairs={{0,4},{2,6},{4,0},{6,2},{8,12},{10,14},{12,8},{14,10},{1,5},{3,7},... | collective-permute-start | bytes 786440 | tf_op jit(solution)/shard_map/ppermute | solution.py:39
  49.3 30.1 %collective-permute-start.2 = (bf16[4,256,256]{2,1,0:T(8,128)(2,1)S(1)}, bf16[4,256,256]{2,1,0:T(8,128)(2,1)S(1)}, u32[]{:S(2)}, u32[]{:S(2)}) collective-permute-start(bf16[4,256,256]{2,1,0:T(8,128)(2,1)S(1)} %pad_maximum_fusion.1), channel_id=1, source_target_pairs={{0,2},{2,0},{4,6},{6,4},{8,10},{10,8},{12,14},{14,12},{1,3},{3,1},... | collective-permute-start | bytes 1572872 | tf_op jit(solution)/shard_map/ppermute | solution.py:39
  54.2 15.7 %all-to-all-start.2 = ((bf16[16,30,256]{2,1,0:T(8,128)(2,1)}), bf16[16,30,256]{2,1,0:T(8,128)(2,1)S(1)}, u32[]{:S(2)}, u32[]{:S(2)}) async-start(bf16[16,30,256]{2,1,0:T(8,128)(2,1)} %copy.119), calls=%async_computation.2 | async-start | bytes 524288 | tf_op jit(solution)/shard_map/all_to_all | solution.py:14
  70.0 3.6 %copy-start = (bf16[2,256,4096]{2,1,0:T(8,128)(2,1)S(1)}, bf16[2,256,4096]{2,1,0:T(8,128)(2,1)}, u32[]{:S(2)}) copy-start(bf16[2,256,4096]{2,1,0:T(8,128)(2,1)} %param.24) | copy-start | bytes 12582916
  75.9 12.2 %all-to-all-start.3 = ((f32[16,29,128]{2,1,0:T(8,128)}), f32[16,29,128]{2,1,0:T(8,128)S(1)}, u32[]{:S(2)}, u32[]{:S(2)}) async-start(f32[16,29,128]{2,1,0:T(8,128)} %copy.129), calls=%async_computation.3 | async-start | bytes 524288 | tf_op jit(solution)/shard_map/all_to_all | solution.py:14
  79.5 22.8 %collective-permute-start.3 = (bf16[8,256,256]{2,1,0:T(8,128)(2,1)S(1)}, bf16[8,256,256]{2,1,0:T(8,128)(2,1)S(1)}, u32[]{:S(2)}, u32[]{:S(2)}) collective-permute-start(bf16[8,256,256]{2,1,0:T(8,128)(2,1)S(1)} %pad_maximum_fusion), channel_id=1, source_target_pairs={{0,1},{1,0},{2,3},{3,2},{4,5},{5,4},{6,7},{7,6},{8,9},{9,8},{10,11... | collective-permute-start | bytes 3145736 | tf_op jit(solution)/shard_map/ppermute | solution.py:41
  89.7 11.5 %all-to-all-start.4 = ((bf16[16,14,256]{2,1,0:T(8,128)(2,1)}), bf16[16,14,256]{2,1,0:T(8,128)(2,1)S(1)}, u32[]{:S(2)}, u32[]{:S(2)}) async-start(bf16[16,14,256]{2,1,0:T(8,128)(2,1)} %broadcast_in_dim.107), calls=%async_computation.4 | async-start | bytes 262144 | tf_op jit(solution)/shard_map/all_to_all | solution.py:14
  104.0 12.2 %all-to-all-start.5 = ((f32[16,16,256]{2,1,0:T(8,128)}), f32[16,16,256]{2,1,0:T(8,128)S(1)}, u32[]{:S(2)}, u32[]{:S(2)}) async-start(f32[16,16,256]{2,1,0:T(8,128)} %broadcast_in_dim.111), calls=%async_computation.5 | async-start | bytes 524288 | tf_op jit(solution)/shard_map/all_to_all | solution.py:14

commit v2 on v1

v2 whole, which is shorter than its diff:
```python
import jax
import jax.numpy as jnp
from jax import lax
from jax.sharding import Mesh
from jax.sharding import PartitionSpec as P


HEAD_DIM = 128
SEQ = ("seq_0", "seq_1")
GRP = ("z", "core")
NEG = -1e30


def exchange(pieces, axis):
    return lax.all_to_all(pieces, axis, split_axis=0, concat_axis=0, tiled=True)


def copy_for_each(shard, axis):
    return exchange(jnp.broadcast_to(shard[None], (lax.axis_size(axis), *shard.shape)), axis)


def from_partner(x, axis, k):
    return lax.ppermute(x, axis, [(i, i ^ k) for i in range(lax.axis_size(axis))])


def in_order(own, axis):
    i = lax.axis_index(axis)
    odd = (i & 1) == 1
    high = (i & 2) == 2
    a, b, c, d = own
    a, b = jnp.where(odd, b, a), jnp.where(odd, a, b)
    c, d = jnp.where(odd, d, c), jnp.where(odd, c, d)
    return (
        jnp.where(high, c, a),
        jnp.where(high, d, b),
        jnp.where(high, a, c),
        jnp.where(high, b, d),
    )


def from_all(x, axis):
    return (x, *(from_partner(x, axis, k) for k in (1, 2, 3)))


def after(x, anchor):
    return lax.optimization_barrier((x, anchor))[0]


def halves(x):
    both = lax.reduce_precision(x, 8, 15)
    high = lax.reduce_precision(both, 8, 7)
    return high.astype(jnp.bfloat16), (both - high).astype(jnp.bfloat16), both


def joined(high, low):
    return high.astype(jnp.float32) + low.astype(jnp.float32)


def merge(tops, totals, accs):
    best = tops[0]
    for t in tops[1:]:
        best = jnp.maximum(best, t)
    factors = [jnp.exp(t - best) for t in tops]
    total = sum(l * f for l, f in zip(totals, factors))
    acc = sum(x.astype(jnp.float32) * f[:, None] for x, f in zip(accs, factors))
    return best, total, acc


def packed(top, total, acc):
    th, tl, _ = halves(top)
    lh, ll, _ = halves(total)
    stats = jnp.stack([th, tl, lh, ll])
    stats = jnp.pad(stats, ((0, 12), (0, 0)))
    return jnp.concatenate([acc.astype(jnp.bfloat16), stats], axis=0)


def unpacked(x):
    n = x.shape[1]
    stats = x[n : n + 4]
    return joined(stats[0], stats[1]), joined(stats[2], stats[3]), x[:n]


def rotate(values, places):
    half = values.shape[-1] // 2
    freq = 10000.0 ** (-(jnp.arange(half, dtype=jnp.float32) * 2.0 / values.shape[-1]))
    angle = places[..., None, None] * freq
    first = values[..., :half]
    second = values[..., half:]
    cosine = jnp.cos(angle)
    sine = jnp.sin(angle)
    return jnp.concatenate(
        [first * cosine - second * sine, second * cosine + first * sine], axis=-1
    )


def on_device(
    actions,
    lengths,
    embed,
    attn_gain,
    w_query,
    w_key,
    w_value,
    w_out,
    key_cache,
    value_cache,
    final_gain,
    head,
):
    s0 = lax.axis_index("seq_0")
    s = lax.axis_index(SEQ)
    g = lax.axis_index(GRP)
    z = lax.axis_index("z")
    core = lax.axis_index("core")
    seqs = lax.axis_size(SEQ)
    side = lax.axis_size("seq_0")
    groups = lax.axis_size(GRP)
    robots, true_steps = actions.shape
    steps = 8
    rows = robots * steps
    prompt_dev, width = key_cache.shape[1:]
    feats, cols = w_query.shape
    bins = embed.shape[0]
    own_bins = head.shape[0]
    lh = cols // HEAD_DIM
    heads = seqs * lh
    scale = HEAD_DIM ** (-0.5)
    bin_ids = jnp.arange(bins, dtype=jnp.int32)

    blocks = w_out[None]
    zs = [0]
    blocks = jnp.concatenate([blocks, from_partner(blocks, "z", 4)], axis=0)
    zs = zs + [m ^ 4 for m in zs]

    pad_steps = ((0, 0), (0, steps - true_steps))
    acts = copy_for_each(actions, GRP).reshape(groups * robots, true_steps)
    acts = jnp.pad(acts, pad_steps).reshape(groups * rows)
    actions = jnp.pad(actions, pad_steps)
    wide = embed.astype(jnp.float32)
    mean_square = jnp.mean(wide * wide, axis=-1, keepdims=True)
    part = lax.dynamic_slice(embed, (0, g * feats), (bins, feats)).astype(jnp.float32)
    part_gain = lax.dynamic_slice(attn_gain, (g * feats,), (feats,))
    table = (part * lax.rsqrt(mean_square + 1e-05) * part_gain).astype(jnp.bfloat16)
    onehot = (acts[:, None] == bin_ids[None, :]).astype(jnp.bfloat16)
    normed = jnp.dot(onehot, table, preferred_element_type=jnp.float32).astype(jnp.bfloat16)
    weights = jnp.concatenate([w_query, w_key, w_value], axis=1)
    terms = jnp.dot(normed, weights, preferred_element_type=jnp.float32).astype(jnp.bfloat16)
    sums = exchange(terms.reshape(groups, rows, 3 * cols), GRP)
    sums = jnp.sum(sums.astype(jnp.float32), axis=0)

    blocks = after(blocks, sums)
    blocks = jnp.concatenate([blocks, from_partner(blocks, "z", 2)], axis=0)
    zs = zs + [m ^ 2 for m in zs]

    places = (lengths[:, None] + jnp.arange(steps, dtype=jnp.int32)[None, :]).astype(jnp.float32)
    heads_of = lambda flat: flat.reshape(robots, steps, lh, HEAD_DIM)
    query = rotate(heads_of(sums[:, :cols]), places).astype(jnp.bfloat16)
    key = rotate(heads_of(sums[:, cols : 2 * cols]), places).astype(jnp.bfloat16)
    value = heads_of(sums[:, 2 * cols :]).astype(jnp.bfloat16)

    flat_query = query.reshape(1, rows, cols)
    head_parts = head.reshape(own_bins, side, side, cols).transpose(2, 1, 0, 3)
    head_parts = in_order([head_parts[k] for k in range(side)], "seq_1")
    near = [jnp.concatenate([flat_query, head_parts[0]], axis=0)]
    for k in (1, 2, 3):
        sent = jnp.concatenate([flat_query, head_parts[k]], axis=0)
        near.append(from_partner(sent, "seq_1", k))
    near = jnp.stack(in_order(near, "seq_1"))
    head_parts = in_order([near[:, 1 + k] for k in range(side)], "seq_0")
    far = [jnp.concatenate([near[:, 0], head_parts[0]], axis=0)]
    for k in (1, 2, 3):
        sent = jnp.concatenate([near[:, 0], head_parts[k]], axis=0)
        far.append(from_partner(sent, "seq_0", k))
    far = jnp.stack(in_order(far, "seq_0"))
    all_query = far[:, :side].reshape(seqs, robots, steps, lh, HEAD_DIM)
    head_cols = far[:, side:].reshape(bins, cols)

    prompt_ids = s * prompt_dev + jnp.arange(prompt_dev, dtype=jnp.int32)
    mask = (prompt_ids[None, :] < lengths[:, None])[:, None, None, :]
    q = jnp.moveaxis(all_query, 0, 2).reshape(robots, steps, heads, HEAD_DIM)
    cache_keys = key_cache.reshape(robots, prompt_dev, heads, HEAD_DIM)
    cache_values = value_cache.reshape(robots, prompt_dev, heads, HEAD_DIM)
    scores = jnp.einsum("rthd,rphd->rhtp", q, cache_keys, preferred_element_type=jnp.float32)
    scores = jnp.where(mask, scores * scale, NEG)
    top = lax.reduce_precision(jnp.max(scores, axis=-1), 8, 15)
    e = jnp.where(mask, jnp.exp(scores - top[..., None]), 0.0)
    total = jnp.sum(e, axis=-1)
    acc = jnp.einsum(
        "rhtp,rphd->rhtd", e.astype(jnp.bfloat16), cache_values, preferred_element_type=jnp.float32
    )
    blocks = after(blocks, acc)
    blocks = jnp.concatenate([blocks, from_partner(blocks, "z", 1)], axis=0)
    zs = zs + [m ^ 1 for m in zs]

    step_ids = jnp.arange(steps, dtype=jnp.int32)
    causal = step_ids[None, :] <= step_ids[:, None]
    w_scores = jnp.einsum("rthd,rjhd->rhtj", query, key, preferred_element_type=jnp.float32)
    w_scores = jnp.where(causal, w_scores * scale, NEG)
    w_top = lax.reduce_precision(jnp.max(w_scores, axis=-1), 8, 15)
    w_e = jnp.where(causal, jnp.exp(w_scores - w_top[..., None]), 0.0)
    w_total = jnp.sum(w_e, axis=-1)
    w_acc = jnp.einsum(
        "rhtj,rjhd->rhtd", w_e.astype(jnp.bfloat16), value, preferred_element_type=jnp.float32
    )

    def quarters(x):
        x = x.reshape(robots, side, side, lh, steps, -1)
        return [x[:, k].reshape(robots * side * lh * steps, -1) for k in range(side)]

    tops = in_order(quarters(top), "seq_0")
    totals = in_order(quarters(total), "seq_0")
    accs = in_order(quarters(acc.astype(jnp.bfloat16)), "seq_0")
    pieces = [(tops[0][:, 0], totals[0][:, 0], accs[0])]
    for k in (1, 2, 3):
        sent = packed(tops[k][:, 0], totals[k][:, 0], accs[k])
        pieces.append(unpacked(from_partner(sent, "seq_0", k)))
    top, total, acc = merge(*zip(*pieces))

    s1 = lax.axis_index("seq_1")
    at_owner = (jnp.arange(side) == s1)[None, :, None, None]
    spread = lambda x: jnp.broadcast_to(x[:, None], (robots, side, *x.shape[1:]))
    flat = lambda x: x.reshape(robots * side * lh * steps, *x.shape[4:])
    w_top = flat(jnp.where(at_owner, spread(w_top), NEG))
    w_total = flat(jnp.where(at_owner, spread(w_total), 0.0))
    w_acc = flat(jnp.where(at_owner[..., None], spread(w_acc), 0.0))
    top, total, acc = merge((top, w_top), (total, w_total), (acc, w_acc))

    sent = packed(top, total, acc)
    _, _, total = halves(total)
    pieces = [(top, total, sent[: acc.shape[0]])]
    for k in (1, 2, 3):
        pieces.append(unpacked(from_partner(sent, "seq_1", k)))
    top, total, acc = merge(*zip(*pieces))
    attended = (acc / total[:, None]).astype(jnp.bfloat16)
    attended = attended.reshape(robots, side, lh, steps, HEAD_DIM)
    attended = attended.transpose(1, 0, 3, 2, 4).reshape(side, rows, cols)

    blocks = after(blocks, attended)
    other = from_partner(blocks, "core", 1)

    gathered = jnp.concatenate(from_all(attended, "seq_0"), axis=0)
    order = (z ^ jnp.array(zs, jnp.int32)) * lax.axis_size("core")
    place = lambda b: ((b // side) ^ s0) * side + b % side
    take = lambda b: jnp.moveaxis(jnp.take(gathered, place(b), axis=0), 0, 1).reshape(rows, -1)
    branch = jnp.dot(take(order + core), blocks.reshape(-1, cols), preferred_element_type=jnp.float32)
    branch += jnp.dot(take(order + 1 - core), other.reshape(-1, cols), preferred_element_type=jnp.float32)

    own_hot = (actions.reshape(rows)[:, None] == bin_ids[None, :]).astype(jnp.bfloat16)
    own_embed = lax.dynamic_slice(embed, (0, s * cols), (bins, cols))
    inputs = jnp.dot(own_hot, own_embed, preferred_element_type=jnp.float32)
    residual = inputs + branch
    gained = (residual * lax.dynamic_slice(final_gain, (s * cols,), (cols,))).astype(jnp.bfloat16)
    part_logits = lax.dot_general(
        gained, head_cols, (((1,), (1,)), ((), ())), preferred_element_type=jnp.float32
    )
    squares = jnp.sum(residual * residual, axis=-1)
    last = (jnp.arange(rows) == rows - 1)[:, None]
    parts = jnp.where(last, jnp.pad(squares, (0, bins - rows))[None], part_logits)
    parts = sum(from_all(parts, "seq_1"))
    parts = sum(from_all(parts, "seq_0"))
    inverse = lax.rsqrt(parts[rows - 1, :rows] / width + 1e-05)
    logits = parts * inverse[:, None]
    top_logit = jnp.max(logits, axis=-1, keepdims=True)
    exp_total = jnp.sum(jnp.exp(logits - top_logit), axis=-1, keepdims=True)
    own = lax.dynamic_slice(parts, (0, s * own_bins), (rows, own_bins)) * inverse[:, None]
    logprob = own - top_logit - jnp.log(exp_total)
    return logprob.reshape(robots, steps, own_bins)[:, :true_steps]


def solution(mesh):
    torus = Mesh(mesh.devices.reshape(4, 4, 8, 2), ("seq_0", "seq_1", "z", "core"))
    in_specs = (
        P(GRP, None),
        P(GRP),
        P(),
        P(),
        P(GRP, SEQ),
        P(GRP, SEQ),
        P(GRP, SEQ),
        P(GRP, SEQ),
        P(GRP, SEQ, None),
        P(GRP, SEQ, None),
        P(),
        P(SEQ, None),
    )
    out_specs = P(GRP, None, SEQ)

    return jax.shard_map(
        on_device, mesh=torus, in_specs=in_specs, out_specs=out_specs, check_vma=False
    )
```

time: 118 us -> 118 us (level); the launches traced: 117 us -> 116 us
  starting transfers between devices: 41.7 us -> 53.7 us
  waiting for transfers between devices: 49.5 us -> 41.8 us
  local copies, waits for them, and re-layouts: 10.7 us -> 7.33 us
  matrix products: 8.16 us -> 6.67 us
  other arithmetic: 6.84 us -> 5.62 us
    ppermute x4 -> x25, starting transfers between devices: 10.7 us -> 40.3 us  [from_partner(): lax.ppermute(x, axis, [(i, i ^ k) for i in range(lax.axis_size(axis))])]
    all_to_all x6 -> x2, waiting for transfers between devices: 32.9 us -> 11.4 us  [exchange(): return lax.all_to_all(pieces, axis, split_axis=0, concat_axis=0, tiled=True)]
    all_to_all x6 -> x2, starting transfers between devices: 31 us -> 13.4 us  [exchange(): return lax.all_to_all(pieces, axis, split_axis=0, concat_axis=0, tiled=True)]
    ppermute x4 -> x25, waiting for transfers between devices: 16.7 us -> 30.4 us  [from_partner(): lax.ppermute(x, axis, [(i, i ^ k) for i in range(lax.axis_size(axis))])]
    dot_general x1, matrix products: 3.6 us -> 1.26 us  [on_device(): jnp.einsum('rthd,rphd->rhtp', q, cache_keys, preferred_element_type=jnp.f...]
    concatenate x3 -> x0, local copies, waits for them, and re-layouts: 1.61 us -> none  [the longest x1 0.77 us: on_device(): packed = exchange(jnp.concatenate([to_owner(acc), stats], axis=1), SEQ)]
  transfers between devices with their start and end apart: 10 -> 27, of which waited for: 5 -> 18; matrix products, arithmetic and copies ran while one was open for 18% -> 11% of each run, Pallas kernels for 0% -> 0%
where the time goes in v2:
time: 118 us; the launch traced here: 116 us
  starting transfers between devices  53.7 us (46%)
  waiting for transfers between devices  41.8 us (35%)
  local copies, waits for them, and re-layouts  7.33 us (6%)
  matrix products  6.67 us (6%)
  other arithmetic  5.62 us (5%)
    ppermute x25, starting transfers between devices, from_partner(): lax.ppermute(x, axis, [(i, i ^ k) for i in range(lax.axis_size(axis))])  40.3 us
    ppermute x25, waiting for transfers between devices, from_partner(): lax.ppermute(x, axis, [(i, i ^ k) for i in range(lax.axis_size(axis))])  30.4 us
    all_to_all x2, starting transfers between devices, exchange(): return lax.all_to_all(pieces, axis, split_axis=0, concat_axis=0, tiled=True)  13.4 us
    all_to_all x2, waiting for transfers between devices, exchange(): return lax.all_to_all(pieces, axis, split_axis=0, concat_axis=0, tiled=True)  11.4 us
  transfers between devices with their start and end apart: 27, of which 18 were waited for; matrix products, arithmetic and copies ran while one was open for 11% of the time, Pallas kernels for 0%

profile of v2, /device:TPU:32, one launch (start us, length us, event | category | flops | bytes accessed | tf_op | source)
XLA Modules:
  0.0 115.7 jit_solution(11769286715256688361)
XLA Ops:
  1.3 8.6 %all-to-all-start = ((s32[16,2,7]{2,1,0:T(2,128)}), s32[16,2,7]{2,1,0:T(2,128)S(1)}, u32[]{:S(2)}, u32[]{:S(2)}) async-start(s32[16,2,7]{2,1,0:T(2,128)} %broadcast_in_dim.164), calls=%async_computation | async-start | bytes 32768 | tf_op jit(solution)/shard_map/all_to_all | solution.py:15
  9.9 4.5 %collective-permute-start.15 = (bf16[1,256,256]{2,1,0:T(8,128)(2,1)}, bf16[1,256,256]{2,1,0:T(8,128)(2,1)S(1)}, u32[]{:S(2)}, u32[]{:S(2)}) collective-permute-start(bf16[1,256,256]{2,1,0:T(8,128)(2,1)} %bitcast.240), channel_id=1, source_target_pairs={{0,8},{2,10},{4,12},{6,14},{8,0},{10,2},{12,4},{14,6},{1,9},{3,11}... | collective-permute-start | bytes 393224 | tf_op jit(solution)/shard_map/ppermute | solution.py:23
  15.1 2.1 %multiply_reduce_fusion = f32[256]{0:T(256)S(1)} fusion(bf16[256,4096]{1,0:T(8,128)(2,1)} %param.17), kind=kLoop, calls=%fused_computation.8 | loop fusion | flops 3145472 | bytes 2098176 | tf_op jit(solution)/shard_map/reduce_sum | solution.py:140
  19.6 2.4 %convolution_convert_fusion = bf16[256,768]{1,0:T(8,128)(2,1)} fusion(bf16[256,256]{1,0:T(8,128)(2,1)} %param.21, bf16[256,256]{1,0:T(8,128)(2,1)} %param.20, bf16[256,256]{1,0:T(8,128)(2,1)} %param.19, f32[256]{0:T(256)S(1)} %dynamic_slice.17, f32[256]{0:T(256)S(1)} %add_rsqrt_fusion, bf16[256,4096]{1,0:T(8,128)(2,1)} %param.17, s32[]{:T(128)S(6)} %select_n.869, ...), kind=kOutput, calls=%fused_computation.9 | convolution fusion | flops 135987200 | bytes 920580 | tf_op jit(solution)/shard_map/dot_general | solution.py:147
  22.0 4.8 %all-to-all-start.1 = ((bf16[16,16,768]{2,1,0:T(8,128)(2,1)}), bf16[16,16,768]{2,1,0:T(8,128)(2,1)S(1)}, u32[]{:S(2)}, u32[]{:S(2)}) async-start(bf16[16,16,768]{2,1,0:T(8,128)(2,1)} %bitcast.1), calls=%async_computation.1 | async-start | bytes 786432 | tf_op jit(solution)/shard_map/all_to_all | solution.py:15
  27.2 11.4 %all-to-all-done.1 = bf16[16,16,768]{2,1,0:T(8,128)(2,1)S(1)} async-done(((bf16[16,16,768]{2,1,0:T(8,128)(2,1)}), bf16[16,16,768]{2,1,0:T(8,128)(2,1)S(1)}, u32[]{:S(2)}, u32[]{:S(2)}) %all-to-all-start.1) | async-done | bytes 393248 | tf_op jit(solution)/shard_map/all_to_all | solution.py:15
  39.1 1.6 %collective-permute-start.2 = (bf16[5,16,256]{2,1,0:T(8,128)(2,1)S(1)}, bf16[5,16,256]{2,1,0:T(8,128)(2,1)S(1)}, u32[]{:S(2)}, u32[]{:S(2)}) collective-permute-start(bf16[5,16,256]{2,1,0:T(8,128)(2,1)S(1)} %get-tuple-element.72), channel_id=1, source_target_pairs={{0,16},{16,0},{32,48},{48,32},{1,17},{17,1},{33,49},{49,33},{2,18}... | collective-permute-start | bytes 122888 | tf_op jit(solution)/shard_map/ppermute | solution.py:23
  40.7 2.7 %collective-permute-start.1 = (bf16[5,16,256]{2,1,0:T(8,128)(2,1)S(1)}, bf16[5,16,256]{2,1,0:T(8,128)(2,1)S(1)}, u32[]{:S(2)}, u32[]{:S(2)}) collective-permute-start(bf16[5,16,256]{2,1,0:T(8,128)(2,1)S(1)} %get-tuple-element.73), channel_id=1, source_target_pairs={{0,32},{16,48},{32,0},{48,16},{1,33},{17,49},{33,1},{49,17},{2,34}... | collective-permute-start | bytes 122888 | tf_op jit(solution)/shard_map/ppermute | solution.py:23
  44.1 2.2 %collective-permute-done.1 = bf16[5,16,256]{2,1,0:T(8,128)(2,1)S(1)} collective-permute-done((bf16[5,16,256]{2,1,0:T(8,128)(2,1)S(1)}, bf16[5,16,256]{2,1,0:T(8,128)(2,1)S(1)}, u32[]{:S(2)}, u32[]{:S(2)}) %collective-permute-start.1) | collective-permute-done | bytes 40992 | tf_op jit(solution)/shard_map/ppermute | solution.py:23
  46.3 2.3 %collective-permute-done = bf16[5,16,256]{2,1,0:T(8,128)(2,1)S(1)} collective-permute-done((bf16[5,16,256]{2,1,0:T(8,128)(2,1)S(1)}, bf16[5,16,256]{2,1,0:T(8,128)(2,1)S(1)}, u32[]{:S(2)}, u32[]{:S(2)}) %collective-permute-start) | collective-permute-done | bytes 40992 | tf_op jit(solution)/shard_map/ppermute | solution.py:23
  48.8 1.7 %collective-permute-start.5 = (bf16[8,16,256]{2,1,0:T(8,128)(2,1)S(1)}, bf16[8,16,256]{2,1,0:T(8,128)(2,1)S(1)}, u32[]{:S(2)}, u32[]{:S(2)}) collective-permute-start(bf16[8,16,256]{2,1,0:T(8,128)(2,1)S(1)} %get-tuple-element.67), channel_id=1, source_target_pairs={{0,64},{64,0},{128,192},{192,128},{1,65},{65,1},{129,193},{193,129... | collective-permute-start | bytes 196616 | tf_op jit(solution)/shard_map/ppermute | solution.py:23
  50.4 2.9 %collective-permute-start.4 = (bf16[8,16,256]{2,1,0:T(8,128)(2,1)S(1)}, bf16[8,16,256]{2,1,0:T(8,128)(2,1)S(1)}, u32[]{:S(2)}, u32[]{:S(2)}) collective-permute-start(bf16[8,16,256]{2,1,0:T(8,128)(2,1)S(1)} %get-tuple-element.68), channel_id=1, source_target_pairs={{0,128},{64,192},{128,0},{192,64},{1,129},{65,193},{129,1},{193,65... | collective-permute-start | bytes 196616 | tf_op jit(solution)/shard_map/ppermute | solution.py:23
  53.6 2.7 %collective-permute-done.4 = bf16[8,16,256]{2,1,0:T(8,128)(2,1)S(1)} collective-permute-done((bf16[8,16,256]{2,1,0:T(8,128)(2,1)S(1)}, bf16[8,16,256]{2,1,0:T(8,128)(2,1)S(1)}, u32[]{:S(2)}, u32[]{:S(2)}) %collective-permute-start.4) | collective-permute-done | bytes 65568 | tf_op jit(solution)/shard_map/ppermute | solution.py:23
  56.4 2.4 %collective-permute-done.3 = bf16[8,16,256]{2,1,0:T(8,128)(2,1)S(1)} collective-permute-done((bf16[8,16,256]{2,1,0:T(8,128)(2,1)S(1)}, bf16[8,16,256]{2,1,0:T(8,128)(2,1)S(1)}, u32[]{:S(2)}, u32[]{:S(2)}) %collective-permute-start.3) | collective-permute-done | bytes 65568 | tf_op jit(solution)/shard_map/ppermute | solution.py:23
  63.3 3.2 %collective-permute-start.6 = (bf16[144,128]{1,0:T(8,128)(2,1)S(1)}, bf16[144,128]{1,0:T(8,128)(2,1)S(1)}, u32[]{:S(2)}, u32[]{:S(2)}) collective-permute-start(bf16[144,128]{1,0:T(8,128)(2,1)S(1)} %pad_maximum_fusion.14), channel_id=1, source_target_pairs={{0,64},{64,0},{128,192},{192,128},{1,65},{65,1},{129,193},{193,129... | collective-permute-start | bytes 110600 | tf_op jit(solution)/shard_map/ppermute | solution.py:23
  66.8 2.8 %collective-permute-start.16 = (bf16[2,256,256]{2,1,0:T(8,128)(2,1)S(1)}, bf16[2,256,256]{2,1,0:T(8,128)(2,1)S(1)}, u32[]{:S(2)}, u32[]{:S(2)}) collective-permute-start(bf16[2,256,256]{2,1,0:T(8,128)(2,1)S(1)} %pad_maximum_fusion.3), channel_id=1, source_target_pairs={{0,4},{2,6},{4,0},{6,2},{8,12},{10,14},{12,8},{14,10},{1,5},{3,7},... | collective-permute-start | bytes 786440 | tf_op jit(solution)/shard_map/ppermute | solution.py:23
  70.3 7.4 %collective-permute-done.16 = bf16[2,256,256]{2,1,0:T(8,128)(2,1)S(1)} collective-permute-done((bf16[2,256,256]{2,1,0:T(8,128)(2,1)S(1)}, bf16[2,256,256]{2,1,0:T(8,128)(2,1)S(1)}, u32[]{:S(2)}, u32[]{:S(2)}) %collective-permute-start.16) | collective-permute-done | bytes 262176 | tf_op jit(solution)/shard_map/ppermute | solution.py:23
  77.8 2.4 %collective-permute-start.17 = (bf16[4,256,256]{2,1,0:T(8,128)(2,1)S(1)}, bf16[4,256,256]{2,1,0:T(8,128)(2,1)S(1)}, u32[]{:S(2)}, u32[]{:S(2)}) collective-permute-start(bf16[4,256,256]{2,1,0:T(8,128)(2,1)S(1)} %pad_maximum_fusion.1), channel_id=1, source_target_pairs={{0,2},{2,0},{4,6},{6,4},{8,10},{10,8},{12,14},{14,12},{1,3},{3,1},... | collective-permute-start | bytes 1572872 | tf_op jit(solution)/shard_map/ppermute | solution.py:23
  81.5 2.9 %collective-permute-start.9 = (bf16[144,128]{1,0:T(8,128)(2,1)S(1)}, bf16[144,128]{1,0:T(8,128)(2,1)S(1)}, u32[]{:S(2)}, u32[]{:S(2)}) collective-permute-start(bf16[144,128]{1,0:T(8,128)(2,1)S(1)} %pad_maximum_fusion.17), channel_id=1, source_target_pairs={{0,16},{16,0},{32,48},{48,32},{1,17},{17,1},{33,49},{49,33},{2,18}... | collective-permute-start | bytes 110600 | tf_op jit(solution)/shard_map/ppermute | solution.py:23
  86.9 4.3 %collective-permute-done.17 = bf16[4,256,256]{2,1,0:T(8,128)(2,1)S(1)} collective-permute-done((bf16[4,256,256]{2,1,0:T(8,128)(2,1)S(1)}, bf16[4,256,256]{2,1,0:T(8,128)(2,1)S(1)}, u32[]{:S(2)}, u32[]{:S(2)}) %collective-permute-start.17) | collective-permute-done | bytes 524320 | tf_op jit(solution)/shard_map/ppermute | solution.py:23
  92.9 2.3 %collective-permute-start.13 = (bf16[4,16,256]{2,1,0:T(8,128)(2,1)S(1)}, bf16[4,16,256]{2,1,0:T(8,128)(2,1)S(1)}, u32[]{:S(2)}, u32[]{:S(2)}) collective-permute-start(bf16[4,16,256]{2,1,0:T(8,128)(2,1)S(1)} %bitcast.245), channel_id=1, source_target_pairs={{0,128},{64,192},{128,0},{192,64},{1,129},{65,193},{129,1},{193,65... | collective-permute-start | bytes 98312 | tf_op jit(solution)/shard_map/ppermute | solution.py:23
  102.5 2.7 %collective-permute-start.19 = (f32[16,256]{1,0:T(8,128)S(1)}, f32[16,256]{1,0:T(8,128)S(1)}, u32[]{:S(2)}, u32[]{:S(2)}) collective-permute-start(f32[16,256]{1,0:T(8,128)S(1)} %convolution_select_fusion), channel_id=1, source_target_pairs={{0,16},{16,0},{32,48},{48,32},{1,17},{17,1},{33,49},{49,33},{2,18}... | collective-permute-start | bytes 49160 | tf_op jit(solution)/shard_map/ppermute | solution.py:23
  107.2 2.2 %collective-permute-start.24 = (f32[16,256]{1,0:T(8,128)S(1)}, f32[16,256]{1,0:T(8,128)S(1)}, u32[]{:S(2)}, u32[]{:S(2)}) collective-permute-start(f32[16,256]{1,0:T(8,128)S(1)} %add_add_fusion.1), channel_id=1, source_target_pairs={{0,192},{64,128},{128,64},{192,0},{1,193},{65,129},{129,65},{193,1... | collective-permute-start | bytes 49160 | tf_op jit(solution)/shard_map/ppermute | solution.py:23
  112.2 2.4 %collective-permute-done.23 = f32[16,256]{1,0:T(8,128)S(1)} collective-permute-done((f32[16,256]{1,0:T(8,128)S(1)}, f32[16,256]{1,0:T(8,128)S(1)}, u32[]{:S(2)}, u32[]{:S(2)}) %collective-permute-start.23) | collective-permute-done | bytes 16416 | tf_op jit(solution)/shard_map/ppermute | solution.py:23
  (156 shorter events, 30.1 us)
Async XLA Ops:
  1.3 18.2 %all-to-all-start = ((s32[16,2,7]{2,1,0:T(2,128)}), s32[16,2,7]{2,1,0:T(2,128)S(1)}, u32[]{:S(2)}, u32[]{:S(2)}) async-start(s32[16,2,7]{2,1,0:T(2,128)} %broadcast_in_dim.164), calls=%async_computation | async-start | bytes 32768 | tf_op jit(solution)/shard_map/all_to_all | solution.py:15
  9.9 17.2 %collective-permute-start.15 = (bf16[1,256,256]{2,1,0:T(8,128)(2,1)}, bf16[1,256,256]{2,1,0:T(8,128)(2,1)S(1)}, u32[]{:S(2)}, u32[]{:S(2)}) collective-permute-start(bf16[1,256,256]{2,1,0:T(8,128)(2,1)} %bitcast.240), channel_id=1, source_target_pairs={{0,8},{2,10},{4,12},{6,14},{8,0},{10,2},{12,4},{14,6},{1,9},{3,11}... | collective-permute-start | bytes 393224 | tf_op jit(solution)/shard_map/ppermute | solution.py:23
  22.0 16.6 %all-to-all-start.1 = ((bf16[16,16,768]{2,1,0:T(8,128)(2,1)}), bf16[16,16,768]{2,1,0:T(8,128)(2,1)S(1)}, u32[]{:S(2)}, u32[]{:S(2)}) async-start(bf16[16,16,768]{2,1,0:T(8,128)(2,1)} %bitcast.1), calls=%async_computation.1 | async-start | bytes 786432 | tf_op jit(solution)/shard_map/all_to_all | solution.py:15
  39.1 5.0 %collective-permute-start.2 = (bf16[5,16,256]{2,1,0:T(8,128)(2,1)S(1)}, bf16[5,16,256]{2,1,0:T(8,128)(2,1)S(1)}, u32[]{:S(2)}, u32[]{:S(2)}) collective-permute-start(bf16[5,16,256]{2,1,0:T(8,128)(2,1)S(1)} %get-tuple-element.72), channel_id=1, source_target_pairs={{0,16},{16,0},{32,48},{48,32},{1,17},{17,1},{33,49},{49,33},{2,18}... | collective-permute-start | bytes 122888 | tf_op jit(solution)/shard_map/ppermute | solution.py:23
  40.7 5.6 %collective-permute-start.1 = (bf16[5,16,256]{2,1,0:T(8,128)(2,1)S(1)}, bf16[5,16,256]{2,1,0:T(8,128)(2,1)S(1)}, u32[]{:S(2)}, u32[]{:S(2)}) collective-permute-start(bf16[5,16,256]{2,1,0:T(8,128)(2,1)S(1)} %get-tuple-element.73), channel_id=1, source_target_pairs={{0,32},{16,48},{32,0},{48,16},{1,33},{17,49},{33,1},{49,17},{2,34}... | collective-permute-start | bytes 122888 | tf_op jit(solution)/shard_map/ppermute | solution.py:23
  43.4 5.2 %collective-permute-start = (bf16[5,16,256]{2,1,0:T(8,128)(2,1)S(1)}, bf16[5,16,256]{2,1,0:T(8,128)(2,1)S(1)}, u32[]{:S(2)}, u32[]{:S(2)}) collective-permute-start(bf16[5,16,256]{2,1,0:T(8,128)(2,1)S(1)} %get-tuple-element.74), channel_id=1, source_target_pairs={{0,48},{16,32},{32,16},{48,0},{1,49},{17,33},{33,17},{49,1},{2,50}... | collective-permute-start | bytes 122888 | tf_op jit(solution)/shard_map/ppermute | solution.py:23
  48.8 4.9 %collective-permute-start.5 = (bf16[8,16,256]{2,1,0:T(8,128)(2,1)S(1)}, bf16[8,16,256]{2,1,0:T(8,128)(2,1)S(1)}, u32[]{:S(2)}, u32[]{:S(2)}) collective-permute-start(bf16[8,16,256]{2,1,0:T(8,128)(2,1)S(1)} %get-tuple-element.67), channel_id=1, source_target_pairs={{0,64},{64,0},{128,192},{192,128},{1,65},{65,1},{129,193},{193,129... | collective-permute-start | bytes 196616 | tf_op jit(solution)/shard_map/ppermute | solution.py:23
  50.4 5.9 %collective-permute-start.4 = (bf16[8,16,256]{2,1,0:T(8,128)(2,1)S(1)}, bf16[8,16,256]{2,1,0:T(8,128)(2,1)S(1)}, u32[]{:S(2)}, u32[]{:S(2)}) collective-permute-start(bf16[8,16,256]{2,1,0:T(8,128)(2,1)S(1)} %get-tuple-element.68), channel_id=1, source_target_pairs={{0,128},{64,192},{128,0},{192,64},{1,129},{65,193},{129,1},{193,65... | collective-permute-start | bytes 196616 | tf_op jit(solution)/shard_map/ppermute | solution.py:23
  53.3 5.5 %collective-permute-start.3 = (bf16[8,16,256]{2,1,0:T(8,128)(2,1)S(1)}, bf16[8,16,256]{2,1,0:T(8,128)(2,1)S(1)}, u32[]{:S(2)}, u32[]{:S(2)}) collective-permute-start(bf16[8,16,256]{2,1,0:T(8,128)(2,1)S(1)} %get-tuple-element.69), channel_id=1, source_target_pairs={{0,192},{64,128},{128,64},{192,0},{1,193},{65,129},{129,65},{193,1... | collective-permute-start | bytes 196616 | tf_op jit(solution)/shard_map/ppermute | solution.py:23
  62.0 7.9 %collective-permute-start.8 = (bf16[144,128]{1,0:T(8,128)(2,1)S(1)}, bf16[144,128]{1,0:T(8,128)(2,1)S(1)}, u32[]{:S(2)}, u32[]{:S(2)}) collective-permute-start(bf16[144,128]{1,0:T(8,128)(2,1)S(1)} %pad_maximum_fusion.16), channel_id=1, source_target_pairs={{0,192},{64,128},{128,64},{192,0},{1,193},{65,129},{129,65},{193,1... | collective-permute-start | bytes 110600 | tf_op jit(solution)/shard_map/ppermute | solution.py:23
  62.4 7.5 %collective-permute-start.7 = (bf16[144,128]{1,0:T(8,128)(2,1)S(1)}, bf16[144,128]{1,0:T(8,128)(2,1)S(1)}, u32[]{:S(2)}, u32[]{:S(2)}) collective-permute-start(bf16[144,128]{1,0:T(8,128)(2,1)S(1)} %pad_maximum_fusion.15), channel_id=1, source_target_pairs={{0,128},{64,192},{128,0},{192,64},{1,129},{65,193},{129,1},{193,65... | collective-permute-start | bytes 110600 | tf_op jit(solution)/shard_map/ppermute | solution.py:23
  63.3 6.7 %collective-permute-start.6 = (bf16[144,128]{1,0:T(8,128)(2,1)S(1)}, bf16[144,128]{1,0:T(8,128)(2,1)S(1)}, u32[]{:S(2)}, u32[]{:S(2)}) collective-permute-start(bf16[144,128]{1,0:T(8,128)(2,1)S(1)} %pad_maximum_fusion.14), channel_id=1, source_target_pairs={{0,64},{64,0},{128,192},{192,128},{1,65},{65,1},{129,193},{193,129... | collective-permute-start | bytes 110600 | tf_op jit(solution)/shard_map/ppermute | solution.py:23
  66.8 10.9 %collective-permute-start.16 = (bf16[2,256,256]{2,1,0:T(8,128)(2,1)S(1)}, bf16[2,256,256]{2,1,0:T(8,128)(2,1)S(1)}, u32[]{:S(2)}, u32[]{:S(2)}) collective-permute-start(bf16[2,256,256]{2,1,0:T(8,128)(2,1)S(1)} %pad_maximum_fusion.3), channel_id=1, source_target_pairs={{0,4},{2,6},{4,0},{6,2},{8,12},{10,14},{12,8},{14,10},{1,5},{3,7},... | collective-permute-start | bytes 786440 | tf_op jit(solution)/shard_map/ppermute | solution.py:23
  77.8 13.4 %collective-permute-start.17 = (bf16[4,256,256]{2,1,0:T(8,128)(2,1)S(1)}, bf16[4,256,256]{2,1,0:T(8,128)(2,1)S(1)}, u32[]{:S(2)}, u32[]{:S(2)}) collective-permute-start(bf16[4,256,256]{2,1,0:T(8,128)(2,1)S(1)} %pad_maximum_fusion.1), channel_id=1, source_target_pairs={{0,2},{2,0},{4,6},{6,4},{8,10},{10,8},{12,14},{14,12},{1,3},{3,1},... | collective-permute-start | bytes 1572872 | tf_op jit(solution)/shard_map/ppermute | solution.py:23
  80.2 5.2 %collective-permute-start.11 = (bf16[144,128]{1,0:T(8,128)(2,1)S(1)}, bf16[144,128]{1,0:T(8,128)(2,1)S(1)}, u32[]{:S(2)}, u32[]{:S(2)}) collective-permute-start(bf16[144,128]{1,0:T(8,128)(2,1)S(1)} %pad_maximum_fusion.17), channel_id=1, source_target_pairs={{0,48},{16,32},{32,16},{48,0},{1,49},{17,33},{33,17},{49,1},{2,50}... | collective-permute-start | bytes 110600 | tf_op jit(solution)/shard_map/ppermute | solution.py:23
  80.9 5.5 %collective-permute-start.10 = (bf16[144,128]{1,0:T(8,128)(2,1)S(1)}, bf16[144,128]{1,0:T(8,128)(2,1)S(1)}, u32[]{:S(2)}, u32[]{:S(2)}) collective-permute-start(bf16[144,128]{1,0:T(8,128)(2,1)S(1)} %pad_maximum_fusion.17), channel_id=1, source_target_pairs={{0,32},{16,48},{32,0},{48,16},{1,33},{17,49},{33,1},{49,17},{2,34}... | collective-permute-start | bytes 110600 | tf_op jit(solution)/shard_map/ppermute | solution.py:23
  81.5 5.2 %collective-permute-start.9 = (bf16[144,128]{1,0:T(8,128)(2,1)S(1)}, bf16[144,128]{1,0:T(8,128)(2,1)S(1)}, u32[]{:S(2)}, u32[]{:S(2)}) collective-permute-start(bf16[144,128]{1,0:T(8,128)(2,1)S(1)} %pad_maximum_fusion.17), channel_id=1, source_target_pairs={{0,16},{16,0},{32,48},{48,32},{1,17},{17,1},{33,49},{49,33},{2,18}... | collective-permute-start | bytes 110600 | tf_op jit(solution)/shard_map/ppermute | solution.py:23
  91.3 9.3 %collective-permute-start.18 = (bf16[8,256,256]{2,1,0:T(8,128)(2,1)S(1)}, bf16[8,256,256]{2,1,0:T(8,128)(2,1)S(1)}, u32[]{:S(2)}, u32[]{:S(2)}) collective-permute-start(bf16[8,256,256]{2,1,0:T(8,128)(2,1)S(1)} %pad_maximum_fusion), channel_id=1, source_target_pairs={{0,1},{1,0},{2,3},{3,2},{4,5},{5,4},{6,7},{7,6},{8,9},{9,8},{10,11... | collective-permute-start | bytes 3145736 | tf_op jit(solution)/shard_map/ppermute | solution.py:23
  92.5 5.4 %collective-permute-start.14 = (bf16[4,16,256]{2,1,0:T(8,128)(2,1)S(1)}, bf16[4,16,256]{2,1,0:T(8,128)(2,1)S(1)}, u32[]{:S(2)}, u32[]{:S(2)}) collective-permute-start(bf16[4,16,256]{2,1,0:T(8,128)(2,1)S(1)} %bitcast.244), channel_id=1, source_target_pairs={{0,192},{64,128},{128,64},{192,0},{1,193},{65,129},{129,65},{193,1... | collective-permute-start | bytes 98312 | tf_op jit(solution)/shard_map/ppermute | solution.py:23
  92.9 5.4 %collective-permute-start.13 = (bf16[4,16,256]{2,1,0:T(8,128)(2,1)S(1)}, bf16[4,16,256]{2,1,0:T(8,128)(2,1)S(1)}, u32[]{:S(2)}, u32[]{:S(2)}) collective-permute-start(bf16[4,16,256]{2,1,0:T(8,128)(2,1)S(1)} %bitcast.245), channel_id=1, source_target_pairs={{0,128},{64,192},{128,0},{192,64},{1,129},{65,193},{129,1},{193,65... | collective-permute-start | bytes 98312 | tf_op jit(solution)/shard_map/ppermute | solution.py:23
  101.1 5.0 %collective-permute-start.21 = (f32[16,256]{1,0:T(8,128)S(1)}, f32[16,256]{1,0:T(8,128)S(1)}, u32[]{:S(2)}, u32[]{:S(2)}) collective-permute-start(f32[16,256]{1,0:T(8,128)S(1)} %convolution_select_fusion), channel_id=1, source_target_pairs={{0,48},{16,32},{32,16},{48,0},{1,49},{17,33},{33,17},{49,1},{2,50}... | collective-permute-start | bytes 49160 | tf_op jit(solution)/shard_map/ppermute | solution.py:23
  101.9 5.2 %collective-permute-start.20 = (f32[16,256]{1,0:T(8,128)S(1)}, f32[16,256]{1,0:T(8,128)S(1)}, u32[]{:S(2)}, u32[]{:S(2)}) collective-permute-start(f32[16,256]{1,0:T(8,128)S(1)} %convolution_select_fusion), channel_id=1, source_target_pairs={{0,32},{16,48},{32,0},{48,16},{1,33},{17,49},{33,1},{49,17},{2,34}... | collective-permute-start | bytes 49160 | tf_op jit(solution)/shard_map/ppermute | solution.py:23
  107.2 5.0 %collective-permute-start.24 = (f32[16,256]{1,0:T(8,128)S(1)}, f32[16,256]{1,0:T(8,128)S(1)}, u32[]{:S(2)}, u32[]{:S(2)}) collective-permute-start(f32[16,256]{1,0:T(8,128)S(1)} %add_add_fusion.1), channel_id=1, source_target_pairs={{0,192},{64,128},{128,64},{192,0},{1,193},{65,129},{129,65},{193,1... | collective-permute-start | bytes 49160 | tf_op jit(solution)/shard_map/ppermute | solution.py:23
  109.4 5.2 %collective-permute-start.23 = (f32[16,256]{1,0:T(8,128)S(1)}, f32[16,256]{1,0:T(8,128)S(1)}, u32[]{:S(2)}, u32[]{:S(2)}) collective-permute-start(f32[16,256]{1,0:T(8,128)S(1)} %add_add_fusion.1), channel_id=1, source_target_pairs={{0,128},{64,192},{128,0},{192,64},{1,129},{65,193},{129,1},{193,65... | collective-permute-start | bytes 49160 | tf_op jit(solution)/shard_map/ppermute | solution.py:23
  (9 other events, 153.5 us)

commit v3 on v2

--- a/solution.py
+++ b/solution.py
@@ -148,32 +148,36 @@
     sums = exchange(terms.reshape(groups, rows, 3 * cols), GRP)
     sums = jnp.sum(sums.astype(jnp.float32), axis=0)
 
+    head = after(head, terms).reshape(own_bins, side, side, cols).transpose(2, 1, 0, 3)
+    head = in_order([head[k] for k in range(side)], "seq_1")
+    head = (head[0], *(from_partner(head[k], "seq_1", k) for k in (1, 2, 3)))
+    head = jnp.stack(in_order(head, "seq_1"), axis=1)
+    head = in_order([head[k] for k in range(side)], "seq_0")
+    head = (head[0], *(from_partner(head[k], "seq_0", k) for k in (1, 2, 3)))
+    head_cols = jnp.stack(in_order(head, "seq_0")).reshape(bins, cols)
+    own_hot = (after(actions, terms).reshape(rows)[:, None] == bin_ids[None, :]).astype(jnp.bfloat16)
+    own_embed = lax.dynamic_slice(embed, (0, s * cols), (bins, cols))
+    inputs = jnp.dot(own_hot, own_embed, preferred_element_type=jnp.float32)
+    own_gain = lax.dynamic_slice(after(final_gain, terms), (s * cols,), (cols,))
+    lengths = after(lengths, terms)
+
     blocks = after(blocks, sums)
     blocks = jnp.concatenate([blocks, from_partner(blocks, "z", 2)], axis=0)
     zs = zs + [m ^ 2 for m in zs]
 
+    (sums, head_cols, inputs, own_gain, lengths) = lax.optimization_barrier(
+        (sums, head_cols, inputs, own_gain, lengths)
+    )
     places = (lengths[:, None] + jnp.arange(steps, dtype=jnp.int32)[None, :]).astype(jnp.float32)
     heads_of = lambda flat: flat.reshape(robots, steps, lh, HEAD_DIM)
     query = rotate(heads_of(sums[:, :cols]), places).astype(jnp.bfloat16)
     key = rotate(heads_of(sums[:, cols : 2 * cols]), places).astype(jnp.bfloat16)
     value = heads_of(sums[:, 2 * cols :]).astype(jnp.bfloat16)
 
-    flat_query = query.reshape(1, rows, cols)
-    head_parts = head.reshape(own_bins, side, side, cols).transpose(2, 1, 0, 3)
-    head_parts = in_order([head_parts[k] for k in range(side)], "seq_1")
-    near = [jnp.concatenate([flat_query, head_parts[0]], axis=0)]
-    for k in (1, 2, 3):
-        sent = jnp.concatenate([flat_query, head_parts[k]], axis=0)
-        near.append(from_partner(sent, "seq_1", k))
-    near = jnp.stack(in_order(near, "seq_1"))
-    head_parts = in_order([near[:, 1 + k] for k in range(side)], "seq_0")
-    far = [jnp.concatenate([near[:, 0], head_parts[0]], axis=0)]
-    for k in (1, 2, 3):
-        sent = jnp.concatenate([near[:, 0], head_parts[k]], axis=0)
-        far.append(from_partner(sent, "seq_0", k))
-    far = jnp.stack(in_order(far, "seq_0"))
-    all_query = far[:, :side].reshape(seqs, robots, steps, lh, HEAD_DIM)
-    head_cols = far[:, side:].reshape(bins, cols)
+    flat_query = query.reshape(rows, cols)
+    near = jnp.stack(in_order(from_all(flat_query, "seq_1"), "seq_1"))
+    far = jnp.stack(in_order(from_all(near, "seq_0"), "seq_0"))
+    all_query = far.reshape(seqs, robots, steps, lh, HEAD_DIM)
 
     prompt_ids = s * prompt_dev + jnp.arange(prompt_dev, dtype=jnp.int32)
     mask = (prompt_ids[None, :] < lengths[:, None])[:, None, None, :]
@@ -245,11 +249,8 @@
     branch = jnp.dot(take(order + core), blocks.reshape(-1, cols), preferred_element_type=jnp.float32)
     branch += jnp.dot(take(order + 1 - core), other.reshape(-1, cols), preferred_element_type=jnp.float32)
 
-    own_hot = (actions.reshape(rows)[:, None] == bin_ids[None, :]).astype(jnp.bfloat16)
-    own_embed = lax.dynamic_slice(embed, (0, s * cols), (bins, cols))
-    inputs = jnp.dot(own_hot, own_embed, preferred_element_type=jnp.float32)
     residual = inputs + branch
-    gained = (residual * lax.dynamic_slice(final_gain, (s * cols,), (cols,))).astype(jnp.bfloat16)
+    gained = (residual * own_gain).astype(jnp.bfloat16)
     part_logits = lax.dot_general(
         gained, head_cols, (((1,), (1,)), ((), ())), preferred_element_type=jnp.float32
     )

time: 118 us -> 122 us (1.034)
  starting transfers between devices: 53.7 us -> 63.4 us
  waiting for transfers between devices: 41.8 us -> 34.3 us
  matrix products: 6.67 us -> 8.85 us
    ppermute x25 -> x31, starting transfers between devices: 40.3 us -> 50.1 us  [from_partner(): lax.ppermute(x, axis, [(i, i ^ k) for i in range(lax.axis_size(axis))])]
    all_to_all x2, waiting for transfers between devices: 11.4 us -> 2.48 us  [exchange(): return lax.all_to_all(pieces, axis, split_axis=0, concat_axis=0, tiled=True)]
    dot_general x1, matrix products: 1.26 us -> 3.45 us  [on_device(): jnp.einsum('rthd,rphd->rhtp', q, cache_keys, preferred_element_type=jnp.f...]
    ppermute x25 -> x31, waiting for transfers between devices: 30.4 us -> 31.9 us  [from_partner(): lax.ppermute(x, axis, [(i, i ^ k) for i in range(lax.axis_size(axis))])]
  transfers between devices with their start and end apart: 27 -> 33, of which waited for: 18 -> 19; matrix products, arithmetic and copies ran while one was open for 11% -> 10% of each run, Pallas kernels for 0% -> 0%
where the time goes in v3:
time: 122 us; the launch traced here: 120 us
  starting transfers between devices  63.4 us (52%)
  waiting for transfers between devices  34.3 us (28%)
  matrix products  8.85 us (7%)
  local copies, waits for them, and re-layouts  7.31 us (6%)
  other arithmetic  5.06 us (4%)
    ppermute x31, starting transfers between devices, from_partner(): lax.ppermute(x, axis, [(i, i ^ k) for i in range(lax.axis_size(axis))])  50.1 us
    ppermute x31, waiting for transfers between devices, from_partner(): lax.ppermute(x, axis, [(i, i ^ k) for i in range(lax.axis_size(axis))])  31.9 us
    all_to_all x2, starting transfers between devices, exchange(): return lax.all_to_all(pieces, axis, split_axis=0, concat_axis=0, tiled=True)  13.4 us
    dot_general x1, matrix products, on_device(): jnp.einsum('rthd,rphd->rhtp', q, cache_keys, preferred_element_type=jnp.f...  3.45 us
    all_to_all x2, waiting for transfers between devices, exchange(): return lax.all_to_all(pieces, axis, split_axis=0, concat_axis=0, tiled=True)  2.48 us
  transfers between devices with their start and end apart: 33, of which 19 were waited for; matrix products, arithmetic and copies ran while one was open for 10% of the time, Pallas kernels for 0%

profile of v3, /device:TPU:32, one launch (start us, length us, event | category | flops | bytes accessed | tf_op | source)
XLA Modules:
  0.0 119.6 jit_solution(3087113509223535067)
XLA Ops:
  1.4 8.6 %all-to-all-start = ((s32[16,2,7]{2,1,0:T(2,128)}), s32[16,2,7]{2,1,0:T(2,128)S(1)}, u32[]{:S(2)}, u32[]{:S(2)}) async-start(s32[16,2,7]{2,1,0:T(2,128)} %broadcast_in_dim.163), calls=%async_computation | async-start | bytes 32768 | tf_op jit(solution)/shard_map/all_to_all | solution.py:15
  9.9 4.5 %collective-permute-start.21 = (bf16[1,256,256]{2,1,0:T(8,128)(2,1)}, bf16[1,256,256]{2,1,0:T(8,128)(2,1)S(1)}, u32[]{:S(2)}, u32[]{:S(2)}) collective-permute-start(bf16[1,256,256]{2,1,0:T(8,128)(2,1)} %bitcast.270), channel_id=1, source_target_pairs={{0,8},{2,10},{4,12},{6,14},{8,0},{10,2},{12,4},{14,6},{1,9},{3,11}... | collective-permute-start | bytes 393224 | tf_op jit(solution)/shard_map/ppermute | solution.py:23
  14.4 2.1 %multiply_reduce_fusion = f32[256]{0:T(256)S(1)} fusion(bf16[256,4096]{1,0:T(8,128)(2,1)} %param.17), kind=kLoop, calls=%fused_computation.8 | loop fusion | flops 3145472 | bytes 2098176 | tf_op jit(solution)/shard_map/reduce_sum | solution.py:140
  17.4 2.4 %convolution_convert_fusion = bf16[256,768]{1,0:T(8,128)(2,1)} fusion(bf16[256,256]{1,0:T(8,128)(2,1)} %param.21, bf16[256,256]{1,0:T(8,128)(2,1)} %param.20, bf16[256,256]{1,0:T(8,128)(2,1)} %param.19, f32[256]{0:T(256)S(1)} %dynamic_slice.16, f32[256]{0:T(256)S(1)} %add_rsqrt_fusion, bf16[256,4096]{1,0:T(8,128)(2,1)} %param.17, s32[]{:T(128)S(6)} %select_n.928, ...), kind=kOutput, calls=%fused_computation.9 | convolution fusion | flops 135987200 | bytes 920580 | tf_op jit(solution)/shard_map/dot_general | solution.py:147
  21.2 2.8 %collective-permute-start = (bf16[4,16,256]{2,1,0:T(8,128)(2,1)S(1)}, bf16[4,16,256]{2,1,0:T(8,128)(2,1)S(1)}, u32[]{:S(2)}, u32[]{:S(2)}) collective-permute-start(bf16[4,16,256]{2,1,0:T(8,128)(2,1)S(1)} %bitcast.282), channel_id=1, source_target_pairs={{0,48},{16,32},{32,16},{48,0},{1,49},{17,33},{33,17},{49,1},{2,50}... | collective-permute-start | bytes 98312 | tf_op jit(solution)/shard_map/ppermute | solution.py:23
  26.3 4.8 %all-to-all-start.1 = ((bf16[16,16,768]{2,1,0:T(8,128)(2,1)}), bf16[16,16,768]{2,1,0:T(8,128)(2,1)S(1)}, u32[]{:S(2)}, u32[]{:S(2)}) async-start(bf16[16,16,768]{2,1,0:T(8,128)(2,1)} %bitcast.1), calls=%async_computation.1 | async-start | bytes 786432 | tf_op jit(solution)/shard_map/all_to_all | solution.py:15
  31.2 3.3 %collective-permute-start.4 = (bf16[4,16,256]{2,1,0:T(8,128)(2,1)S(1)}, bf16[4,16,256]{2,1,0:T(8,128)(2,1)S(1)}, u32[]{:S(2)}, u32[]{:S(2)}) collective-permute-start(bf16[4,16,256]{2,1,0:T(8,128)(2,1)S(1)} %get-tuple-element.50), channel_id=1, source_target_pairs={{0,128},{64,192},{128,0},{192,64},{1,129},{65,193},{129,1},{193,65... | collective-permute-start | bytes 98312 | tf_op jit(solution)/shard_map/ppermute | solution.py:23
  38.4 1.9 %collective-permute-done.3 = bf16[4,16,256]{2,1,0:T(8,128)(2,1)S(1)} collective-permute-done((bf16[4,16,256]{2,1,0:T(8,128)(2,1)S(1)}, bf16[4,16,256]{2,1,0:T(8,128)(2,1)S(1)}, u32[]{:S(2)}, u32[]{:S(2)}) %collective-permute-start.3) | collective-permute-done | bytes 32800 | tf_op jit(solution)/shard_map/ppermute | solution.py:23
  40.4 2.5 %all-to-all-done.1 = bf16[16,16,768]{2,1,0:T(8,128)(2,1)S(1)} async-done(((bf16[16,16,768]{2,1,0:T(8,128)(2,1)}), bf16[16,16,768]{2,1,0:T(8,128)(2,1)S(1)}, u32[]{:S(2)}, u32[]{:S(2)}) %all-to-all-start.1) | async-done | bytes 393248 | tf_op jit(solution)/shard_map/all_to_all | solution.py:15
  43.6 3.9 %collective-permute-start.7 = (bf16[16,256]{1,0:T(8,128)(2,1)S(1)}, bf16[16,256]{1,0:T(8,128)(2,1)S(1)}, u32[]{:S(2)}, u32[]{:S(2)}) collective-permute-start(bf16[16,256]{1,0:T(8,128)(2,1)S(1)} %fusion.154), channel_id=1, source_target_pairs={{0,32},{16,48},{32,0},{48,16},{1,33},{17,49},{33,1},{49,17},{2,34}... | collective-permute-start | bytes 24584 | tf_op jit(solution)/shard_map/ppermute | solution.py:23
  49.3 3.1 %collective-permute-done.6 = bf16[16,256]{1,0:T(8,128)(2,1)S(1)} collective-permute-done((bf16[16,256]{1,0:T(8,128)(2,1)S(1)}, bf16[16,256]{1,0:T(8,128)(2,1)S(1)}, u32[]{:S(2)}, u32[]{:S(2)}) %collective-permute-start.6) | collective-permute-done | bytes 8224 | tf_op jit(solution)/shard_map/ppermute | solution.py:23
  54.2 2.9 %collective-permute-start.10 = (bf16[4,16,256]{2,1,0:T(8,128)(2,1)S(1)}, bf16[4,16,256]{2,1,0:T(8,128)(2,1)S(1)}, u32[]{:S(2)}, u32[]{:S(2)}) collective-permute-start(bf16[4,16,256]{2,1,0:T(8,128)(2,1)S(1)} %pad_maximum_fusion.11), channel_id=1, source_target_pairs={{0,128},{64,192},{128,0},{192,64},{1,129},{65,193},{129,1},{193,65... | collective-permute-start | bytes 98312 | tf_op jit(solution)/shard_map/ppermute | solution.py:23
  57.3 2.4 %collective-permute-done.10 = bf16[4,16,256]{2,1,0:T(8,128)(2,1)S(1)} collective-permute-done((bf16[4,16,256]{2,1,0:T(8,128)(2,1)S(1)}, bf16[4,16,256]{2,1,0:T(8,128)(2,1)S(1)}, u32[]{:S(2)}, u32[]{:S(2)}) %collective-permute-start.10) | collective-permute-done | bytes 32800 | tf_op jit(solution)/shard_map/ppermute | solution.py:23
  59.7 2.5 %collective-permute-done.9 = bf16[4,16,256]{2,1,0:T(8,128)(2,1)S(1)} collective-permute-done((bf16[4,16,256]{2,1,0:T(8,128)(2,1)S(1)}, bf16[4,16,256]{2,1,0:T(8,128)(2,1)S(1)}, u32[]{:S(2)}, u32[]{:S(2)}) %collective-permute-start.9) | collective-permute-done | bytes 32800 | tf_op jit(solution)/shard_map/ppermute | solution.py:23
  62.3 3.5 %fusion.152 = (f32[2,32,8]{2,1,0:T(8,128)S(1)}, f32[2,32,8,256]{3,2,1,0:T(8,128)S(1)}) fusion(bf16[2,8,32,128]{3,1,2,0:T(8,128)(2,1)S(1)} %bitcast.265, pred[2,256]{1,0:T(4,128)(4,1)S(1)} %broadcast_compare_fusion, bf16[2,256,4096]{2,1,0:T(8,128)(2,1)} %param.23), kind=kOutput, calls=%fused_computation.349 | convolution fusion | flops 33947136 | bytes 4852224 | tf_op jit(solution)/shard_map/rthd,rphd->rhtp/dot_general | solution.py:187
  68.8 3.3 %collective-permute-start.13 = (bf16[144,128]{1,0:T(8,128)(2,1)S(1)}, bf16[144,128]{1,0:T(8,128)(2,1)S(1)}, u32[]{:S(2)}, u32[]{:S(2)}) collective-permute-start(bf16[144,128]{1,0:T(8,128)(2,1)S(1)} %pad_maximum_fusion.8), channel_id=1, source_target_pairs={{0,128},{64,192},{128,0},{192,64},{1,129},{65,193},{129,1},{193,65... | collective-permute-start | bytes 110600 | tf_op jit(solution)/shard_map/ppermute | solution.py:23
  72.5 2.8 %collective-permute-start.22 = (bf16[2,256,256]{2,1,0:T(8,128)(2,1)S(1)}, bf16[2,256,256]{2,1,0:T(8,128)(2,1)S(1)}, u32[]{:S(2)}, u32[]{:S(2)}) collective-permute-start(bf16[2,256,256]{2,1,0:T(8,128)(2,1)S(1)} %pad_maximum_fusion.2), channel_id=1, source_target_pairs={{0,4},{2,6},{4,0},{6,2},{8,12},{10,14},{12,8},{14,10},{1,5},{3,7},... | collective-permute-start | bytes 786440 | tf_op jit(solution)/shard_map/ppermute | solution.py:23
  76.0 6.5 %collective-permute-done.22 = bf16[2,256,256]{2,1,0:T(8,128)(2,1)S(1)} collective-permute-done((bf16[2,256,256]{2,1,0:T(8,128)(2,1)S(1)}, bf16[2,256,256]{2,1,0:T(8,128)(2,1)S(1)}, u32[]{:S(2)}, u32[]{:S(2)}) %collective-permute-start.22) | collective-permute-done | bytes 262176 | tf_op jit(solution)/shard_map/ppermute | solution.py:23
  82.6 3.0 %collective-permute-start.23 = (bf16[4,256,256]{2,1,0:T(8,128)(2,1)S(1)}, bf16[4,256,256]{2,1,0:T(8,128)(2,1)S(1)}, u32[]{:S(2)}, u32[]{:S(2)}) collective-permute-start(bf16[4,256,256]{2,1,0:T(8,128)(2,1)S(1)} %pad_maximum_fusion.1), channel_id=1, source_target_pairs={{0,2},{2,0},{4,6},{6,4},{8,10},{10,8},{12,14},{14,12},{1,3},{3,1},... | collective-permute-start | bytes 1572872 | tf_op jit(solution)/shard_map/ppermute | solution.py:23
  86.1 3.6 %collective-permute-start.15 = (bf16[144,128]{1,0:T(8,128)(2,1)S(1)}, bf16[144,128]{1,0:T(8,128)(2,1)S(1)}, u32[]{:S(2)}, u32[]{:S(2)}) collective-permute-start(bf16[144,128]{1,0:T(8,128)(2,1)S(1)} %pad_maximum_fusion.10), channel_id=1, source_target_pairs={{0,16},{16,0},{32,48},{48,32},{1,17},{17,1},{33,49},{49,33},{2,18}... | collective-permute-start | bytes 110600 | tf_op jit(solution)/shard_map/ppermute | solution.py:23
  92.2 4.0 %collective-permute-done.23 = bf16[4,256,256]{2,1,0:T(8,128)(2,1)S(1)} collective-permute-done((bf16[4,256,256]{2,1,0:T(8,128)(2,1)S(1)}, bf16[4,256,256]{2,1,0:T(8,128)(2,1)S(1)}, u32[]{:S(2)}, u32[]{:S(2)}) %collective-permute-start.23) | collective-permute-done | bytes 524320 | tf_op jit(solution)/shard_map/ppermute | solution.py:23
  105.8 3.5 %collective-permute-start.25 = (f32[16,256]{1,0:T(8,128)S(1)}, f32[16,256]{1,0:T(8,128)S(1)}, u32[]{:S(2)}, u32[]{:S(2)}) collective-permute-start(f32[16,256]{1,0:T(8,128)S(1)} %convolution_select_fusion), channel_id=1, source_target_pairs={{0,16},{16,0},{32,48},{48,32},{1,17},{17,1},{33,49},{49,33},{2,18}... | collective-permute-start | bytes 49160 | tf_op jit(solution)/shard_map/ppermute | solution.py:23
  111.2 2.1 %collective-permute-start.30 = (f32[16,256]{1,0:T(8,128)S(1)}, f32[16,256]{1,0:T(8,128)S(1)}, u32[]{:S(2)}, u32[]{:S(2)}) collective-permute-start(f32[16,256]{1,0:T(8,128)S(1)} %add_add_fusion.1), channel_id=1, source_target_pairs={{0,192},{64,128},{128,64},{192,0},{1,193},{65,129},{129,65},{193,1... | collective-permute-start | bytes 49160 | tf_op jit(solution)/shard_map/ppermute | solution.py:23
  116.2 2.3 %collective-permute-done.29 = f32[16,256]{1,0:T(8,128)S(1)} collective-permute-done((f32[16,256]{1,0:T(8,128)S(1)}, f32[16,256]{1,0:T(8,128)S(1)}, u32[]{:S(2)}, u32[]{:S(2)}) %collective-permute-start.29) | collective-permute-done | bytes 16416 | tf_op jit(solution)/shard_map/ppermute | solution.py:23
  (166 shorter events, 36.7 us)
Async XLA Ops:
  1.4 16.0 %all-to-all-start = ((s32[16,2,7]{2,1,0:T(2,128)}), s32[16,2,7]{2,1,0:T(2,128)S(1)}, u32[]{:S(2)}, u32[]{:S(2)}) async-start(s32[16,2,7]{2,1,0:T(2,128)} %broadcast_in_dim.163), calls=%async_computation | async-start | bytes 32768 | tf_op jit(solution)/shard_map/all_to_all | solution.py:15
  9.9 30.4 %collective-permute-start.21 = (bf16[1,256,256]{2,1,0:T(8,128)(2,1)}, bf16[1,256,256]{2,1,0:T(8,128)(2,1)S(1)}, u32[]{:S(2)}, u32[]{:S(2)}) collective-permute-start(bf16[1,256,256]{2,1,0:T(8,128)(2,1)} %bitcast.270), channel_id=1, source_target_pairs={{0,8},{2,10},{4,12},{6,14},{8,0},{10,2},{12,4},{14,6},{1,9},{3,11}... | collective-permute-start | bytes 393224 | tf_op jit(solution)/shard_map/ppermute | solution.py:23
  21.2 9.9 %collective-permute-start = (bf16[4,16,256]{2,1,0:T(8,128)(2,1)S(1)}, bf16[4,16,256]{2,1,0:T(8,128)(2,1)S(1)}, u32[]{:S(2)}, u32[]{:S(2)}) collective-permute-start(bf16[4,16,256]{2,1,0:T(8,128)(2,1)S(1)} %bitcast.282), channel_id=1, source_target_pairs={{0,48},{16,32},{32,16},{48,0},{1,49},{17,33},{33,17},{49,1},{2,50}... | collective-permute-start | bytes 98312 | tf_op jit(solution)/shard_map/ppermute | solution.py:23
  24.0 7.0 %collective-permute-start.2 = (bf16[4,16,256]{2,1,0:T(8,128)(2,1)S(1)}, bf16[4,16,256]{2,1,0:T(8,128)(2,1)S(1)}, u32[]{:S(2)}, u32[]{:S(2)}) collective-permute-start(bf16[4,16,256]{2,1,0:T(8,128)(2,1)S(1)} %bitcast.281), channel_id=1, source_target_pairs={{0,16},{16,0},{32,48},{48,32},{1,17},{17,1},{33,49},{49,33},{2,18}... | collective-permute-start | bytes 98312 | tf_op jit(solution)/shard_map/ppermute | solution.py:23
  24.3 6.8 %collective-permute-start.1 = (bf16[4,16,256]{2,1,0:T(8,128)(2,1)S(1)}, bf16[4,16,256]{2,1,0:T(8,128)(2,1)S(1)}, u32[]{:S(2)}, u32[]{:S(2)}) collective-permute-start(bf16[4,16,256]{2,1,0:T(8,128)(2,1)S(1)} %bitcast.280), channel_id=1, source_target_pairs={{0,32},{16,48},{32,0},{48,16},{1,33},{17,49},{33,1},{49,17},{2,34}... | collective-permute-start | bytes 98312 | tf_op jit(solution)/shard_map/ppermute | solution.py:23
  26.3 16.6 %all-to-all-start.1 = ((bf16[16,16,768]{2,1,0:T(8,128)(2,1)}), bf16[16,16,768]{2,1,0:T(8,128)(2,1)S(1)}, u32[]{:S(2)}, u32[]{:S(2)}) async-start(bf16[16,16,768]{2,1,0:T(8,128)(2,1)} %bitcast.1), calls=%async_computation.1 | async-start | bytes 786432 | tf_op jit(solution)/shard_map/all_to_all | solution.py:15
  31.2 6.2 %collective-permute-start.4 = (bf16[4,16,256]{2,1,0:T(8,128)(2,1)S(1)}, bf16[4,16,256]{2,1,0:T(8,128)(2,1)S(1)}, u32[]{:S(2)}, u32[]{:S(2)}) collective-permute-start(bf16[4,16,256]{2,1,0:T(8,128)(2,1)S(1)} %get-tuple-element.50), channel_id=1, source_target_pairs={{0,128},{64,192},{128,0},{192,64},{1,129},{65,193},{129,1},{193,65... | collective-permute-start | bytes 98312 | tf_op jit(solution)/shard_map/ppermute | solution.py:23
  43.3 5.3 %collective-permute-start.8 = (bf16[16,256]{1,0:T(8,128)(2,1)S(1)}, bf16[16,256]{1,0:T(8,128)(2,1)S(1)}, u32[]{:S(2)}, u32[]{:S(2)}) collective-permute-start(bf16[16,256]{1,0:T(8,128)(2,1)S(1)} %fusion.154), channel_id=1, source_target_pairs={{0,16},{16,0},{32,48},{48,32},{1,17},{17,1},{33,49},{49,33},{2,18}... | collective-permute-start | bytes 24584 | tf_op jit(solution)/shard_map/ppermute | solution.py:23
  43.6 5.7 %collective-permute-start.7 = (bf16[16,256]{1,0:T(8,128)(2,1)S(1)}, bf16[16,256]{1,0:T(8,128)(2,1)S(1)}, u32[]{:S(2)}, u32[]{:S(2)}) collective-permute-start(bf16[16,256]{1,0:T(8,128)(2,1)S(1)} %fusion.154), channel_id=1, source_target_pairs={{0,32},{16,48},{32,0},{48,16},{1,33},{17,49},{33,1},{49,17},{2,34}... | collective-permute-start | bytes 24584 | tf_op jit(solution)/shard_map/ppermute | solution.py:23
  54.2 5.5 %collective-permute-start.10 = (bf16[4,16,256]{2,1,0:T(8,128)(2,1)S(1)}, bf16[4,16,256]{2,1,0:T(8,128)(2,1)S(1)}, u32[]{:S(2)}, u32[]{:S(2)}) collective-permute-start(bf16[4,16,256]{2,1,0:T(8,128)(2,1)S(1)} %pad_maximum_fusion.11), channel_id=1, source_target_pairs={{0,128},{64,192},{128,0},{192,64},{1,129},{65,193},{129,1},{193,65... | collective-permute-start | bytes 98312 | tf_op jit(solution)/shard_map/ppermute | solution.py:23
  67.5 8.1 %collective-permute-start.12 = (bf16[144,128]{1,0:T(8,128)(2,1)S(1)}, bf16[144,128]{1,0:T(8,128)(2,1)S(1)}, u32[]{:S(2)}, u32[]{:S(2)}) collective-permute-start(bf16[144,128]{1,0:T(8,128)(2,1)S(1)} %pad_maximum_fusion.7), channel_id=1, source_target_pairs={{0,64},{64,0},{128,192},{192,128},{1,65},{65,1},{129,193},{193,129... | collective-permute-start | bytes 110600 | tf_op jit(solution)/shard_map/ppermute | solution.py:23
  67.8 7.8 %collective-permute-start.14 = (bf16[144,128]{1,0:T(8,128)(2,1)S(1)}, bf16[144,128]{1,0:T(8,128)(2,1)S(1)}, u32[]{:S(2)}, u32[]{:S(2)}) collective-permute-start(bf16[144,128]{1,0:T(8,128)(2,1)S(1)} %pad_maximum_fusion.9), channel_id=1, source_target_pairs={{0,192},{64,128},{128,64},{192,0},{1,193},{65,129},{129,65},{193,1... | collective-permute-start | bytes 110600 | tf_op jit(solution)/shard_map/ppermute | solution.py:23
  68.8 6.8 %collective-permute-start.13 = (bf16[144,128]{1,0:T(8,128)(2,1)S(1)}, bf16[144,128]{1,0:T(8,128)(2,1)S(1)}, u32[]{:S(2)}, u32[]{:S(2)}) collective-permute-start(bf16[144,128]{1,0:T(8,128)(2,1)S(1)} %pad_maximum_fusion.8), channel_id=1, source_target_pairs={{0,128},{64,192},{128,0},{192,64},{1,129},{65,193},{129,1},{193,65... | collective-permute-start | bytes 110600 | tf_op jit(solution)/shard_map/ppermute | solution.py:23
  72.5 10.0 %collective-permute-start.22 = (bf16[2,256,256]{2,1,0:T(8,128)(2,1)S(1)}, bf16[2,256,256]{2,1,0:T(8,128)(2,1)S(1)}, u32[]{:S(2)}, u32[]{:S(2)}) collective-permute-start(bf16[2,256,256]{2,1,0:T(8,128)(2,1)S(1)} %pad_maximum_fusion.2), channel_id=1, source_target_pairs={{0,4},{2,6},{4,0},{6,2},{8,12},{10,14},{12,8},{14,10},{1,5},{3,7},... | collective-permute-start | bytes 786440 | tf_op jit(solution)/shard_map/ppermute | solution.py:23
  82.6 13.6 %collective-permute-start.23 = (bf16[4,256,256]{2,1,0:T(8,128)(2,1)S(1)}, bf16[4,256,256]{2,1,0:T(8,128)(2,1)S(1)}, u32[]{:S(2)}, u32[]{:S(2)}) collective-permute-start(bf16[4,256,256]{2,1,0:T(8,128)(2,1)S(1)} %pad_maximum_fusion.1), channel_id=1, source_target_pairs={{0,2},{2,0},{4,6},{6,4},{8,10},{10,8},{12,14},{14,12},{1,3},{3,1},... | collective-permute-start | bytes 1572872 | tf_op jit(solution)/shard_map/ppermute | solution.py:23
  85.6 5.2 %collective-permute-start.17 = (bf16[144,128]{1,0:T(8,128)(2,1)S(1)}, bf16[144,128]{1,0:T(8,128)(2,1)S(1)}, u32[]{:S(2)}, u32[]{:S(2)}) collective-permute-start(bf16[144,128]{1,0:T(8,128)(2,1)S(1)} %pad_maximum_fusion.10), channel_id=1, source_target_pairs={{0,48},{16,32},{32,16},{48,0},{1,49},{17,33},{33,17},{49,1},{2,50}... | collective-permute-start | bytes 110600 | tf_op jit(solution)/shard_map/ppermute | solution.py:23
  86.1 5.5 %collective-permute-start.16 = (bf16[144,128]{1,0:T(8,128)(2,1)S(1)}, bf16[144,128]{1,0:T(8,128)(2,1)S(1)}, u32[]{:S(2)}, u32[]{:S(2)}) collective-permute-start(bf16[144,128]{1,0:T(8,128)(2,1)S(1)} %pad_maximum_fusion.10), channel_id=1, source_target_pairs={{0,32},{16,48},{32,0},{48,16},{1,33},{17,49},{33,1},{49,17},{2,34}... | collective-permute-start | bytes 110600 | tf_op jit(solution)/shard_map/ppermute | solution.py:23
  86.1 5.9 %collective-permute-start.15 = (bf16[144,128]{1,0:T(8,128)(2,1)S(1)}, bf16[144,128]{1,0:T(8,128)(2,1)S(1)}, u32[]{:S(2)}, u32[]{:S(2)}) collective-permute-start(bf16[144,128]{1,0:T(8,128)(2,1)S(1)} %pad_maximum_fusion.10), channel_id=1, source_target_pairs={{0,16},{16,0},{32,48},{48,32},{1,17},{17,1},{33,49},{49,33},{2,18}... | collective-permute-start | bytes 110600 | tf_op jit(solution)/shard_map/ppermute | solution.py:23
  96.3 8.3 %collective-permute-start.24 = (bf16[8,256,256]{2,1,0:T(8,128)(2,1)S(1)}, bf16[8,256,256]{2,1,0:T(8,128)(2,1)S(1)}, u32[]{:S(2)}, u32[]{:S(2)}) collective-permute-start(bf16[8,256,256]{2,1,0:T(8,128)(2,1)S(1)} %pad_maximum_fusion), channel_id=1, source_target_pairs={{0,1},{1,0},{2,3},{3,2},{4,5},{5,4},{6,7},{7,6},{8,9},{9,8},{10,11... | collective-permute-start | bytes 3145736 | tf_op jit(solution)/shard_map/ppermute | solution.py:23
  96.4 5.2 %collective-permute-start.20 = (bf16[4,16,256]{2,1,0:T(8,128)(2,1)S(1)}, bf16[4,16,256]{2,1,0:T(8,128)(2,1)S(1)}, u32[]{:S(2)}, u32[]{:S(2)}) collective-permute-start(bf16[4,16,256]{2,1,0:T(8,128)(2,1)S(1)} %bitcast.273), channel_id=1, source_target_pairs={{0,192},{64,128},{128,64},{192,0},{1,193},{65,129},{129,65},{193,1... | collective-permute-start | bytes 98312 | tf_op jit(solution)/shard_map/ppermute | solution.py:23
  97.7 5.4 %collective-permute-start.19 = (bf16[4,16,256]{2,1,0:T(8,128)(2,1)S(1)}, bf16[4,16,256]{2,1,0:T(8,128)(2,1)S(1)}, u32[]{:S(2)}, u32[]{:S(2)}) collective-permute-start(bf16[4,16,256]{2,1,0:T(8,128)(2,1)S(1)} %bitcast.274), channel_id=1, source_target_pairs={{0,128},{64,192},{128,0},{192,64},{1,129},{65,193},{129,1},{193,65... | collective-permute-start | bytes 98312 | tf_op jit(solution)/shard_map/ppermute | solution.py:23
  105.7 5.2 %collective-permute-start.26 = (f32[16,256]{1,0:T(8,128)S(1)}, f32[16,256]{1,0:T(8,128)S(1)}, u32[]{:S(2)}, u32[]{:S(2)}) collective-permute-start(f32[16,256]{1,0:T(8,128)S(1)} %convolution_select_fusion), channel_id=1, source_target_pairs={{0,32},{16,48},{32,0},{48,16},{1,33},{17,49},{33,1},{49,17},{2,34}... | collective-permute-start | bytes 49160 | tf_op jit(solution)/shard_map/ppermute | solution.py:23
  105.8 5.4 %collective-permute-start.25 = (f32[16,256]{1,0:T(8,128)S(1)}, f32[16,256]{1,0:T(8,128)S(1)}, u32[]{:S(2)}, u32[]{:S(2)}) collective-permute-start(f32[16,256]{1,0:T(8,128)S(1)} %convolution_select_fusion), channel_id=1, source_target_pairs={{0,16},{16,0},{32,48},{48,32},{1,17},{17,1},{33,49},{49,33},{2,18}... | collective-permute-start | bytes 49160 | tf_op jit(solution)/shard_map/ppermute | solution.py:23
  113.2 5.2 %collective-permute-start.29 = (f32[16,256]{1,0:T(8,128)S(1)}, f32[16,256]{1,0:T(8,128)S(1)}, u32[]{:S(2)}, u32[]{:S(2)}) collective-permute-start(f32[16,256]{1,0:T(8,128)S(1)} %add_add_fusion.1), channel_id=1, source_target_pairs={{0,128},{64,192},{128,0},{192,64},{1,129},{65,193},{129,1},{193,65... | collective-permute-start | bytes 49160 | tf_op jit(solution)/shard_map/ppermute | solution.py:23
  (14 other events, 190.0 us)

commit v4 on v1

v4 whole, which is shorter than its diff:
```python
import functools

import jax
import jax.numpy as jnp
from jax import lax
from jax.experimental import pallas as pl
from jax.experimental.pallas import tpu as pltpu
from jax.sharding import Mesh
from jax.sharding import PartitionSpec as P


HEAD_DIM = 128
SEQ = ("seq_0", "seq_1")
GRP = ("z", "core")
NEG = -1e30


def exchange(pieces, axis):
    return lax.all_to_all(pieces, axis, split_axis=0, concat_axis=0, tiled=True)


def from_partner(x, axis, k):
    return lax.ppermute(x, axis, [(i, i ^ k) for i in range(lax.axis_size(axis))])


def fenced(*arrays):
    return lax.optimization_barrier(arrays)


def halves(x):
    both = lax.reduce_precision(x, 8, 15)
    high = lax.reduce_precision(both, 8, 7)
    return high.astype(jnp.bfloat16), (both - high).astype(jnp.bfloat16), both


def in_vmem():
    return pl.BlockSpec(memory_space=pltpu.VMEM)


def in_smem():
    return pl.BlockSpec(memory_space=pltpu.SMEM)


def call(kernel, out, specs, *args):
    outs = (in_vmem(),) * len(out) if isinstance(out, tuple) else in_vmem()
    small = pltpu.CompilerParams(vmem_limit_bytes=8 * 2**20)
    return pl.pallas_call(
        kernel, out_shape=out, in_specs=specs, out_specs=outs, compiler_params=small
    )(*args)


def merge_kernel(query, key, value, stats, packed, out):
    seqs, _, head_dim = packed.shape
    rows, cols = query.shape
    lh = cols // head_dim
    steps = 8
    n = rows * lh
    scale = head_dim ** (-0.5)
    causal = lax.broadcasted_iota(jnp.int32, (steps, steps), 1) <= lax.broadcasted_iota(
        jnp.int32, (steps, steps), 0
    )
    tops, totals, accs = [], [], []
    for r in range(rows // steps):
        for h in range(lh):
            at = (slice(r * steps, (r + 1) * steps), slice(h * head_dim, (h + 1) * head_dim))
            q, k, v = (ref[at].astype(jnp.bfloat16) for ref in (query, key, value))
            scores = lax.dot_general(
                q, k, (((1,), (1,)), ((), ())), preferred_element_type=jnp.float32
            )
            scores = jnp.where(causal, scores * scale, NEG)
            top = jnp.max(scores, axis=-1, keepdims=True)
            e = jnp.where(causal, jnp.exp(scores - top), 0.0)
            tops.append(top)
            totals.append(jnp.sum(e, axis=-1, keepdims=True))
            accs.append(jnp.dot(e.astype(jnp.bfloat16), v, preferred_element_type=jnp.float32))
    w_top, w_total, w_acc = (jnp.concatenate(x, axis=0) for x in (tops, totals, accs))
    part = stats[...].astype(jnp.float32)
    part = jnp.concatenate([part, jnp.zeros((4 * n - seqs, 4 * n), jnp.float32)], axis=0).T
    there = lax.broadcasted_iota(jnp.int32, (n, 4 * n), 1) < seqs
    top = jnp.where(there, part[:n] + part[n : 2 * n], NEG)
    total = part[2 * n : 3 * n] + part[3 * n :]
    best = jnp.maximum(jnp.max(top, axis=-1, keepdims=True), w_top)
    factor = jnp.where(there, jnp.exp(top - best), 0.0)
    w_factor = jnp.exp(w_top - best)
    denom = jnp.sum(total * factor, axis=-1, keepdims=True) + w_total * w_factor
    numer = w_acc * w_factor
    for d in range(seqs):
        numer += packed[d, :n, :].astype(jnp.float32) * factor[:, d : d + 1]
    attended = numer / denom
    lines = []
    for r in range(rows // steps):
        own = [attended[(r * lh + h) * steps : (r * lh + h + 1) * steps] for h in range(lh)]
        lines.append(jnp.concatenate(own, axis=1))
    attended = jnp.concatenate(lines, axis=0).astype(jnp.bfloat16)
    for d in range(seqs):
        out[d] = attended


def output_kernel(places, blocks, mine, other, inputs, gain, head, out):
    count = mine.shape[0]
    seqs, rows, _ = blocks.shape
    residual = inputs[...]
    for m in range(count):
        residual += jnp.dot(blocks[places[m]], mine[m], preferred_element_type=jnp.float32)
        residual += jnp.dot(blocks[places[count + m]], other[m], preferred_element_type=jnp.float32)
    gained = (residual * gain[...]).astype(jnp.bfloat16)
    logits = lax.dot_general(
        gained, head[...], (((1,), (1,)), ((), ())), preferred_element_type=jnp.float32
    )
    row = lax.broadcasted_iota(jnp.int32, logits.shape, 0)
    lane = lax.broadcasted_iota(jnp.int32, logits.shape, 1)
    squares = jnp.sum(residual * residual, axis=-1, keepdims=True)
    squares = jnp.sum(jnp.where(row == lane, squares, 0.0), axis=0, keepdims=True)
    result = jnp.where(row == rows - 1, squares, logits)
    for d in range(seqs):
        out[d] = result


def final_kernel(shard, parts, out, *, width, steps):
    seqs, rows, _ = parts.shape
    robots, true_steps, own_bins = out.shape
    total = parts[0]
    for d in range(1, seqs):
        total += parts[d]
    row = lax.broadcasted_iota(jnp.int32, total.shape, 0)
    lane = lax.broadcasted_iota(jnp.int32, total.shape, 1)
    squares = jnp.sum(
        jnp.where(row == lane, total[rows - 1 :], 0.0), axis=-1, keepdims=True
    )
    logits = total * lax.rsqrt(squares / width + 1e-05)
    top = jnp.max(logits, axis=-1, keepdims=True)
    logprob = logits - top - jnp.log(jnp.sum(jnp.exp(logits - top), axis=-1, keepdims=True))
    own = logprob[:, :own_bins]
    for k in range(1, seqs):
        own = jnp.where(shard[0] == k, logprob[:, k * own_bins : (k + 1) * own_bins], own)
    for r in range(robots):
        out[r] = own[r * steps : r * steps + true_steps]


def heads_kernel(sums, cosine, sine, head, spread, query, key, value):
    seqs = sums.shape[0]
    cols = query.shape[1]
    rows = query.shape[0]
    total = sums[0].astype(jnp.float32)
    for d in range(1, seqs):
        total += sums[d].astype(jnp.float32)

    def rotated(x):
        parts = []
        for h in range(cols // HEAD_DIM):
            part = x[:, h * HEAD_DIM : (h + 1) * HEAD_DIM]
            turned = pltpu.roll(part, HEAD_DIM // 2, 1)
            parts.append(part * cosine[...] + turned * sine[...])
        return jnp.concatenate(parts, axis=1)

    own = rotated(total[:, :cols])
    query[...] = own
    key[...] = rotated(total[:, cols : 2 * cols])
    value[...] = total[:, 2 * cols :]
    own = own.astype(jnp.bfloat16)
    for d in range(head.shape[0]):
        spread[d, :rows, :] = own
        spread[d, rows:, :] = head[d]


def on_device(
    actions,
    lengths,
    embed,
    attn_gain,
    w_query,
    w_key,
    w_value,
    w_out,
    key_cache,
    value_cache,
    final_gain,
    head,
):
    s = lax.axis_index(SEQ)
    g = lax.axis_index(GRP)
    z = lax.axis_index("z")
    core = lax.axis_index("core")
    seqs = lax.axis_size(SEQ)
    groups = lax.axis_size(GRP)
    robots, true_steps = actions.shape
    steps = 8
    rows = robots * steps
    prompt_dev, width = key_cache.shape[1:]
    feats, cols = w_query.shape
    bins = embed.shape[0]
    own_bins = head.shape[0]
    lh = cols // HEAD_DIM
    heads = seqs * lh
    n = robots * lh * steps
    scale = HEAD_DIM ** (-0.5)
    bin_ids = jnp.arange(bins, dtype=jnp.int32)
    f32 = jnp.float32
    array = jax.ShapeDtypeStruct

    blocks = w_out[None]
    arrived = from_partner(blocks, "z", 4)
    zs = [0, 4]
    zs = zs + [m ^ 2 for m in zs]
    zs = zs + [m ^ 1 for m in zs]

    acts = jnp.broadcast_to(actions[None], (groups, robots, true_steps))
    acts = exchange(acts, GRP).reshape(groups * robots, true_steps)
    pad_steps = ((0, 0), (0, steps - true_steps))
    acts = jnp.pad(acts, pad_steps).reshape(groups * rows)
    wide = embed.astype(f32)
    mean_square = jnp.mean(wide * wide, axis=-1, keepdims=True)
    part = lax.dynamic_slice(embed, (0, g * feats), (bins, feats)).astype(f32)
    part_gain = lax.dynamic_slice(attn_gain, (g * feats,), (feats,))
    table = (part * lax.rsqrt(mean_square + 1e-05) * part_gain).astype(jnp.bfloat16)
    onehot = (acts[:, None] == bin_ids[None, :]).astype(jnp.bfloat16)
    normed = jnp.dot(onehot, table, preferred_element_type=f32).astype(jnp.bfloat16)
    weights = jnp.concatenate([w_query, w_key, w_value], axis=1)
    terms = jnp.dot(normed, weights, preferred_element_type=f32).astype(jnp.bfloat16)
    terms, lengths, actions, final_gain, head, shard = fenced(
        terms, lengths, actions, final_gain, head, s[None]
    )
    sums = exchange(terms.reshape(groups, rows, 3 * cols), GRP)

    places = (lengths[:, None] + jnp.arange(steps, dtype=jnp.int32)[None, :]).astype(f32)
    half = HEAD_DIM // 2
    freq = 10000.0 ** (-(jnp.arange(half, dtype=f32) * 2.0 / HEAD_DIM))
    angle = places.reshape(rows, 1) * freq
    cosine = jnp.concatenate([jnp.cos(angle)] * 2, axis=1)
    sine = jnp.concatenate([-jnp.sin(angle), jnp.sin(angle)], axis=1)
    prompt_ids = shard[0] * prompt_dev + jnp.arange(prompt_dev, dtype=jnp.int32)
    mask = (prompt_ids[None, :] < lengths[:, None]).astype(f32)
    actions = jnp.pad(actions, pad_steps)
    own_hot = (actions.reshape(rows)[:, None] == bin_ids[None, :]).astype(jnp.bfloat16)
    own_embed = lax.dynamic_slice(embed, (0, s * cols), (bins, cols))
    inputs = jnp.dot(own_hot, own_embed, preferred_element_type=f32)
    own_gain = lax.dynamic_slice(final_gain, (s * cols,), (cols,))[None]
    head_parts = jnp.swapaxes(head.reshape(own_bins, seqs, cols), 0, 1)
    order = (z ^ jnp.array(zs, jnp.int32)) * lax.axis_size("core")
    order = jnp.concatenate([order + core, order + 1 - core])
    blocks = jnp.concatenate([blocks, arrived], axis=0)
    (sums, cosine, sine, mask, inputs, own_gain, head_parts, order, shard, blocks) = fenced(
        sums, cosine, sine, mask, inputs, own_gain, head_parts, order, shard, blocks
    )
    arrived = from_partner(blocks, "z", 2)

    spread, query, key, value = call(
        heads_kernel,
        (array((seqs, rows + own_bins, cols), jnp.bfloat16), *[array((rows, cols), f32)] * 3),
        [in_vmem()] * 4,
        sums,
        cosine,
        sine,
        head_parts,
    )
    spread = exchange(spread, SEQ)
    spread, mask = fenced(spread, mask)
    all_query = spread[:, :rows].reshape(seqs, robots, steps, lh, HEAD_DIM)
    head_cols = spread[:, rows:].reshape(bins, cols)

    mask = (mask > 0.0)[:, None, None, :]
    q = jnp.moveaxis(all_query, 0, 2).reshape(robots, steps, heads, HEAD_DIM)
    cache_keys = key_cache.reshape(robots, prompt_dev, heads, HEAD_DIM)
    cache_values = value_cache.reshape(robots, prompt_dev, heads, HEAD_DIM)
    scores = jnp.einsum("rthd,rphd->rhtp", q, cache_keys, preferred_element_type=f32)
    scores = jnp.where(mask, scores * scale, NEG)
    top = halves(jnp.max(scores, axis=-1))[2]
    e = jnp.where(mask, jnp.exp(scores - top[..., None]), 0.0)
    total = jnp.sum(e, axis=-1)
    acc = jnp.einsum(
        "rhtp,rphd->rhtd", e.astype(jnp.bfloat16), cache_values, preferred_element_type=f32
    )

    def to_owner(x):
        x = x.reshape(robots, seqs, lh, steps, -1)
        return jnp.moveaxis(x, 1, 0).reshape(seqs, n, -1)

    th, tl, _ = halves(to_owner(top)[..., 0])
    lo, ll, _ = halves(to_owner(total)[..., 0])
    stats = jnp.concatenate([th, tl, lo, ll], axis=1)[:, None]
    packed = jnp.concatenate([to_owner(acc.astype(jnp.bfloat16)), stats], axis=1)
    packed, blocks, arrived, head_cols = fenced(packed, blocks, arrived, head_cols)
    blocks = jnp.concatenate([blocks, arrived], axis=0)
    arrived = from_partner(blocks, "z", 1)
    packed = exchange(packed, SEQ)
    attended = call(
        merge_kernel,
        array((seqs, rows, cols), jnp.bfloat16),
        [in_vmem()] * 5,
        query,
        key,
        value,
        packed[:, n],
        packed,
    )
    attended, blocks, arrived = fenced(attended, blocks, arrived)
    blocks = jnp.concatenate([blocks, arrived], axis=0)
    other = from_partner(blocks, "core", 1)

    attended = exchange(attended, SEQ)
    parts = call(
        output_kernel,
        array((seqs, rows, bins), f32),
        [in_smem()] + [in_vmem()] * 6,
        order,
        attended,
        blocks,
        other,
        inputs,
        own_gain,
        head_cols,
    )
    parts = exchange(parts, SEQ)
    return call(
        functools.partial(final_kernel, width=width, steps=steps),
        array((robots, true_steps, own_bins), f32),
        [in_smem(), in_vmem()],
        shard,
        parts,
    )


def solution(mesh):
    torus = Mesh(mesh.devices.reshape(4, 4, 8, 2), ("seq_0", "seq_1", "z", "core"))
    in_specs = (
        P(GRP, None),
        P(GRP),
        P(),
        P(),
        P(GRP, SEQ),
        P(GRP, SEQ),
        P(GRP, SEQ),
        P(GRP, SEQ),
        P(GRP, SEQ, None),
        P(GRP, SEQ, None),
        P(),
        P(SEQ, None),
    )
    out_specs = P(GRP, None, SEQ)

    return jax.shard_map(
        on_device, mesh=torus, in_specs=in_specs, out_specs=out_specs, check_vma=False
    )
```

time: 118 us -> 106 us (0.90)
  blocking collectives: 0 us -> 34.9 us
  waiting for transfers between devices: 49.5 us -> 16.2 us
  starting transfers between devices: 41.7 us -> 30.5 us
  local copies, waits for them, and re-layouts: 10.7 us -> 4.9 us
  Pallas kernels: 0 us -> 4.25 us
  other arithmetic: 6.84 us -> 4.31 us
  matrix products: 8.16 us -> 9.8 us
    all_to_all x0 -> x3, blocking collectives: none -> 34.9 us  [exchange(): return lax.all_to_all(pieces, axis, split_axis=0, concat_axis=0, tiled=True)]
    ppermute x4, waiting for transfers between devices: 16.7 us -> 0.01 us  [from_partner(): lax.ppermute(x, axis, [(i, i ^ k) for i in range(lax.axis_size(axis))])]
    all_to_all x6 -> x3, waiting for transfers between devices: 32.9 us -> 16.2 us  [exchange(): return lax.all_to_all(pieces, axis, split_axis=0, concat_axis=0, tiled=True)]
    all_to_all x6 -> x3, starting transfers between devices: 31 us -> 20.4 us  [exchange(): return lax.all_to_all(pieces, axis, split_axis=0, concat_axis=0, tiled=True)]
    pallas_call x0 -> x4, Pallas kernels: none -> 4.25 us  [call(): pl.pallas_call(kernel, out_shape=out, in_specs=specs, out_specs=outs, com...]
    dot_general x1, matrix products: 0.74 us -> 2.92 us  [on_device(): jnp.einsum('rhtp,rphd->rhtd', e.astype(jnp.bfloat16), cache_values, prefe...]
    reshape x7 -> x1, local copies, waits for them, and re-layouts: 1.61 us -> 0.01 us  [on_device(): head_parts = jnp.swapaxes(head.reshape(own_bins, seqs, cols), 0, 1)]
    concatenate x3 -> x2, local copies, waits for them, and re-layouts: 1.61 us -> 0.06 us  [on_device(): blocks = jnp.concatenate([blocks, arrived], axis=0)]
  transfers between devices with their start and end apart: 10 -> 7, of which waited for: 5 -> 2; matrix products, arithmetic and copies ran while one was open for 18% -> 16% of each run, Pallas kernels for 0% -> 1%
where the time goes in v4:
time: 106 us; the launch traced here: 105 us
  blocking collectives  34.9 us (33%)
  starting transfers between devices  30.5 us (29%)
  waiting for transfers between devices  16.2 us (15%)
  matrix products  9.8 us (9%)
  local copies, waits for them, and re-layouts  4.9 us (5%)
  other arithmetic  4.31 us (4%)
  Pallas kernels  4.25 us (4%)
    all_to_all x3, blocking collectives, exchange(): return lax.all_to_all(pieces, axis, split_axis=0, concat_axis=0, tiled=True)  34.9 us
    all_to_all x3, starting transfers between devices, exchange(): return lax.all_to_all(pieces, axis, split_axis=0, concat_axis=0, tiled=True)  20.4 us
    all_to_all x3, waiting for transfers between devices, exchange(): return lax.all_to_all(pieces, axis, split_axis=0, concat_axis=0, tiled=True)  16.2 us
    ppermute x4, starting transfers between devices, from_partner(): lax.ppermute(x, axis, [(i, i ^ k) for i in range(lax.axis_size(axis))])  10.1 us
    pallas_call x4, Pallas kernels, call(): pl.pallas_call(kernel, out_shape=out, in_specs=specs, out_specs=outs, com...  4.25 us
    dot_general x1, matrix products, on_device(): jnp.einsum('rthd,rphd->rhtp', q, cache_keys, preferred_element_type=f32)  3.45 us
    dot_general x1, matrix products, on_device(): jnp.einsum('rhtp,rphd->rhtd', e.astype(jnp.bfloat16), cache_values, prefe...  2.92 us
    dot_general x1, matrix products, on_device(): jnp.dot(normed, weights, preferred_element_type=f32).astype(jnp.bfloat16)  2.34 us
  transfers between devices with their start and end apart: 7, of which 2 were waited for; matrix products, arithmetic and copies ran while one was open for 16% of the time, Pallas kernels for 1%

profile of v4, /device:TPU:32, one launch (start us, length us, event | category | flops | bytes accessed | tf_op | source)
XLA Modules:
  0.0 105.1 jit_solution(2195416047558638281)
XLA Ops:
  0.0 1.3 %broadcast_in_dim.47 = s32[16,2,7]{2,1,0:T(2,128)} broadcast(s32[2,7]{1,0:T(2,128)} %param.13), dimensions={1,2} | broadcast | bytes 952 | tf_op jit(solution)/shard_map/broadcast_in_dim | solution.py:207
  1.4 8.6 %all-to-all-start = ((s32[16,2,7]{2,1,0:T(2,128)}), s32[16,2,7]{2,1,0:T(2,128)S(1)}, u32[]{:S(2)}, u32[]{:S(2)}) async-start(s32[16,2,7]{2,1,0:T(2,128)} %broadcast_in_dim.47), calls=%async_computation | async-start | bytes 32768 | tf_op jit(solution)/shard_map/all_to_all | solution.py:19
  9.9 4.5 %collective-permute-start = (bf16[1,256,256]{2,1,0:T(8,128)(2,1)}, bf16[1,256,256]{2,1,0:T(8,128)(2,1)S(1)}, u32[]{:S(2)}, u32[]{:S(2)}) collective-permute-start(bf16[1,256,256]{2,1,0:T(8,128)(2,1)} %bitcast.69), channel_id=1, source_target_pairs={{0,8},{2,10},{4,12},{6,14},{8,0},{10,2},{12,4},{14,6},{1,9},{3,11}... | collective-permute-start | bytes 393224 | tf_op jit(solution)/shard_map/ppermute | solution.py:23
  14.4 2.1 %multiply_reduce_fusion = f32[256]{0:T(256)S(1)} fusion(bf16[256,4096]{1,0:T(8,128)(2,1)} %param.15), kind=kLoop, calls=%fused_computation.6 | loop fusion | flops 3145472 | bytes 2098176 | tf_op jit(solution)/shard_map/reduce_sum | solution.py:212
  17.3 0.8 dynamic_slice.13
  18.1 2.3 %convolution_convert_fusion = bf16[256,768]{1,0:T(8,128)(2,1)} fusion(bf16[256,256]{1,0:T(8,128)(2,1)} %param.19, bf16[256,256]{1,0:T(8,128)(2,1)} %param.18, bf16[256,256]{1,0:T(8,128)(2,1)} %param.17, f32[256]{0:T(256)S(1)} %dynamic_slice.13, f32[256]{0:T(256)S(1)} %add_rsqrt_fusion, bf16[256,4096]{1,0:T(8,128)(2,1)} %param.15, s32[]{:T(128)S(6)} %select_n.15, ...), kind=kOutput, calls=%fused_computation.7 | convolution fusion | flops 135987200 | bytes 920580 | tf_op jit(solution)/shard_map/dot_general | solution.py:219
  21.2 0.7 add_convert_fusion
  22.0 4.8 %all-to-all-start.1 = ((bf16[16,16,768]{2,1,0:T(8,128)(2,1)}), bf16[16,16,768]{2,1,0:T(8,128)(2,1)S(1)}, u32[]{:S(2)}, u32[]{:S(2)}) async-start(bf16[16,16,768]{2,1,0:T(8,128)(2,1)} %bitcast.2), calls=%async_computation.1 | async-start | bytes 786432 | tf_op jit(solution)/shard_map/all_to_all | solution.py:19
  26.9 1.1 %fusion.26.inputs = f32[16,256]{1,0:T(8,128)S(1)} fusion(bf16[256,4096]{1,0:T(8,128)(2,1)} %param.15, s32[]{:T(128)S(6)} %select_n.16, s32[16]{0:T(128)S(1)} %eq.34), kind=kOutput, calls=%fused_computation.29 | convolution fusion | flops 2101248 | bytes 147524 | tf_op jit(solution)/shard_map/dot_general | solution.py:236
  28.2 0.8 dynamic_slice.15
  29.0 9.6 %all-to-all-done.1.sums = bf16[16,16,768]{2,1,0:T(8,128)(2,1)S(1)} async-done(((bf16[16,16,768]{2,1,0:T(8,128)(2,1)}), bf16[16,16,768]{2,1,0:T(8,128)(2,1)S(1)}, u32[]{:S(2)}, u32[]{:S(2)}) %all-to-all-start.1) | async-done | bytes 393248 | tf_op jit(solution)/shard_map/all_to_all | solution.py:19
  38.7 0.8 shard_map.127
  39.5 7.0 %all-to-all-start.2 = ((bf16[16,32,256]{2,1,0:T(8,128)(2,1)}), bf16[16,32,256]{2,1,0:T(8,128)(2,1)S(1)}, u32[]{:S(2)}, u32[]{:S(2)}) async-start(bf16[16,32,256]{2,1,0:T(8,128)(2,1)} %get-tuple-element.49), calls=%async_computation.2 | async-start | bytes 524288 | tf_op jit(solution)/shard_map/all_to_all | solution.py:19
  46.5 2.8 %collective-permute-start.1 = (bf16[2,256,256]{2,1,0:T(8,128)(2,1)S(1)}, bf16[2,256,256]{2,1,0:T(8,128)(2,1)S(1)}, u32[]{:S(2)}, u32[]{:S(2)}) collective-permute-start(bf16[2,256,256]{2,1,0:T(8,128)(2,1)S(1)} %pad_maximum_fusion), channel_id=1, source_target_pairs={{0,4},{2,6},{4,0},{6,2},{8,12},{10,14},{12,8},{14,10},{1,5},{3,7},... | collective-permute-start | bytes 786440 | tf_op jit(solution)/shard_map/ppermute | solution.py:23
  49.3 6.6 %all-to-all-done.2 = bf16[16,32,256]{2,1,0:T(8,128)(2,1)S(1)} async-done(((bf16[16,32,256]{2,1,0:T(8,128)(2,1)}), bf16[16,32,256]{2,1,0:T(8,128)(2,1)S(1)}, u32[]{:S(2)}, u32[]{:S(2)}) %all-to-all-start.2) | async-done | bytes 262176 | tf_op jit(solution)/shard_map/all_to_all | solution.py:19
  55.9 3.4 %fusion.47 = (f32[2,32,8]{2,1,0:T(8,128)S(1)}, f32[2,32,8,256]{3,2,1,0:T(8,128)S(1)}) fusion(bf16[2,8,32,128]{3,1,2,0:T(8,128)(2,1)S(1)} %bitcast.64, pred[2,256]{1,0:T(4,128)(4,1)S(1)} %broadcast_compare_fusion, bf16[2,256,4096]{2,1,0:T(8,128)(2,1)} %param.21), kind=kOutput, calls=%fused_computation.70 | convolution fusion | flops 33947136 | bytes 4852224 | tf_op jit(solution)/shard_map/rthd,rphd->rhtp/dot_general | solution.py:265
  59.9 2.9 %fusion.12 = bf16[2,32,8,128]{3,2,1,0:T(8,128)(2,1)S(1)} fusion(f32[2,32,8,256]{3,2,1,0:T(8,128)S(1)} %get-tuple-element.77, f32[2,32,8]{2,1,0:T(8,128)S(1)} %get-tuple-element.66, pred[2,256]{1,0:T(4,128)(4,1)S(1)} %broadcast_compare_fusion, bf16[2,256,4096]{2,1,0:T(8,128)(2,1)} %param.22), kind=kOutput, calls=%fused_computation.10 | convolution fusion | flops 34013184 | bytes 4852224 | tf_op jit(solution)/shard_map/rhtp,rphd->rhtd/dot_general | solution.py:270
  63.2 2.7 %collective-permute-start.2 = (bf16[4,256,256]{2,1,0:T(8,128)(2,1)S(1)}, bf16[4,256,256]{2,1,0:T(8,128)(2,1)S(1)}, u32[]{:S(2)}, u32[]{:S(2)}) collective-permute-start(bf16[4,256,256]{2,1,0:T(8,128)(2,1)S(1)} %constant_dynamic-update-slice_fusion), channel_id=1, source_target_pairs={{0,2},{2,0},{4,6},{6,4},{8,10},{10,8},{12,14},{14,12},{1,3},{3,1},... | collective-permute-start | bytes 1572872 | tf_op jit(solution)/shard_map/ppermute | solution.py:23
  65.9 12.1 %all_to_all.30.packed = bf16[16,33,128]{2,1,0:T(8,128)(2,1)S(1)} all-to-all(bf16[16,33,128]{2,1,0:T(8,128)(2,1)S(1)} %pad_maximum_fusion.1), channel_id=1, replica_groups=mesh['seq_0'=4,'seq_1'=4,'z'=8,'core'=2] {'seq_0','seq_1'}, dimensions={0} | all-to-all | bytes 270336 | tf_op jit(solution)/shard_map/all_to_all | solution.py:19
  78.0 1.0 shard_map.128
  79.2 11.0 %all_to_all.31.blocks = bf16[16,16,256]{2,1,0:T(8,128)(2,1)S(1)} all-to-all(bf16[16,16,256]{2,1,0:T(8,128)(2,1)S(1)} %shard_map.128), channel_id=1, replica_groups=mesh['seq_0'=4,'seq_1'=4,'z'=8,'core'=2] {'seq_0','seq_1'}, dimensions={0} | all-to-all | bytes 262144 | tf_op jit(solution)/shard_map/all_to_all | solution.py:19
  90.2 1.1 %shard_map.129 = f32[16,16,256]{2,1,0:T(8,128)S(1)} custom-call(s32[16]{0:T(128)S(1)} %pad_add_fusion.places, bf16[16,16,256]{2,1,0:T(8,128)(2,1)S(1)} %all_to_all.31.blocks, bf16[8,256,256]{2,1,0:T(8,128)(2,1)S(1)} %constant_dynamic-update-slice_fusion.2.mine, bf16[8,256,256]{2,1,0:T(8,128)(2,1)S(1)} %collective-permute-done.3.other, ...), custom_call_target="tpu_custom_call" | custom-call | tf_op jit(solution)/shard_map/pallas_call | solution.py:47
  91.3 11.8 %all_to_all.32.parts = f32[16,16,256]{2,1,0:T(8,128)S(1)} all-to-all(f32[16,16,256]{2,1,0:T(8,128)S(1)} %shard_map.129), channel_id=1, replica_groups=mesh['seq_0'=4,'seq_1'=4,'z'=8,'core'=2] {'seq_0','seq_1'}, dimensions={0} | all-to-all | bytes 524288 | tf_op jit(solution)/shard_map/all_to_all | solution.py:19
  103.1 1.4 %shard_map.130 = f32[2,7,16]{2,1,0:T(8,128)S(1)} custom-call(s32[1]{0:T(128)} %bitcast.1.shard, f32[16,16,256]{2,1,0:T(8,128)S(1)} %all_to_all.32.parts), custom_call_target="tpu_custom_call" | custom-call | tf_op jit(solution)/shard_map/pallas_call | solution.py:47
  (50 shorter events, 3.6 us)
Async XLA Ops:
  0.0 29.0 %copy-start.1 = (bf16[256,256]{1,0:T(8,128)(2,1)S(1)}, bf16[256,256]{1,0:T(8,128)(2,1)}, u32[]{:S(2)}) copy-start(bf16[256,256]{1,0:T(8,128)(2,1)} %param.20) | copy-start | bytes 393220
  0.0 28.9 %copy-start = (bf16[16,4096]{1,0:T(8,128)(2,1)S(1)}, bf16[16,4096]{1,0:T(8,128)(2,1)}, u32[]{:S(2)}) copy-start(bf16[16,4096]{1,0:T(8,128)(2,1)} %param.24) | copy-start | bytes 393220
  0.0 28.1 %copy-start.2 = (s32[2]{0:T(128)S(1)}, s32[2]{0:T(128)}, u32[]{:S(2)}) copy-start(s32[2]{0:T(128)} %param.14) | copy-start | bytes 28
  1.4 16.7 %all-to-all-start = ((s32[16,2,7]{2,1,0:T(2,128)}), s32[16,2,7]{2,1,0:T(2,128)S(1)}, u32[]{:S(2)}, u32[]{:S(2)}) async-start(s32[16,2,7]{2,1,0:T(2,128)} %broadcast_in_dim.47), calls=%async_computation | async-start | bytes 32768 | tf_op jit(solution)/shard_map/all_to_all | solution.py:19
  9.9 19.1 %collective-permute-start = (bf16[1,256,256]{2,1,0:T(8,128)(2,1)}, bf16[1,256,256]{2,1,0:T(8,128)(2,1)S(1)}, u32[]{:S(2)}, u32[]{:S(2)}) collective-permute-start(bf16[1,256,256]{2,1,0:T(8,128)(2,1)} %bitcast.69), channel_id=1, source_target_pairs={{0,8},{2,10},{4,12},{6,14},{8,0},{10,2},{12,4},{14,6},{1,9},{3,11}... | collective-permute-start | bytes 393224 | tf_op jit(solution)/shard_map/ppermute | solution.py:23
  22.0 16.6 %all-to-all-start.1 = ((bf16[16,16,768]{2,1,0:T(8,128)(2,1)}), bf16[16,16,768]{2,1,0:T(8,128)(2,1)S(1)}, u32[]{:S(2)}, u32[]{:S(2)}) async-start(bf16[16,16,768]{2,1,0:T(8,128)(2,1)} %bitcast.2), calls=%async_computation.1 | async-start | bytes 786432 | tf_op jit(solution)/shard_map/all_to_all | solution.py:19
  39.5 16.4 %all-to-all-start.2 = ((bf16[16,32,256]{2,1,0:T(8,128)(2,1)}), bf16[16,32,256]{2,1,0:T(8,128)(2,1)S(1)}, u32[]{:S(2)}, u32[]{:S(2)}) async-start(bf16[16,32,256]{2,1,0:T(8,128)(2,1)} %get-tuple-element.49), calls=%async_computation.2 | async-start | bytes 524288 | tf_op jit(solution)/shard_map/all_to_all | solution.py:19
  46.5 16.6 %collective-permute-start.1 = (bf16[2,256,256]{2,1,0:T(8,128)(2,1)S(1)}, bf16[2,256,256]{2,1,0:T(8,128)(2,1)S(1)}, u32[]{:S(2)}, u32[]{:S(2)}) collective-permute-start(bf16[2,256,256]{2,1,0:T(8,128)(2,1)S(1)} %pad_maximum_fusion), channel_id=1, source_target_pairs={{0,4},{2,6},{4,0},{6,2},{8,12},{10,14},{12,8},{14,10},{1,5},{3,7},... | collective-permute-start | bytes 786440 | tf_op jit(solution)/shard_map/ppermute | solution.py:23
  63.2 15.9 %collective-permute-start.2 = (bf16[4,256,256]{2,1,0:T(8,128)(2,1)S(1)}, bf16[4,256,256]{2,1,0:T(8,128)(2,1)S(1)}, u32[]{:S(2)}, u32[]{:S(2)}) collective-permute-start(bf16[4,256,256]{2,1,0:T(8,128)(2,1)S(1)} %constant_dynamic-update-slice_fusion), channel_id=1, source_target_pairs={{0,2},{2,0},{4,6},{6,4},{8,10},{10,8},{12,14},{14,12},{1,3},{3,1},... | collective-permute-start | bytes 1572872 | tf_op jit(solution)/shard_map/ppermute | solution.py:23
  79.1 11.1 %collective-permute-start.3 = (bf16[8,256,256]{2,1,0:T(8,128)(2,1)S(1)}, bf16[8,256,256]{2,1,0:T(8,128)(2,1)S(1)}, u32[]{:S(2)}, u32[]{:S(2)}) collective-permute-start(bf16[8,256,256]{2,1,0:T(8,128)(2,1)S(1)} %constant_dynamic-update-slice_fusion.2.mine), channel_id=1, source_target_pairs={{0,1},{1,0},{2,3},{3,2},{4,5},{5,4},{6,7},{7,6},{8,9},{9,8},{10,11... | collective-permute-start | bytes 3145736 | tf_op jit(solution)/shard_map/ppermute | solution.py:23

commit v5 on v4

--- a/solution.py
+++ b/solution.py
@@ -23,16 +23,14 @@
     return lax.ppermute(x, axis, [(i, i ^ k) for i in range(lax.axis_size(axis))])
 
 
+def here(x):
+    return lax.ppermute(x, "core", [(i, i) for i in range(lax.axis_size("core"))])
+
+
 def fenced(*arrays):
     return lax.optimization_barrier(arrays)
 
 
-def halves(x):
-    both = lax.reduce_precision(x, 8, 15)
-    high = lax.reduce_precision(both, 8, 7)
-    return high.astype(jnp.bfloat16), (both - high).astype(jnp.bfloat16), both
-
-
 def in_vmem():
     return pl.BlockSpec(memory_space=pltpu.VMEM)
 
@@ -41,11 +39,19 @@
     return pl.BlockSpec(memory_space=pltpu.SMEM)
 
 
-def call(kernel, out, specs, *args):
+def far():
+    return pl.BlockSpec(memory_space=pltpu.HBM)
+
+
+def call(kernel, out, specs, *args, scratch=(), limit=8):
     outs = (in_vmem(),) * len(out) if isinstance(out, tuple) else in_vmem()
-    small = pltpu.CompilerParams(vmem_limit_bytes=8 * 2**20)
     return pl.pallas_call(
-        kernel, out_shape=out, in_specs=specs, out_specs=outs, compiler_params=small
+        kernel,
+        out_shape=out,
+        in_specs=specs,
+        out_specs=outs,
+        scratch_shapes=scratch,
+        compiler_params=pltpu.CompilerParams(vmem_limit_bytes=limit * 2**20),
     )(*args)
 
 
@@ -117,8 +123,8 @@
 
 
 def final_kernel(shard, parts, out, *, width, steps):
-    seqs, rows, _ = parts.shape
-    robots, true_steps, own_bins = out.shape
+    seqs, rows, bins = parts.shape
+    true_steps, robots, own_bins = out.shape
     total = parts[0]
     for d in range(1, seqs):
         total += parts[d]
@@ -130,11 +136,102 @@
     logits = total * lax.rsqrt(squares / width + 1e-05)
     top = jnp.max(logits, axis=-1, keepdims=True)
     logprob = logits - top - jnp.log(jnp.sum(jnp.exp(logits - top), axis=-1, keepdims=True))
-    own = logprob[:, :own_bins]
-    for k in range(1, seqs):
-        own = jnp.where(shard[0] == k, logprob[:, k * own_bins : (k + 1) * own_bins], own)
+    own = pltpu.roll(logprob, (bins - shard[0] * own_bins) % bins, 1)[:, :own_bins]
     for r in range(robots):
-        out[r] = own[r * steps : r * steps + true_steps]
+        out[:, r, :] = own[r * steps : r * steps + true_steps]
+
+
+def parts_of(x):
+    high = x.astype(jnp.bfloat16).astype(jnp.float32)
+    low = (x - high).astype(jnp.bfloat16).astype(jnp.float32)
+    return high, low
+
+
+def project_kernel(group, shard, acts, own, embed, gain, w_query, w_key, w_value, terms, inputs):
+    bins, width = embed.shape
+    feats, cols = w_query.shape
+    chunk = 512
+    squares = jnp.zeros((bins, HEAD_DIM), jnp.float32)
+    for c in range(0, width, chunk):
+        wide = embed[:, c : c + chunk].astype(jnp.float32)
+        wide = wide * wide
+        for k in range(0, chunk, HEAD_DIM):
+            squares += wide[:, k : k + HEAD_DIM]
+    mean_square = jnp.sum(squares, axis=-1, keepdims=True) / width
+    here = pl.ds(pl.multiple_of(group[0] * feats, feats), feats)
+    part = embed[:, here].astype(jnp.float32)
+    lines = feats // HEAD_DIM
+    row = jnp.concatenate([gain[pl.ds(group[0] * lines + k, 1)] for k in range(lines)], axis=1)
+    table = (part * lax.rsqrt(mean_square + 1e-05) * row).astype(jnp.bfloat16)
+    by_bin = lax.broadcasted_iota(jnp.int32, (bins, acts.shape[1]), 0)
+
+    def rows_of(numbers, values):
+        hot = jnp.where(by_bin[:, : numbers.shape[1]] == numbers, 1.0, 0.0).astype(jnp.bfloat16)
+        return lax.dot_general(
+            hot, values, (((0,), (0,)), ((), ())), preferred_element_type=jnp.float32
+        )
+
+    normed = rows_of(acts[...], table).astype(jnp.bfloat16)
+    for k, w in enumerate((w_query, w_key, w_value)):
+        out = jnp.dot(normed, w[...], preferred_element_type=jnp.float32)
+        terms[:, k * cols : (k + 1) * cols] = out.astype(jnp.bfloat16)
+    there = pl.ds(pl.multiple_of(shard[0] * cols, cols), cols)
+    inputs[...] = rows_of(own[...], embed[:, there])[: inputs.shape[0]]
+
+
+def attend_kernel(shard, lengths, spread, keys_far, values_far, packed, keys, values, sems):
+    seqs, _, cols = spread.shape
+    robots, prompt_dev, _ = keys.shape
+    steps = 8
+    n = packed.shape[1] - 8
+    scale = HEAD_DIM ** (-0.5)
+    group = 2
+    copies = []
+    for k in range(seqs // group):
+        at = slice(k * group * cols, (k + 1) * group * cols)
+        copies.append(
+            [
+                pltpu.make_async_copy(src.at[:, :, at], dst.at[:, :, at], sems.at[i, k])
+                for i, (src, dst) in enumerate(((keys_far, keys), (values_far, values)))
+            ]
+        )
+        for copy in copies[-1]:
+            copy.start()
+    first = lax.broadcasted_iota(jnp.int32, (steps, cols), 1) < HEAD_DIM
+    place = lax.broadcasted_iota(jnp.int32, (2 * steps, prompt_dev), 1) + shard[0] * prompt_dev
+    block = lax.broadcasted_iota(jnp.int32, (4 * n, HEAD_DIM), 1)
+    stats = jnp.zeros((4 * n, HEAD_DIM), jnp.float32)
+    for b in range(seqs):
+        if b % group == 0:
+            for copy in copies[b // group]:
+                copy.wait()
+        query = spread[b, : robots * steps, :].astype(jnp.float32)
+        at = slice(b * cols, (b + 1) * cols)
+        columns = []
+        for r in range(robots):
+            valid = place < lengths[r]
+            q = query[r * steps : (r + 1) * steps]
+            q = jnp.concatenate([jnp.where(first, q, 0.0), jnp.where(first, 0.0, q)], axis=0)
+            scores = lax.dot_general(
+                q.astype(jnp.bfloat16),
+                keys[r, :, at],
+                (((1,), (1,)), ((), ())),
+                preferred_element_type=jnp.float32,
+            )
+            scores = jnp.where(valid, scores * scale, NEG)
+            high, low = parts_of(jnp.max(scores, axis=-1, keepdims=True))
+            e = jnp.where(valid, jnp.exp(scores - (high + low)), 0.0)
+            columns.append((high, low, *parts_of(jnp.sum(e, axis=-1, keepdims=True))))
+            acc = jnp.dot(
+                e.astype(jnp.bfloat16), values[r, :, at], preferred_element_type=jnp.float32
+            )
+            acc = jnp.concatenate([acc[:steps, :HEAD_DIM], acc[steps:, HEAD_DIM:]], axis=0)
+            packed[b, r * 2 * steps : (r + 1) * 2 * steps, :] = acc.astype(jnp.bfloat16)
+        column = jnp.concatenate([columns[r][k] for k in range(4) for r in range(robots)], axis=0)
+        stats = jnp.where(block == b, column, stats)
+    stats = stats.T.astype(jnp.bfloat16)
+    for b in range(seqs):
+        packed[b, n:, :] = jnp.broadcast_to(stats[b : b + 1], (8, HEAD_DIM))
 
 
 def heads_kernel(sums, cosine, sine, head, spread, query, key, value):
@@ -186,17 +283,16 @@
     robots, true_steps = actions.shape
     steps = 8
     rows = robots * steps
-    prompt_dev, width = key_cache.shape[1:]
-    feats, cols = w_query.shape
+    _, width = key_cache.shape[1:]
+    _, cols = w_query.shape
     bins = embed.shape[0]
     own_bins = head.shape[0]
     lh = cols // HEAD_DIM
-    heads = seqs * lh
     n = robots * lh * steps
-    scale = HEAD_DIM ** (-0.5)
-    bin_ids = jnp.arange(bins, dtype=jnp.int32)
     f32 = jnp.float32
     array = jax.ShapeDtypeStruct
+
+    near = [here(x) for x in (embed, attn_gain.reshape(-1, HEAD_DIM), w_query, w_key, w_value)]
 
     blocks = w_out[None]
     arrived = from_partner(blocks, "z", 4)
@@ -207,19 +303,19 @@
     acts = jnp.broadcast_to(actions[None], (groups, robots, true_steps))
     acts = exchange(acts, GRP).reshape(groups * robots, true_steps)
     pad_steps = ((0, 0), (0, steps - true_steps))
-    acts = jnp.pad(acts, pad_steps).reshape(groups * rows)
-    wide = embed.astype(f32)
-    mean_square = jnp.mean(wide * wide, axis=-1, keepdims=True)
-    part = lax.dynamic_slice(embed, (0, g * feats), (bins, feats)).astype(f32)
-    part_gain = lax.dynamic_slice(attn_gain, (g * feats,), (feats,))
-    table = (part * lax.rsqrt(mean_square + 1e-05) * part_gain).astype(jnp.bfloat16)
-    onehot = (acts[:, None] == bin_ids[None, :]).astype(jnp.bfloat16)
-    normed = jnp.dot(onehot, table, preferred_element_type=f32).astype(jnp.bfloat16)
-    weights = jnp.concatenate([w_query, w_key, w_value], axis=1)
-    terms = jnp.dot(normed, weights, preferred_element_type=f32).astype(jnp.bfloat16)
-    terms, lengths, actions, final_gain, head, shard = fenced(
-        terms, lengths, actions, final_gain, head, s[None]
-    )
+    acts = jnp.pad(acts, pad_steps).reshape(1, groups * rows)
+    own = jnp.pad(jnp.pad(actions, pad_steps).reshape(1, rows), ((0, 0), (0, HEAD_DIM - rows)))
+    terms, inputs = call(
+        project_kernel,
+        (array((groups * rows, 3 * cols), jnp.bfloat16), array((rows, cols), f32)),
+        [in_smem()] * 2 + [in_vmem()] * 7,
+        g[None],
+        s[None],
+        acts,
+        own,
+        *near,
+    )
+    terms, lengths, final_gain, head, shard = fenced(terms, lengths, final_gain, head, s[None])
     sums = exchange(terms.reshape(groups, rows, 3 * cols), GRP)
 
     places = (lengths[:, None] + jnp.arange(steps, dtype=jnp.int32)[None, :]).astype(f32)
@@ -228,19 +324,13 @@
     angle = places.reshape(rows, 1) * freq
     cosine = jnp.concatenate([jnp.cos(angle)] * 2, axis=1)
     sine = jnp.concatenate([-jnp.sin(angle), jnp.sin(angle)], axis=1)
-    prompt_ids = shard[0] * prompt_dev + jnp.arange(prompt_dev, dtype=jnp.int32)
-    mask = (prompt_ids[None, :] < lengths[:, None]).astype(f32)
-    actions = jnp.pad(actions, pad_steps)
-    own_hot = (actions.reshape(rows)[:, None] == bin_ids[None, :]).astype(jnp.bfloat16)
-    own_embed = lax.dynamic_slice(embed, (0, s * cols), (bins, cols))
-    inputs = jnp.dot(own_hot, own_embed, preferred_element_type=f32)
     own_gain = lax.dynamic_slice(final_gain, (s * cols,), (cols,))[None]
     head_parts = jnp.swapaxes(head.reshape(own_bins, seqs, cols), 0, 1)
     order = (z ^ jnp.array(zs, jnp.int32)) * lax.axis_size("core")
     order = jnp.concatenate([order + core, order + 1 - core])
     blocks = jnp.concatenate([blocks, arrived], axis=0)
-    (sums, cosine, sine, mask, inputs, own_gain, head_parts, order, shard, blocks) = fenced(
-        sums, cosine, sine, mask, inputs, own_gain, head_parts, order, shard, blocks
+    (sums, cosine, sine, inputs, own_gain, head_parts, order, shard, blocks) = fenced(
+        sums, cosine, sine, inputs, own_gain, head_parts, order, shard, blocks
     )
     arrived = from_partner(blocks, "z", 2)
 
@@ -254,31 +344,24 @@
         head_parts,
     )
     spread = exchange(spread, SEQ)
-    spread, mask = fenced(spread, mask)
-    all_query = spread[:, :rows].reshape(seqs, robots, steps, lh, HEAD_DIM)
     head_cols = spread[:, rows:].reshape(bins, cols)
 
-    mask = (mask > 0.0)[:, None, None, :]
-    q = jnp.moveaxis(all_query, 0, 2).reshape(robots, steps, heads, HEAD_DIM)
-    cache_keys = key_cache.reshape(robots, prompt_dev, heads, HEAD_DIM)
-    cache_values = value_cache.reshape(robots, prompt_dev, heads, HEAD_DIM)
-    scores = jnp.einsum("rthd,rphd->rhtp", q, cache_keys, preferred_element_type=f32)
-    scores = jnp.where(mask, scores * scale, NEG)
-    top = halves(jnp.max(scores, axis=-1))[2]
-    e = jnp.where(mask, jnp.exp(scores - top[..., None]), 0.0)
-    total = jnp.sum(e, axis=-1)
-    acc = jnp.einsum(
-        "rhtp,rphd->rhtd", e.astype(jnp.bfloat16), cache_values, preferred_element_type=f32
-    )
-
-    def to_owner(x):
-        x = x.reshape(robots, seqs, lh, steps, -1)
-        return jnp.moveaxis(x, 1, 0).reshape(seqs, n, -1)
-
-    th, tl, _ = halves(to_owner(top)[..., 0])
-    lo, ll, _ = halves(to_owner(total)[..., 0])
-    stats = jnp.concatenate([th, tl, lo, ll], axis=1)[:, None]
-    packed = jnp.concatenate([to_owner(acc.astype(jnp.bfloat16)), stats], axis=1)
+    packed = call(
+        attend_kernel,
+        array((seqs, n + 8, HEAD_DIM), jnp.bfloat16),
+        [in_smem()] * 2 + [in_vmem()] + [far()] * 2,
+        shard,
+        lengths,
+        spread,
+        key_cache,
+        value_cache,
+        scratch=[
+            pltpu.VMEM(key_cache.shape, jnp.bfloat16),
+            pltpu.VMEM(value_cache.shape, jnp.bfloat16),
+            pltpu.SemaphoreType.DMA((2, seqs // 2)),
+        ],
+        limit=52,
+    )
     packed, blocks, arrived, head_cols = fenced(packed, blocks, arrived, head_cols)
     blocks = jnp.concatenate([blocks, arrived], axis=0)
     arrived = from_partner(blocks, "z", 1)
@@ -311,13 +394,14 @@
         head_cols,
     )
     parts = exchange(parts, SEQ)
-    return call(
+    logprob = call(
         functools.partial(final_kernel, width=width, steps=steps),
-        array((robots, true_steps, own_bins), f32),
+        array((true_steps, robots, own_bins), f32),
         [in_smem(), in_vmem()],
         shard,
         parts,
     )
+    return jnp.swapaxes(logprob, 0, 1)
 
 
 def solution(mesh):

time: 106 us -> 109 us (1.028)
  blocking collectives: 34.9 us -> 49.4 us
  Pallas kernels: 4.25 us -> 16.9 us
  matrix products: 9.8 us -> 0 us
  waiting for transfers between devices: 16.2 us -> 8.12 us
  starting transfers between devices: 30.5 us -> 26.6 us
  other arithmetic: 4.31 us -> 2.6 us
    all_to_all x3 -> x4, blocking collectives: 34.9 us -> 49.4 us  [exchange(): return lax.all_to_all(pieces, axis, split_axis=0, concat_axis=0, tiled=True)]
    pallas_call x4 -> x6, Pallas kernels: 4.25 us -> 16.9 us  [call(): pl.pallas_call(kernel, out_shape=out, in_specs=specs, out_specs=outs, scr...]
    dot_general x4 -> x0, matrix products: 9.8 us -> none  [the longest x1 3.45 us: on_device(): jnp.einsum('rthd,rphd->rhtp', q, cache_keys, preferred_element_type=f32)]
    all_to_all x3 -> x2, waiting for transfers between devices: 16.2 us -> 7.61 us  [exchange(): return lax.all_to_all(pieces, axis, split_axis=0, concat_axis=0, tiled=True)]
    all_to_all x3 -> x2, starting transfers between devices: 20.4 us -> 13.4 us  [exchange(): return lax.all_to_all(pieces, axis, split_axis=0, concat_axis=0, tiled=True)]
    ppermute x0 -> x5, starting transfers between devices: none -> 5.04 us  [here(): lax.ppermute(x, 'core', [(i, i) for i in range(lax.axis_size('core'))])]
    reduce_sum x2 -> x0, other arithmetic: 2.34 us -> none  [the longest x1 2.09 us: on_device(): mean_square = jnp.mean(wide * wide, axis=-1, keepdims=True)]
    ppermute x4, starting transfers between devices: 10.1 us -> 8.14 us  [from_partner(): lax.ppermute(x, axis, [(i, i ^ k) for i in range(lax.axis_size(axis))])]
  transfers between devices with their start and end apart: 7 -> 11, of which waited for: 2 -> 2; matrix products, arithmetic and copies ran while one was open for 16% -> 6% of each run, Pallas kernels for 1% -> 14%
where the time goes in v5:
time: 109 us; the launch traced here: 108 us
  blocking collectives  49.4 us (45%)
  starting transfers between devices  26.6 us (24%)
  Pallas kernels  16.9 us (16%)
  waiting for transfers between devices  8.12 us (7%)
  local copies, waits for them, and re-layouts  4.05 us (4%)
  other arithmetic  2.6 us (2%)
    all_to_all x4, blocking collectives, exchange(): return lax.all_to_all(pieces, axis, split_axis=0, concat_axis=0, tiled=True)  49.4 us
    pallas_call x6, Pallas kernels, call(): pl.pallas_call(kernel, out_shape=out, in_specs=specs, out_specs=outs, scr...  16.9 us
    all_to_all x2, starting transfers between devices, exchange(): return lax.all_to_all(pieces, axis, split_axis=0, concat_axis=0, tiled=True)  13.4 us
    ppermute x4, starting transfers between devices, from_partner(): lax.ppermute(x, axis, [(i, i ^ k) for i in range(lax.axis_size(axis))])  8.14 us
    all_to_all x2, waiting for transfers between devices, exchange(): return lax.all_to_all(pieces, axis, split_axis=0, concat_axis=0, tiled=True)  7.61 us
    ppermute x5, starting transfers between devices, here(): lax.ppermute(x, 'core', [(i, i) for i in range(lax.axis_size('core'))])  5.04 us
  transfers between devices with their start and end apart: 11, of which 2 were waited for; matrix products, arithmetic and copies ran while one was open for 6% of the time, Pallas kernels for 14%

profile of v5, /device:TPU:32, one launch (start us, length us, event | category | flops | bytes accessed | tf_op | source)
XLA Modules:
  0.0 107.7 jit_solution(6116150412400993382)
XLA Ops:
  0.0 1.6 %collective-permute-start = (bf16[256,4096]{1,0:T(8,128)(2,1)}, bf16[256,4096]{1,0:T(8,128)(2,1)S(1)}, u32[]{:S(2)}, u32[]{:S(2)}) collective-permute-start(bf16[256,4096]{1,0:T(8,128)(2,1)} %param.15), channel_id=1, source_target_pairs={{0,0},{1,1},{2,2},{3,3},{4,4},{5,5},{6,6},{7,7},{8,8},{9,9},{10,10... | collective-permute-start | bytes 6291464 | tf_op jit(solution)/shard_map/ppermute | solution.py:27
  1.6 0.9 collective-permute-start.2
  2.5 0.9 collective-permute-start.3
  3.4 0.9 collective-permute-start.4
  4.3 1.3 %broadcast_in_dim.24 = s32[16,2,7]{2,1,0:T(2,128)} broadcast(s32[2,7]{1,0:T(2,128)} %param.13), dimensions={1,2} | broadcast | bytes 952 | tf_op jit(solution)/shard_map/broadcast_in_dim | solution.py:303
  5.6 8.6 %all-to-all-start = ((s32[16,2,7]{2,1,0:T(2,128)}), s32[16,2,7]{2,1,0:T(2,128)S(1)}, u32[]{:S(2)}, u32[]{:S(2)}) async-start(s32[16,2,7]{2,1,0:T(2,128)} %broadcast_in_dim.24), calls=%async_computation | async-start | bytes 32768 | tf_op jit(solution)/shard_map/all_to_all | solution.py:19
  15.6 4.5 %collective-permute-start.5 = (bf16[1,256,256]{2,1,0:T(8,128)(2,1)}, bf16[1,256,256]{2,1,0:T(8,128)(2,1)S(1)}, u32[]{:S(2)}, u32[]{:S(2)}) collective-permute-start(bf16[1,256,256]{2,1,0:T(8,128)(2,1)} %bitcast.24), channel_id=1, source_target_pairs={{0,8},{2,10},{4,12},{6,14},{8,0},{10,2},{12,4},{14,6},{1,9},{3,11}... | collective-permute-start | bytes 393224 | tf_op jit(solution)/shard_map/ppermute | solution.py:23
  21.0 1.7 %shard_map.127 = (bf16[256,768]{1,0:T(8,128)(2,1)}, f32[16,256]{1,0:T(8,128)S(1)}) custom-call(s32[1]{0:T(128)} %bitcast.group, s32[1]{0:T(128)} %bitcast.1.shard, s32[1,256]{1,0:T(1,128)S(1)} %reshape.47.acts, s32[1,128]{1,0:T(1,128)S(1)} %pad.14.own, bf16[256,4096]{1,0:T(8,128)(2,1)S(1)} %collective-permute-done.embed, ...), custom_call_target="tpu_custom_call" | custom-call | tf_op jit(solution)/shard_map/pallas_call | solution.py:48
  22.6 4.8 %all-to-all-start.1 = ((bf16[16,16,768]{2,1,0:T(8,128)(2,1)}), bf16[16,16,768]{2,1,0:T(8,128)(2,1)S(1)}, u32[]{:S(2)}, u32[]{:S(2)}) async-start(bf16[16,16,768]{2,1,0:T(8,128)(2,1)} %bitcast.4), calls=%async_computation.1 | async-start | bytes 786432 | tf_op jit(solution)/shard_map/all_to_all | solution.py:19
  28.0 0.9 pad_maximum_fusion
  29.0 0.7 add_convert_fusion
  29.8 0.9 copy.19
  30.7 0.8 dynamic_slice.3
  31.7 7.6 %all-to-all-done.1.sums = bf16[16,16,768]{2,1,0:T(8,128)(2,1)S(1)} async-done(((bf16[16,16,768]{2,1,0:T(8,128)(2,1)}), bf16[16,16,768]{2,1,0:T(8,128)(2,1)S(1)}, u32[]{:S(2)}, u32[]{:S(2)}) %all-to-all-start.1) | async-done | bytes 393248 | tf_op jit(solution)/shard_map/all_to_all | solution.py:19
  39.3 2.8 %collective-permute-start.6 = (bf16[2,256,256]{2,1,0:T(8,128)(2,1)S(1)}, bf16[2,256,256]{2,1,0:T(8,128)(2,1)S(1)}, u32[]{:S(2)}, u32[]{:S(2)}) collective-permute-start(bf16[2,256,256]{2,1,0:T(8,128)(2,1)S(1)} %pad_maximum_fusion), channel_id=1, source_target_pairs={{0,4},{2,6},{4,0},{6,2},{8,12},{10,14},{12,8},{14,10},{1,5},{3,7},... | collective-permute-start | bytes 786440 | tf_op jit(solution)/shard_map/ppermute | solution.py:23
  42.1 15.5 %all_to_all.30.spread = bf16[16,32,256]{2,1,0:T(8,128)(2,1)S(1)} all-to-all(bf16[16,32,256]{2,1,0:T(8,128)(2,1)S(1)} %get-tuple-element.48), channel_id=1, replica_groups=mesh['seq_0'=4,'seq_1'=4,'z'=8,'core'=2] {'seq_0','seq_1'}, dimensions={0} | all-to-all | bytes 524288 | tf_op jit(solution)/shard_map/all_to_all | solution.py:19
  57.7 12.1 %shard_map.129 = bf16[16,40,128]{2,1,0:T(8,128)(2,1)S(1)} custom-call(s32[1]{0:T(128)} %bitcast.1.shard, s32[2]{0:T(128)S(1)} %copy-done, bf16[16,32,256]{2,1,0:T(8,128)(2,1)S(1)} %all_to_all.30.spread, bf16[2,256,4096]{2,1,0:T(8,128)(2,1)} %keys_far.1, bf16[2,256,4096]{2,1,0:T(8,128)(2,1)} %values_far.1), custom_call_target="tpu_custom_call" | custom-call | tf_op jit(solution)/shard_map/pallas_call | solution.py:48
  69.8 0.8 collective-permute-start.7
  70.6 11.1 %all_to_all.31.packed = bf16[16,40,128]{2,1,0:T(8,128)(2,1)S(1)} all-to-all(bf16[16,40,128]{2,1,0:T(8,128)(2,1)S(1)} %shard_map.129), channel_id=1, replica_groups=mesh['seq_0'=4,'seq_1'=4,'z'=8,'core'=2] {'seq_0','seq_1'}, dimensions={0} | all-to-all | bytes 327680 | tf_op jit(solution)/shard_map/all_to_all | solution.py:19
  81.7 1.0 shard_map.130
  82.9 11.0 %all_to_all.32.blocks = bf16[16,16,256]{2,1,0:T(8,128)(2,1)S(1)} all-to-all(bf16[16,16,256]{2,1,0:T(8,128)(2,1)S(1)} %shard_map.130), channel_id=1, replica_groups=mesh['seq_0'=4,'seq_1'=4,'z'=8,'core'=2] {'seq_0','seq_1'}, dimensions={0} | all-to-all | bytes 262144 | tf_op jit(solution)/shard_map/all_to_all | solution.py:19
  93.9 1.1 %shard_map.131 = f32[16,16,256]{2,1,0:T(8,128)S(1)} custom-call(s32[16]{0:T(128)S(1)} %pad_add_fusion.places, bf16[16,16,256]{2,1,0:T(8,128)(2,1)S(1)} %all_to_all.32.blocks, bf16[8,256,256]{2,1,0:T(8,128)(2,1)S(1)} %constant_dynamic-update-slice_fusion.2.mine, bf16[8,256,256]{2,1,0:T(8,128)(2,1)S(1)} %collective-permute-done.8.other, ...), custom_call_target="tpu_custom_call" | custom-call | tf_op jit(solution)/shard_map/pallas_call | solution.py:48
  95.0 11.8 %all_to_all.33.parts = f32[16,16,256]{2,1,0:T(8,128)S(1)} all-to-all(f32[16,16,256]{2,1,0:T(8,128)S(1)} %shard_map.131), channel_id=1, replica_groups=mesh['seq_0'=4,'seq_1'=4,'z'=8,'core'=2] {'seq_0','seq_1'}, dimensions={0} | all-to-all | bytes 524288 | tf_op jit(solution)/shard_map/all_to_all | solution.py:19
  106.8 0.9 shard_map.132
  (33 shorter events, 3.5 us)
Async XLA Ops:
  0.0 57.7 %copy-start = (s32[2]{0:T(128)S(1)}, s32[2]{0:T(128)}, u32[]{:S(2)}) copy-start(s32[2]{0:T(128)} %lengths) | copy-start | bytes 28
  0.0 21.0 %collective-permute-start = (bf16[256,4096]{1,0:T(8,128)(2,1)}, bf16[256,4096]{1,0:T(8,128)(2,1)S(1)}, u32[]{:S(2)}, u32[]{:S(2)}) collective-permute-start(bf16[256,4096]{1,0:T(8,128)(2,1)} %param.15), channel_id=1, source_target_pairs={{0,0},{1,1},{2,2},{3,3},{4,4},{5,5},{6,6},{7,7},{8,8},{9,9},{10,10... | collective-permute-start | bytes 6291464 | tf_op jit(solution)/shard_map/ppermute | solution.py:27
  1.6 19.3 %collective-permute-start.2 = (bf16[256,256]{1,0:T(8,128)(2,1)}, bf16[256,256]{1,0:T(8,128)(2,1)S(1)}, u32[]{:S(2)}, u32[]{:S(2)}) collective-permute-start(bf16[256,256]{1,0:T(8,128)(2,1)} %param.17), channel_id=1, source_target_pairs={{0,0},{1,1},{2,2},{3,3},{4,4},{5,5},{6,6},{7,7},{8,8},{9,9},{10,10... | collective-permute-start | bytes 393224 | tf_op jit(solution)/shard_map/ppermute | solution.py:27
  2.5 18.4 %collective-permute-start.3 = (bf16[256,256]{1,0:T(8,128)(2,1)}, bf16[256,256]{1,0:T(8,128)(2,1)S(1)}, u32[]{:S(2)}, u32[]{:S(2)}) collective-permute-start(bf16[256,256]{1,0:T(8,128)(2,1)} %param.18), channel_id=1, source_target_pairs={{0,0},{1,1},{2,2},{3,3},{4,4},{5,5},{6,6},{7,7},{8,8},{9,9},{10,10... | collective-permute-start | bytes 393224 | tf_op jit(solution)/shard_map/ppermute | solution.py:27
  3.4 17.5 %collective-permute-start.4 = (bf16[256,256]{1,0:T(8,128)(2,1)}, bf16[256,256]{1,0:T(8,128)(2,1)S(1)}, u32[]{:S(2)}, u32[]{:S(2)}) collective-permute-start(bf16[256,256]{1,0:T(8,128)(2,1)} %param.19), channel_id=1, source_target_pairs={{0,0},{1,1},{2,2},{3,3},{4,4},{5,5},{6,6},{7,7},{8,8},{9,9},{10,10... | collective-permute-start | bytes 393224 | tf_op jit(solution)/shard_map/ppermute | solution.py:27
  5.6 15.2 %all-to-all-start = ((s32[16,2,7]{2,1,0:T(2,128)}), s32[16,2,7]{2,1,0:T(2,128)S(1)}, u32[]{:S(2)}, u32[]{:S(2)}) async-start(s32[16,2,7]{2,1,0:T(2,128)} %broadcast_in_dim.24), calls=%async_computation | async-start | bytes 32768 | tf_op jit(solution)/shard_map/all_to_all | solution.py:19
  14.2 1.4 %collective-permute-start.1 = (f32[32,128]{1,0:T(8,128)}, f32[32,128]{1,0:T(8,128)S(1)}, u32[]{:S(2)}, u32[]{:S(2)}) collective-permute-start(f32[32,128]{1,0:T(8,128)} %bitcast.27), channel_id=1, source_target_pairs={{0,0},{1,1},{2,2},{3,3},{4,4},{5,5},{6,6},{7,7},{8,8},{9,9},{10,10... | collective-permute-start | bytes 49160 | tf_op jit(solution)/shard_map/ppermute | solution.py:27
  15.6 12.4 %collective-permute-start.5 = (bf16[1,256,256]{2,1,0:T(8,128)(2,1)}, bf16[1,256,256]{2,1,0:T(8,128)(2,1)S(1)}, u32[]{:S(2)}, u32[]{:S(2)}) collective-permute-start(bf16[1,256,256]{2,1,0:T(8,128)(2,1)} %bitcast.24), channel_id=1, source_target_pairs={{0,8},{2,10},{4,12},{6,14},{8,0},{10,2},{12,4},{14,6},{1,9},{3,11}... | collective-permute-start | bytes 393224 | tf_op jit(solution)/shard_map/ppermute | solution.py:23
  22.6 16.6 %all-to-all-start.1 = ((bf16[16,16,768]{2,1,0:T(8,128)(2,1)}), bf16[16,16,768]{2,1,0:T(8,128)(2,1)S(1)}, u32[]{:S(2)}, u32[]{:S(2)}) async-start(bf16[16,16,768]{2,1,0:T(8,128)(2,1)} %bitcast.4), calls=%async_computation.1 | async-start | bytes 786432 | tf_op jit(solution)/shard_map/all_to_all | solution.py:19
  39.3 30.5 %collective-permute-start.6 = (bf16[2,256,256]{2,1,0:T(8,128)(2,1)S(1)}, bf16[2,256,256]{2,1,0:T(8,128)(2,1)S(1)}, u32[]{:S(2)}, u32[]{:S(2)}) collective-permute-start(bf16[2,256,256]{2,1,0:T(8,128)(2,1)S(1)} %pad_maximum_fusion), channel_id=1, source_target_pairs={{0,4},{2,6},{4,0},{6,2},{8,12},{10,14},{12,8},{14,10},{1,5},{3,7},... | collective-permute-start | bytes 786440 | tf_op jit(solution)/shard_map/ppermute | solution.py:23
  69.8 12.9 %collective-permute-start.7 = (bf16[4,256,256]{2,1,0:T(8,128)(2,1)S(1)}, bf16[4,256,256]{2,1,0:T(8,128)(2,1)S(1)}, u32[]{:S(2)}, u32[]{:S(2)}) collective-permute-start(bf16[4,256,256]{2,1,0:T(8,128)(2,1)S(1)} %constant_dynamic-update-slice_fusion), channel_id=1, source_target_pairs={{0,2},{2,0},{4,6},{6,4},{8,10},{10,8},{12,14},{14,12},{1,3},{3,1},... | collective-permute-start | bytes 1572872 | tf_op jit(solution)/shard_map/ppermute | solution.py:23
  82.8 11.1 %collective-permute-start.8 = (bf16[8,256,256]{2,1,0:T(8,128)(2,1)S(1)}, bf16[8,256,256]{2,1,0:T(8,128)(2,1)S(1)}, u32[]{:S(2)}, u32[]{:S(2)}) collective-permute-start(bf16[8,256,256]{2,1,0:T(8,128)(2,1)S(1)} %constant_dynamic-update-slice_fusion.2.mine), channel_id=1, source_target_pairs={{0,1},{1,0},{2,3},{3,2},{4,5},{5,4},{6,7},{7,6},{8,9},{9,8},{10,11... | collective-permute-start | bytes 3145736 | tf_op jit(solution)/shard_map/ppermute | solution.py:23

commit v6 on v5

--- a/solution.py
+++ b/solution.py
@@ -21,10 +21,6 @@
 
 def from_partner(x, axis, k):
     return lax.ppermute(x, axis, [(i, i ^ k) for i in range(lax.axis_size(axis))])
-
-
-def here(x):
-    return lax.ppermute(x, "core", [(i, i) for i in range(lax.axis_size("core"))])
 
 
 def fenced(*arrays):
@@ -147,17 +143,50 @@
     return high, low
 
 
-def project_kernel(group, shard, acts, own, embed, gain, w_query, w_key, w_value, terms, inputs):
+def project_kernel(
+    group,
+    shard,
+    acts,
+    embed_far,
+    gain_far,
+    w_query_far,
+    w_key_far,
+    w_value_far,
+    terms,
+    inputs,
+    embed,
+    gain,
+    w_query,
+    w_key,
+    w_value,
+    sems,
+):
     bins, width = embed.shape
     feats, cols = w_query.shape
-    chunk = 512
-    squares = jnp.zeros((bins, HEAD_DIM), jnp.float32)
-    for c in range(0, width, chunk):
-        wide = embed[:, c : c + chunk].astype(jnp.float32)
-        wide = wide * wide
-        for k in range(0, chunk, HEAD_DIM):
-            squares += wide[:, k : k + HEAD_DIM]
-    mean_square = jnp.sum(squares, axis=-1, keepdims=True) / width
+    rows = inputs.shape[0]
+    chunk = bins // 4
+    slabs = [slice(c, c + chunk) for c in range(0, bins, chunk)]
+    copies = [(embed_far.at[at], embed.at[at]) for at in slabs]
+    copies += [
+        (gain_far, gain),
+        (w_query_far, w_query),
+        (w_key_far, w_key),
+        (w_value_far, w_value),
+    ]
+    copies = [pltpu.make_async_copy(*ends, sems.at[k]) for k, ends in enumerate(copies)]
+    for copy in copies:
+        copy.start()
+    mean_square = []
+    for at, copy in zip(slabs, copies):
+        copy.wait()
+        squares = jnp.zeros((chunk, HEAD_DIM), jnp.float32)
+        for k in range(0, width, HEAD_DIM):
+            wide = embed[at, k : k + HEAD_DIM].astype(jnp.float32)
+            squares += wide * wide
+        mean_square.append(jnp.sum(squares, axis=-1, keepdims=True) / width)
+    mean_square = jnp.concatenate(mean_square, axis=0)
+    for copy in copies[len(slabs) :]:
+        copy.wait()
     here = pl.ds(pl.multiple_of(group[0] * feats, feats), feats)
     part = embed[:, here].astype(jnp.float32)
     lines = feats // HEAD_DIM
@@ -176,7 +205,10 @@
         out = jnp.dot(normed, w[...], preferred_element_type=jnp.float32)
         terms[:, k * cols : (k + 1) * cols] = out.astype(jnp.bfloat16)
     there = pl.ds(pl.multiple_of(shard[0] * cols, cols), cols)
-    inputs[...] = rows_of(own[...], embed[:, there])[: inputs.shape[0]]
+    count = acts.shape[1]
+    own = jnp.broadcast_to(acts[...], (8, count))
+    own = pltpu.roll(own, (count - group[0] * rows) % count, 1)[:1, :HEAD_DIM]
+    inputs[...] = rows_of(own, embed[:, there])[:rows]
 
 
 def attend_kernel(shard, lengths, spread, keys_far, values_far, packed, keys, values, sems):
@@ -185,32 +217,31 @@
     steps = 8
     n = packed.shape[1] - 8
     scale = HEAD_DIM ** (-0.5)
-    group = 2
+    chunk = prompt_dev // 4
     copies = []
-    for k in range(seqs // group):
-        at = slice(k * group * cols, (k + 1) * group * cols)
-        copies.append(
-            [
-                pltpu.make_async_copy(src.at[:, :, at], dst.at[:, :, at], sems.at[i, k])
-                for i, (src, dst) in enumerate(((keys_far, keys), (values_far, values)))
-            ]
-        )
-        for copy in copies[-1]:
-            copy.start()
+    for r in range(robots):
+        for i, (src, dst) in enumerate(((keys_far, keys), (values_far, values))):
+            pieces = [(r, slice(k * chunk, (k + 1) * chunk)) for k in range(4)]
+            copies.append(
+                [
+                    pltpu.make_async_copy(src.at[at], dst.at[at], sems.at[2 * r + i, k])
+                    for k, at in enumerate(pieces)
+                ]
+            )
+            for copy in copies[-1]:
+                copy.start()
     first = lax.broadcasted_iota(jnp.int32, (steps, cols), 1) < HEAD_DIM
     place = lax.broadcasted_iota(jnp.int32, (2 * steps, prompt_dev), 1) + shard[0] * prompt_dev
-    block = lax.broadcasted_iota(jnp.int32, (4 * n, HEAD_DIM), 1)
-    stats = jnp.zeros((4 * n, HEAD_DIM), jnp.float32)
-    for b in range(seqs):
-        if b % group == 0:
-            for copy in copies[b // group]:
-                copy.wait()
-        query = spread[b, : robots * steps, :].astype(jnp.float32)
-        at = slice(b * cols, (b + 1) * cols)
-        columns = []
-        for r in range(robots):
-            valid = place < lengths[r]
-            q = query[r * steps : (r + 1) * steps]
+    lane = lax.broadcasted_iota(jnp.int32, (2 * steps, HEAD_DIM), 1)
+    stats = [[jnp.zeros((2 * steps, HEAD_DIM), jnp.float32)] * 4 for _ in range(robots)]
+    for r in range(robots):
+        valid = place < lengths[r]
+        for copy in copies[2 * r]:
+            copy.wait()
+        weights = []
+        for b in range(seqs):
+            at = slice(b * cols, (b + 1) * cols)
+            q = spread[b, : robots * steps, :].astype(jnp.float32)[r * steps : (r + 1) * steps]
             q = jnp.concatenate([jnp.where(first, q, 0.0), jnp.where(first, 0.0, q)], axis=0)
             scores = lax.dot_general(
                 q.astype(jnp.bfloat16),
@@ -221,14 +252,17 @@
             scores = jnp.where(valid, scores * scale, NEG)
             high, low = parts_of(jnp.max(scores, axis=-1, keepdims=True))
             e = jnp.where(valid, jnp.exp(scores - (high + low)), 0.0)
-            columns.append((high, low, *parts_of(jnp.sum(e, axis=-1, keepdims=True))))
-            acc = jnp.dot(
-                e.astype(jnp.bfloat16), values[r, :, at], preferred_element_type=jnp.float32
-            )
+            columns = (high, low, *parts_of(jnp.sum(e, axis=-1, keepdims=True)))
+            stats[r] = [jnp.where(lane == b, c, old) for c, old in zip(columns, stats[r])]
+            weights.append(e.astype(jnp.bfloat16))
+        for copy in copies[2 * r + 1]:
+            copy.wait()
+        for b in range(seqs):
+            at = slice(b * cols, (b + 1) * cols)
+            acc = jnp.dot(weights[b], values[r, :, at], preferred_element_type=jnp.float32)
             acc = jnp.concatenate([acc[:steps, :HEAD_DIM], acc[steps:, HEAD_DIM:]], axis=0)
             packed[b, r * 2 * steps : (r + 1) * 2 * steps, :] = acc.astype(jnp.bfloat16)
-        column = jnp.concatenate([columns[r][k] for k in range(4) for r in range(robots)], axis=0)
-        stats = jnp.where(block == b, column, stats)
+    stats = jnp.concatenate([stats[r][k] for k in range(4) for r in range(robots)], axis=0)
     stats = stats.T.astype(jnp.bfloat16)
     for b in range(seqs):
         packed[b, n:, :] = jnp.broadcast_to(stats[b : b + 1], (8, HEAD_DIM))
@@ -284,7 +318,7 @@
     steps = 8
     rows = robots * steps
     _, width = key_cache.shape[1:]
-    _, cols = w_query.shape
+    feats, cols = w_query.shape
     bins = embed.shape[0]
     own_bins = head.shape[0]
     lh = cols // HEAD_DIM
@@ -292,8 +326,6 @@
     f32 = jnp.float32
     array = jax.ShapeDtypeStruct
 
-    near = [here(x) for x in (embed, attn_gain.reshape(-1, HEAD_DIM), w_query, w_key, w_value)]
-
     blocks = w_out[None]
     arrived = from_partner(blocks, "z", 4)
     zs = [0, 4]
@@ -304,16 +336,25 @@
     acts = exchange(acts, GRP).reshape(groups * robots, true_steps)
     pad_steps = ((0, 0), (0, steps - true_steps))
     acts = jnp.pad(acts, pad_steps).reshape(1, groups * rows)
-    own = jnp.pad(jnp.pad(actions, pad_steps).reshape(1, rows), ((0, 0), (0, HEAD_DIM - rows)))
     terms, inputs = call(
         project_kernel,
         (array((groups * rows, 3 * cols), jnp.bfloat16), array((rows, cols), f32)),
-        [in_smem()] * 2 + [in_vmem()] * 7,
+        [in_smem()] * 2 + [in_vmem()] + [far()] * 5,
         g[None],
         s[None],
         acts,
-        own,
-        *near,
+        embed,
+        attn_gain.reshape(-1, HEAD_DIM),
+        w_query,
+        w_key,
+        w_value,
+        scratch=[
+            pltpu.VMEM((bins, width), jnp.bfloat16),
+            pltpu.VMEM((width // HEAD_DIM, HEAD_DIM), f32),
+            *[pltpu.VMEM((feats, cols), jnp.bfloat16)] * 3,
+            pltpu.SemaphoreType.DMA((8,)),
+        ],
+        limit=56,
     )
     terms, lengths, final_gain, head, shard = fenced(terms, lengths, final_gain, head, s[None])
     sums = exchange(terms.reshape(groups, rows, 3 * cols), GRP)
@@ -326,6 +367,7 @@
     sine = jnp.concatenate([-jnp.sin(angle), jnp.sin(angle)], axis=1)
     own_gain = lax.dynamic_slice(final_gain, (s * cols,), (cols,))[None]
     head_parts = jnp.swapaxes(head.reshape(own_bins, seqs, cols), 0, 1)
+    z, core = fenced(z, core, terms)[:2]
     order = (z ^ jnp.array(zs, jnp.int32)) * lax.axis_size("core")
     order = jnp.concatenate([order + core, order + 1 - core])
     blocks = jnp.concatenate([blocks, arrived], axis=0)
@@ -358,7 +400,7 @@
         scratch=[
             pltpu.VMEM(key_cache.shape, jnp.bfloat16),
             pltpu.VMEM(value_cache.shape, jnp.bfloat16),
-            pltpu.SemaphoreType.DMA((2, seqs // 2)),
+            pltpu.SemaphoreType.DMA((2 * robots, 4)),
         ],
         limit=52,
     )

time: 109 us -> 100 us (0.917)
  Pallas kernels: 16.9 us -> 11.6 us
  starting transfers between devices: 26.6 us -> 21.5 us
  waiting for transfers between devices: 8.12 us -> 10.1 us
    pallas_call x6, Pallas kernels: 16.9 us -> 11.6 us  [call(): pl.pallas_call(kernel, out_shape=out, in_specs=specs, out_specs=outs, scr...]
    ppermute x5 -> x0, starting transfers between devices: 5.04 us -> none  [here(): lax.ppermute(x, 'core', [(i, i) for i in range(lax.axis_size('core'))])]
    all_to_all x2, waiting for transfers between devices: 7.61 us -> 10.1 us  [exchange(): return lax.all_to_all(pieces, axis, split_axis=0, concat_axis=0, tiled=True)]
  transfers between devices with their start and end apart: 11 -> 6, of which waited for: 2 -> 2; matrix products, arithmetic and copies ran while one was open for 6% -> 5% of each run, Pallas kernels for 14% -> 10%
where the time goes in v6:
time: 100 us; the launch traced here: 99.2 us
  blocking collectives  49.4 us (49%)
  starting transfers between devices  21.5 us (22%)
  Pallas kernels  11.6 us (12%)
  waiting for transfers between devices  10.1 us (10%)
  local copies, waits for them, and re-layouts  3.86 us (4%)
  other arithmetic  2.6 us (3%)
    all_to_all x4, blocking collectives, exchange(): return lax.all_to_all(pieces, axis, split_axis=0, concat_axis=0, tiled=True)  49.4 us
    all_to_all x2, starting transfers between devices, exchange(): return lax.all_to_all(pieces, axis, split_axis=0, concat_axis=0, tiled=True)  13.3 us
    pallas_call x6, Pallas kernels, call(): pl.pallas_call(kernel, out_shape=out, in_specs=specs, out_specs=outs, scr...  11.6 us
    all_to_all x2, waiting for transfers between devices, exchange(): return lax.all_to_all(pieces, axis, split_axis=0, concat_axis=0, tiled=True)  10.1 us
    ppermute x4, starting transfers between devices, from_partner(): lax.ppermute(x, axis, [(i, i ^ k) for i in range(lax.axis_size(axis))])  8.14 us
  transfers between devices with their start and end apart: 6, of which 2 were waited for; matrix products, arithmetic and copies ran while one was open for 5% of the time, Pallas kernels for 10%

profile of v6, /device:TPU:32, one launch (start us, length us, event | category | flops | bytes accessed | tf_op | source)
XLA Modules:
  0.0 99.2 jit_solution(15203792753328765759)
XLA Ops:
  0.0 1.3 %broadcast_in_dim.24 = s32[16,2,7]{2,1,0:T(2,128)} broadcast(s32[2,7]{1,0:T(2,128)} %param.13), dimensions={1,2} | broadcast | bytes 952 | tf_op jit(solution)/shard_map/broadcast_in_dim | solution.py:335
  1.3 8.6 %all-to-all-start = ((s32[16,2,7]{2,1,0:T(2,128)}), s32[16,2,7]{2,1,0:T(2,128)S(1)}, u32[]{:S(2)}, u32[]{:S(2)}) async-start(s32[16,2,7]{2,1,0:T(2,128)} %broadcast_in_dim.24), calls=%async_computation | async-start | bytes 32768 | tf_op jit(solution)/shard_map/all_to_all | solution.py:19
  9.9 4.5 %collective-permute-start = (bf16[1,256,256]{2,1,0:T(8,128)(2,1)}, bf16[1,256,256]{2,1,0:T(8,128)(2,1)S(1)}, u32[]{:S(2)}, u32[]{:S(2)}) collective-permute-start(bf16[1,256,256]{2,1,0:T(8,128)(2,1)} %bitcast.25), channel_id=1, source_target_pairs={{0,8},{2,10},{4,12},{6,14},{8,0},{10,2},{12,4},{14,6},{1,9},{3,11}... | collective-permute-start | bytes 393224 | tf_op jit(solution)/shard_map/ppermute | solution.py:23
  14.4 1.9 %all-to-all-done = s32[16,2,7]{2,1,0:T(2,128)S(1)} async-done(((s32[16,2,7]{2,1,0:T(2,128)}), s32[16,2,7]{2,1,0:T(2,128)S(1)}, u32[]{:S(2)}, u32[]{:S(2)}) %all-to-all-start) | async-done | bytes 928 | tf_op jit(solution)/shard_map/all_to_all | solution.py:19
  16.2 0.7 reshape.44.acts
  16.9 3.8 %shard_map.127 = (bf16[256,768]{1,0:T(8,128)(2,1)}, f32[16,256]{1,0:T(8,128)}) custom-call(s32[1]{0:T(128)} %bitcast.group, s32[1]{0:T(128)} %bitcast.1.shard, s32[1,256]{1,0:T(1,128)} %reshape.44.acts, bf16[256,4096]{1,0:T(8,128)(2,1)} %embed_far.1, f32[32,128]{1,0:T(8,128)} %bitcast.28, bf16[256,256]{1,0:T(8,128)(2,1)} %w_query_far.1, ...), custom_call_target="tpu_custom_call" | custom-call | tf_op jit(solution)/shard_map/pallas_call | solution.py:44
  20.7 0.7 add_convert_fusion
  21.5 4.8 %all-to-all-start.1 = ((bf16[16,16,768]{2,1,0:T(8,128)(2,1)}), bf16[16,16,768]{2,1,0:T(8,128)(2,1)S(1)}, u32[]{:S(2)}, u32[]{:S(2)}) async-start(bf16[16,16,768]{2,1,0:T(8,128)(2,1)} %bitcast.23), calls=%async_computation.1 | async-start | bytes 786432 | tf_op jit(solution)/shard_map/all_to_all | solution.py:19
  26.3 0.7 fusion.1
  26.9 0.1 fusion
  27.1 0.9 copy.19
  28.1 0.8 dynamic_slice.3
  28.9 0.9 pad_maximum_fusion
  29.8 8.2 %all-to-all-done.1.sums = bf16[16,16,768]{2,1,0:T(8,128)(2,1)S(1)} async-done(((bf16[16,16,768]{2,1,0:T(8,128)(2,1)}), bf16[16,16,768]{2,1,0:T(8,128)(2,1)S(1)}, u32[]{:S(2)}, u32[]{:S(2)}) %all-to-all-start.1) | async-done | bytes 393248 | tf_op jit(solution)/shard_map/all_to_all | solution.py:19
  38.1 2.8 %collective-permute-start.1 = (bf16[2,256,256]{2,1,0:T(8,128)(2,1)S(1)}, bf16[2,256,256]{2,1,0:T(8,128)(2,1)S(1)}, u32[]{:S(2)}, u32[]{:S(2)}) collective-permute-start(bf16[2,256,256]{2,1,0:T(8,128)(2,1)S(1)} %pad_maximum_fusion), channel_id=1, source_target_pairs={{0,4},{2,6},{4,0},{6,2},{8,12},{10,14},{12,8},{14,10},{1,5},{3,7},... | collective-permute-start | bytes 786440 | tf_op jit(solution)/shard_map/ppermute | solution.py:23
  41.0 15.5 %all_to_all.30.spread = bf16[16,32,256]{2,1,0:T(8,128)(2,1)S(1)} all-to-all(bf16[16,32,256]{2,1,0:T(8,128)(2,1)S(1)} %get-tuple-element.52), channel_id=1, replica_groups=mesh['seq_0'=4,'seq_1'=4,'z'=8,'core'=2] {'seq_0','seq_1'}, dimensions={0} | all-to-all | bytes 524288 | tf_op jit(solution)/shard_map/all_to_all | solution.py:19
  56.5 4.7 %shard_map.129 = bf16[16,40,128]{2,1,0:T(8,128)(2,1)S(1)} custom-call(s32[1]{0:T(128)} %bitcast.1.shard, s32[2]{0:T(128)S(1)} %copy-done.1, bf16[16,32,256]{2,1,0:T(8,128)(2,1)S(1)} %all_to_all.30.spread, bf16[2,256,4096]{2,1,0:T(8,128)(2,1)} %keys_far.1, bf16[2,256,4096]{2,1,0:T(8,128)(2,1)} %values_far.1), custom_call_target="tpu_custom_call" | custom-call | tf_op jit(solution)/shard_map/pallas_call | solution.py:44
  61.3 0.8 collective-permute-start.2
  62.1 11.1 %all_to_all.31.packed = bf16[16,40,128]{2,1,0:T(8,128)(2,1)S(1)} all-to-all(bf16[16,40,128]{2,1,0:T(8,128)(2,1)S(1)} %shard_map.129), channel_id=1, replica_groups=mesh['seq_0'=4,'seq_1'=4,'z'=8,'core'=2] {'seq_0','seq_1'}, dimensions={0} | all-to-all | bytes 327680 | tf_op jit(solution)/shard_map/all_to_all | solution.py:19
  73.2 1.0 %shard_map.130 = bf16[16,16,256]{2,1,0:T(8,128)(2,1)S(1)} custom-call(f32[16,256]{1,0:T(8,128)S(1)} %get-tuple-element.49.query, f32[16,256]{1,0:T(8,128)S(1)} %get-tuple-element.50.key, f32[16,256]{1,0:T(8,128)S(1)} %get-tuple-element.51.value, bf16[16,128]{1,0:T(8,128)(2,1)S(1)} %bitcast.21, bf16[16,40,128]{2,1,0:T(8,128)(2,1)S(1)} %all_to_all.31.packed), custom_call_target="tpu_custom_call" | custom-call | tf_op jit(solution)/shard_map/pallas_call | solution.py:44
  74.4 11.0 %all_to_all.32.blocks = bf16[16,16,256]{2,1,0:T(8,128)(2,1)S(1)} all-to-all(bf16[16,16,256]{2,1,0:T(8,128)(2,1)S(1)} %shard_map.130), channel_id=1, replica_groups=mesh['seq_0'=4,'seq_1'=4,'z'=8,'core'=2] {'seq_0','seq_1'}, dimensions={0} | all-to-all | bytes 262144 | tf_op jit(solution)/shard_map/all_to_all | solution.py:19
  85.4 1.1 %shard_map.131 = f32[16,16,256]{2,1,0:T(8,128)S(1)} custom-call(s32[16]{0:T(128)S(1)} %pad_add_fusion.places, bf16[16,16,256]{2,1,0:T(8,128)(2,1)S(1)} %all_to_all.32.blocks, bf16[8,256,256]{2,1,0:T(8,128)(2,1)S(1)} %constant_dynamic-update-slice_fusion.2.mine, bf16[8,256,256]{2,1,0:T(8,128)(2,1)S(1)} %collective-permute-done.3.other, ...), custom_call_target="tpu_custom_call" | custom-call | tf_op jit(solution)/shard_map/pallas_call | solution.py:44
  86.5 11.8 %all_to_all.33.parts = f32[16,16,256]{2,1,0:T(8,128)S(1)} all-to-all(f32[16,16,256]{2,1,0:T(8,128)S(1)} %shard_map.131), channel_id=1, replica_groups=mesh['seq_0'=4,'seq_1'=4,'z'=8,'core'=2] {'seq_0','seq_1'}, dimensions={0} | all-to-all | bytes 524288 | tf_op jit(solution)/shard_map/all_to_all | solution.py:19
  98.3 0.9 shard_map.132
  (22 shorter events, 0.6 us)
Async XLA Ops:
  0.0 56.5 %copy-start.1 = (s32[2]{0:T(128)S(1)}, s32[2]{0:T(128)}, u32[]{:S(2)}) copy-start(s32[2]{0:T(128)} %lengths) | copy-start | bytes 28
  1.3 14.9 %all-to-all-start = ((s32[16,2,7]{2,1,0:T(2,128)}), s32[16,2,7]{2,1,0:T(2,128)S(1)}, u32[]{:S(2)}, u32[]{:S(2)}) async-start(s32[16,2,7]{2,1,0:T(2,128)} %broadcast_in_dim.24), calls=%async_computation | async-start | bytes 32768 | tf_op jit(solution)/shard_map/all_to_all | solution.py:19
  9.9 19.0 %collective-permute-start = (bf16[1,256,256]{2,1,0:T(8,128)(2,1)}, bf16[1,256,256]{2,1,0:T(8,128)(2,1)S(1)}, u32[]{:S(2)}, u32[]{:S(2)}) collective-permute-start(bf16[1,256,256]{2,1,0:T(8,128)(2,1)} %bitcast.25), channel_id=1, source_target_pairs={{0,8},{2,10},{4,12},{6,14},{8,0},{10,2},{12,4},{14,6},{1,9},{3,11}... | collective-permute-start | bytes 393224 | tf_op jit(solution)/shard_map/ppermute | solution.py:23
  21.5 16.6 %all-to-all-start.1 = ((bf16[16,16,768]{2,1,0:T(8,128)(2,1)}), bf16[16,16,768]{2,1,0:T(8,128)(2,1)S(1)}, u32[]{:S(2)}, u32[]{:S(2)}) async-start(bf16[16,16,768]{2,1,0:T(8,128)(2,1)} %bitcast.23), calls=%async_computation.1 | async-start | bytes 786432 | tf_op jit(solution)/shard_map/all_to_all | solution.py:19
  38.1 23.1 %collective-permute-start.1 = (bf16[2,256,256]{2,1,0:T(8,128)(2,1)S(1)}, bf16[2,256,256]{2,1,0:T(8,128)(2,1)S(1)}, u32[]{:S(2)}, u32[]{:S(2)}) collective-permute-start(bf16[2,256,256]{2,1,0:T(8,128)(2,1)S(1)} %pad_maximum_fusion), channel_id=1, source_target_pairs={{0,4},{2,6},{4,0},{6,2},{8,12},{10,14},{12,8},{14,10},{1,5},{3,7},... | collective-permute-start | bytes 786440 | tf_op jit(solution)/shard_map/ppermute | solution.py:23
  56.5 28.9 %copy-start = (f32[16,256]{1,0:T(8,128)S(1)}, f32[16,256]{1,0:T(8,128)}, u32[]{:S(2)}) copy-start(f32[16,256]{1,0:T(8,128)} %get-tuple-element.60.inputs) | copy-start | bytes 49156
  61.3 12.9 %collective-permute-start.2 = (bf16[4,256,256]{2,1,0:T(8,128)(2,1)S(1)}, bf16[4,256,256]{2,1,0:T(8,128)(2,1)S(1)}, u32[]{:S(2)}, u32[]{:S(2)}) collective-permute-start(bf16[4,256,256]{2,1,0:T(8,128)(2,1)S(1)} %constant_dynamic-update-slice_fusion), channel_id=1, source_target_pairs={{0,2},{2,0},{4,6},{6,4},{8,10},{10,8},{12,14},{14,12},{1,3},{3,1},... | collective-permute-start | bytes 1572872 | tf_op jit(solution)/shard_map/ppermute | solution.py:23
  74.3 11.1 %collective-permute-start.3 = (bf16[8,256,256]{2,1,0:T(8,128)(2,1)S(1)}, bf16[8,256,256]{2,1,0:T(8,128)(2,1)S(1)}, u32[]{:S(2)}, u32[]{:S(2)}) collective-permute-start(bf16[8,256,256]{2,1,0:T(8,128)(2,1)S(1)} %constant_dynamic-update-slice_fusion.2.mine), channel_id=1, source_target_pairs={{0,1},{1,0},{2,3},{3,2},{4,5},{5,4},{6,7},{7,6},{8,9},{9,8},{10,11... | collective-permute-start | bytes 3145736 | tf_op jit(solution)/shard_map/ppermute | solution.py:23

commit v7 on v6

--- a/solution.py
+++ b/solution.py
@@ -143,75 +143,50 @@
     return high, low
 
 
-def project_kernel(
-    group,
-    shard,
-    acts,
-    embed_far,
-    gain_far,
-    w_query_far,
-    w_key_far,
-    w_value_far,
-    terms,
-    inputs,
-    embed,
-    gain,
-    w_query,
-    w_key,
-    w_value,
-    sems,
-):
+def table_kernel(group, embed_far, gain_far, table, embed, gain, sems):
     bins, width = embed.shape
-    feats, cols = w_query.shape
-    rows = inputs.shape[0]
+    feats = table.shape[1]
     chunk = bins // 4
     slabs = [slice(c, c + chunk) for c in range(0, bins, chunk)]
-    copies = [(embed_far.at[at], embed.at[at]) for at in slabs]
-    copies += [
-        (gain_far, gain),
-        (w_query_far, w_query),
-        (w_key_far, w_key),
-        (w_value_far, w_value),
-    ]
+    copies = [(embed_far.at[at], embed.at[at]) for at in slabs] + [(gain_far, gain)]
     copies = [pltpu.make_async_copy(*ends, sems.at[k]) for k, ends in enumerate(copies)]
     for copy in copies:
         copy.start()
-    mean_square = []
+    here = pl.ds(pl.multiple_of(group[0] * feats, feats), feats)
+    lines = feats // HEAD_DIM
+    copies[-1].wait()
+    row = jnp.concatenate([gain[pl.ds(group[0] * lines + k, 1)] for k in range(lines)], axis=1)
     for at, copy in zip(slabs, copies):
         copy.wait()
         squares = jnp.zeros((chunk, HEAD_DIM), jnp.float32)
         for k in range(0, width, HEAD_DIM):
             wide = embed[at, k : k + HEAD_DIM].astype(jnp.float32)
             squares += wide * wide
-        mean_square.append(jnp.sum(squares, axis=-1, keepdims=True) / width)
-    mean_square = jnp.concatenate(mean_square, axis=0)
-    for copy in copies[len(slabs) :]:
-        copy.wait()
-    here = pl.ds(pl.multiple_of(group[0] * feats, feats), feats)
-    part = embed[:, here].astype(jnp.float32)
-    lines = feats // HEAD_DIM
-    row = jnp.concatenate([gain[pl.ds(group[0] * lines + k, 1)] for k in range(lines)], axis=1)
-    table = (part * lax.rsqrt(mean_square + 1e-05) * row).astype(jnp.bfloat16)
-    by_bin = lax.broadcasted_iota(jnp.int32, (bins, acts.shape[1]), 0)
-
-    def rows_of(numbers, values):
-        hot = jnp.where(by_bin[:, : numbers.shape[1]] == numbers, 1.0, 0.0).astype(jnp.bfloat16)
-        return lax.dot_general(
-            hot, values, (((0,), (0,)), ((), ())), preferred_element_type=jnp.float32
-        )
-
-    normed = rows_of(acts[...], table).astype(jnp.bfloat16)
+        mean_square = jnp.sum(squares, axis=-1, keepdims=True) / width
+        part = embed[at, here].astype(jnp.float32)
+        table[at] = (part * lax.rsqrt(mean_square + 1e-05) * row).astype(jnp.bfloat16)
+
+
+def project_kernel(acts, table, w_query, w_key, w_value, terms):
+    bins, cols = table.shape[0], w_query.shape[1]
+    count = acts.shape[1]
+    by_bin = lax.broadcasted_iota(jnp.int32, (bins, count), 0)
+    hot = jnp.where(by_bin == acts[...], 1.0, 0.0).astype(jnp.bfloat16)
+    normed = lax.dot_general(
+        hot, table[...], (((0,), (0,)), ((), ())), preferred_element_type=jnp.float32
+    ).astype(jnp.bfloat16)
     for k, w in enumerate((w_query, w_key, w_value)):
         out = jnp.dot(normed, w[...], preferred_element_type=jnp.float32)
         terms[:, k * cols : (k + 1) * cols] = out.astype(jnp.bfloat16)
-    there = pl.ds(pl.multiple_of(shard[0] * cols, cols), cols)
-    count = acts.shape[1]
-    own = jnp.broadcast_to(acts[...], (8, count))
-    own = pltpu.roll(own, (count - group[0] * rows) % count, 1)[:1, :HEAD_DIM]
-    inputs[...] = rows_of(own, embed[:, there])[:rows]
-
-
-def attend_kernel(shard, lengths, spread, keys_far, values_far, packed, keys, values, sems):
+
+
+def fetch_kernel(keys_far, keys, sem):
+    copy = pltpu.make_async_copy(keys_far.at[0], keys, sem)
+    copy.start()
+    copy.wait()
+
+
+def attend_kernel(shard, lengths, spread, early, keys_far, values_far, packed, keys, values, sems):
     seqs, _, cols = spread.shape
     robots, prompt_dev, _ = keys.shape
     steps = 8
@@ -221,6 +196,9 @@
     copies = []
     for r in range(robots):
         for i, (src, dst) in enumerate(((keys_far, keys), (values_far, values))):
+            if r == 0 and i == 0:
+                copies.append([])
+                continue
             pieces = [(r, slice(k * chunk, (k + 1) * chunk)) for k in range(4)]
             copies.append(
                 [
@@ -245,7 +223,7 @@
             q = jnp.concatenate([jnp.where(first, q, 0.0), jnp.where(first, 0.0, q)], axis=0)
             scores = lax.dot_general(
                 q.astype(jnp.bfloat16),
-                keys[r, :, at],
+                keys[r, :, at] if r else early[:, at],
                 (((1,), (1,)), ((), ())),
                 preferred_element_type=jnp.float32,
             )
@@ -336,27 +314,34 @@
     acts = exchange(acts, GRP).reshape(groups * robots, true_steps)
     pad_steps = ((0, 0), (0, steps - true_steps))
     acts = jnp.pad(acts, pad_steps).reshape(1, groups * rows)
-    terms, inputs = call(
-        project_kernel,
-        (array((groups * rows, 3 * cols), jnp.bfloat16), array((rows, cols), f32)),
-        [in_smem()] * 2 + [in_vmem()] + [far()] * 5,
+    table = call(
+        table_kernel,
+        array((bins, feats), jnp.bfloat16),
+        [in_smem()] + [far()] * 2,
         g[None],
-        s[None],
-        acts,
         embed,
         attn_gain.reshape(-1, HEAD_DIM),
+        scratch=[
+            pltpu.VMEM((bins, width), jnp.bfloat16),
+            pltpu.VMEM((width // HEAD_DIM, HEAD_DIM), f32),
+            pltpu.SemaphoreType.DMA((5,)),
+        ],
+        limit=56,
+    )
+    terms = call(
+        project_kernel,
+        array((groups * rows, 3 * cols), jnp.bfloat16),
+        [in_vmem()] * 5,
+        acts,
+        table,
         w_query,
         w_key,
         w_value,
-        scratch=[
-            pltpu.VMEM((bins, width), jnp.bfloat16),
-            pltpu.VMEM((width // HEAD_DIM, HEAD_DIM), f32),
-            *[pltpu.VMEM((feats, cols), jnp.bfloat16)] * 3,
-            pltpu.SemaphoreType.DMA((8,)),
-        ],
         limit=56,
     )
-    terms, lengths, final_gain, head, shard = fenced(terms, lengths, final_gain, head, s[None])
+    terms, lengths, final_gain, head, shard, actions, key_cache = fenced(
+        terms, lengths, final_gain, head, s[None], actions, key_cache
+    )
     sums = exchange(terms.reshape(groups, rows, 3 * cols), GRP)
 
     places = (lengths[:, None] + jnp.arange(steps, dtype=jnp.int32)[None, :]).astype(f32)
@@ -365,14 +350,26 @@
     angle = places.reshape(rows, 1) * freq
     cosine = jnp.concatenate([jnp.cos(angle)] * 2, axis=1)
     sine = jnp.concatenate([-jnp.sin(angle), jnp.sin(angle)], axis=1)
+    own = jnp.pad(actions, pad_steps).reshape(rows)
+    own = (own[:, None] == jnp.arange(bins, dtype=jnp.int32)[None, :]).astype(jnp.bfloat16)
+    own_embed = lax.dynamic_slice(embed, (0, s * cols), (bins, cols))
+    inputs = jnp.dot(own, own_embed, preferred_element_type=f32)
+    early = call(
+        fetch_kernel,
+        array(key_cache.shape[1:], key_cache.dtype),
+        [far()],
+        key_cache,
+        scratch=[pltpu.SemaphoreType.DMA(())],
+        limit=50,
+    )
     own_gain = lax.dynamic_slice(final_gain, (s * cols,), (cols,))[None]
     head_parts = jnp.swapaxes(head.reshape(own_bins, seqs, cols), 0, 1)
     z, core = fenced(z, core, terms)[:2]
     order = (z ^ jnp.array(zs, jnp.int32)) * lax.axis_size("core")
     order = jnp.concatenate([order + core, order + 1 - core])
     blocks = jnp.concatenate([blocks, arrived], axis=0)
-    (sums, cosine, sine, inputs, own_gain, head_parts, order, shard, blocks) = fenced(
-        sums, cosine, sine, inputs, own_gain, head_parts, order, shard, blocks
+    (sums, cosine, sine, inputs, own_gain, head_parts, order, shard, blocks, early) = fenced(
+        sums, cosine, sine, inputs, own_gain, head_parts, order, shard, blocks, early
     )
     arrived = from_partner(blocks, "z", 2)
 
@@ -391,10 +388,11 @@
     packed = call(
         attend_kernel,
         array((seqs, n + 8, HEAD_DIM), jnp.bfloat16),
-        [in_smem()] * 2 + [in_vmem()] + [far()] * 2,
+        [in_smem()] * 2 + [in_vmem()] * 2 + [far()] * 2,
         shard,
         lengths,
         spread,
+        early,
         key_cache,
         value_cache,
         scratch=[
@@ -402,7 +400,7 @@
             pltpu.VMEM(value_cache.shape, jnp.bfloat16),
             pltpu.SemaphoreType.DMA((2 * robots, 4)),
         ],
-        limit=52,
+        limit=50,
     )
     packed, blocks, arrived, head_cols = fenced(packed, blocks, arrived, head_cols)
     blocks = jnp.concatenate([blocks, arrived], axis=0)

time: 100 us -> 99.2 us (level)
  Pallas kernels: 11.6 us -> 14.6 us
  other arithmetic: 2.6 us -> 0.38 us
  waiting for transfers between devices: 10.1 us -> 7.96 us
  matrix products: 0 us -> 1.08 us
    pallas_call x6 -> x8, Pallas kernels: 11.6 us -> 14.6 us  [call(): pl.pallas_call(kernel, out_shape=out, in_specs=specs, out_specs=outs, scr...]
    all_to_all x2, waiting for transfers between devices: 10.1 us -> 7.95 us  [exchange(): return lax.all_to_all(pieces, axis, split_axis=0, concat_axis=0, tiled=True)]
    dot_general x0 -> x1, matrix products: none -> 1.08 us  [on_device(): inputs = jnp.dot(own, own_embed, preferred_element_type=f32)]
  transfers between devices with their start and end apart: 6 -> 6, of which waited for: 2 -> 1; matrix products, arithmetic and copies ran while one was open for 5% -> 3% of each run, Pallas kernels for 10% -> 13%
where the time goes in v7:
time: 99.2 us; the launch traced here: 98.2 us
  blocking collectives  49.4 us (50%)
  starting transfers between devices  21.5 us (22%)
  Pallas kernels  14.6 us (15%)
  waiting for transfers between devices  7.96 us (8%)
  local copies, waits for them, and re-layouts  3.1 us (3%)
  matrix products  1.08 us (1%)
    all_to_all x4, blocking collectives, exchange(): return lax.all_to_all(pieces, axis, split_axis=0, concat_axis=0, tiled=True)  49.4 us
    pallas_call x8, Pallas kernels, call(): pl.pallas_call(kernel, out_shape=out, in_specs=specs, out_specs=outs, scr...  14.6 us
    all_to_all x2, starting transfers between devices, exchange(): return lax.all_to_all(pieces, axis, split_axis=0, concat_axis=0, tiled=True)  13.4 us
    ppermute x4, starting transfers between devices, from_partner(): lax.ppermute(x, axis, [(i, i ^ k) for i in range(lax.axis_size(axis))])  8.14 us
    all_to_all x2, waiting for transfers between devices, exchange(): return lax.all_to_all(pieces, axis, split_axis=0, concat_axis=0, tiled=True)  7.95 us
  transfers between devices with their start and end apart: 6, of which 1 were waited for; matrix products, arithmetic and copies ran while one was open for 3% of the time, Pallas kernels for 13%

profile of v7, /device:TPU:32, one launch (start us, length us, event | category | flops | bytes accessed | tf_op | source)
XLA Modules:
  0.0 98.2 jit_solution(1809369213560684743)
XLA Ops:
  0.0 1.3 %broadcast_in_dim.10 = s32[16,2,7]{2,1,0:T(2,128)} broadcast(s32[2,7]{1,0:T(2,128)} %param.13), dimensions={1,2} | broadcast | bytes 952 | tf_op jit(solution)/shard_map/broadcast_in_dim | solution.py:313
  1.4 8.6 %all-to-all-start = ((s32[16,2,7]{2,1,0:T(2,128)}), s32[16,2,7]{2,1,0:T(2,128)S(1)}, u32[]{:S(2)}, u32[]{:S(2)}) async-start(s32[16,2,7]{2,1,0:T(2,128)} %broadcast_in_dim.10), calls=%async_computation | async-start | bytes 32768 | tf_op jit(solution)/shard_map/all_to_all | solution.py:19
  9.9 4.5 %collective-permute-start = (bf16[1,256,256]{2,1,0:T(8,128)(2,1)}, bf16[1,256,256]{2,1,0:T(8,128)(2,1)S(1)}, u32[]{:S(2)}, u32[]{:S(2)}) collective-permute-start(bf16[1,256,256]{2,1,0:T(8,128)(2,1)} %bitcast.25), channel_id=1, source_target_pairs={{0,8},{2,10},{4,12},{6,14},{8,0},{10,2},{12,4},{14,6},{1,9},{3,11}... | collective-permute-start | bytes 393224 | tf_op jit(solution)/shard_map/ppermute | solution.py:23
  14.4 2.9 %shard_map.127.table = bf16[256,256]{1,0:T(8,128)(2,1)} custom-call(s32[1]{0:T(128)} %bitcast.1.group, bf16[256,4096]{1,0:T(8,128)(2,1)} %embed_far.1, f32[32,128]{1,0:T(8,128)} %bitcast.28), custom_call_target="tpu_custom_call" | custom-call | tf_op jit(solution)/shard_map/pallas_call | solution.py:44
  17.3 0.7 reshape.45.acts
  18.0 2.3 %shard_map.128 = bf16[256,768]{1,0:T(8,128)(2,1)} custom-call(s32[1,256]{1,0:T(1,128)} %reshape.45.acts, bf16[256,256]{1,0:T(8,128)(2,1)} %shard_map.127.table, bf16[256,256]{1,0:T(8,128)(2,1)} %w_query.1, bf16[256,256]{1,0:T(8,128)(2,1)} %w_key.1, bf16[256,256]{1,0:T(8,128)(2,1)} %w_value.1), custom_call_target="tpu_custom_call" | custom-call | tf_op jit(solution)/shard_map/pallas_call | solution.py:44
  20.5 4.8 %all-to-all-start.1 = ((bf16[16,16,768]{2,1,0:T(8,128)(2,1)}), bf16[16,16,768]{2,1,0:T(8,128)(2,1)S(1)}, u32[]{:S(2)}, u32[]{:S(2)}) async-start(bf16[16,16,768]{2,1,0:T(8,128)(2,1)} %bitcast.23), calls=%async_computation.1 | async-start | bytes 786432 | tf_op jit(solution)/shard_map/all_to_all | solution.py:19
  25.4 1.1 %fusion.inputs = f32[16,256]{1,0:T(8,128)S(1)} fusion(bf16[256,4096]{1,0:T(8,128)(2,1)} %embed_far.1, s32[]{:T(128)S(6)} %select_n.4, s32[16]{0:T(128)S(1)} %eq.15), kind=kOutput, calls=%fused_computation.2 | convolution fusion | flops 2101248 | bytes 147524 | tf_op jit(solution)/shard_map/dot_general | solution.py:356
  26.5 0.1 fusion.3
  26.7 0.8 dynamic_slice.7
  27.4 1.6 %shard_map.129.early = bf16[256,4096]{1,0:T(8,128)(2,1)S(1)} custom-call(bf16[2,256,4096]{2,1,0:T(8,128)(2,1)} %keys_far.1), custom_call_target="tpu_custom_call" | custom-call | tf_op jit(solution)/shard_map/pallas_call | solution.py:44
  29.2 7.9 %all-to-all-done.1.sums = bf16[16,16,768]{2,1,0:T(8,128)(2,1)S(1)} async-done(((bf16[16,16,768]{2,1,0:T(8,128)(2,1)}), bf16[16,16,768]{2,1,0:T(8,128)(2,1)S(1)}, u32[]{:S(2)}, u32[]{:S(2)}) %all-to-all-start.1) | async-done | bytes 393248 | tf_op jit(solution)/shard_map/all_to_all | solution.py:19
  37.2 2.8 %collective-permute-start.1 = (bf16[2,256,256]{2,1,0:T(8,128)(2,1)S(1)}, bf16[2,256,256]{2,1,0:T(8,128)(2,1)S(1)}, u32[]{:S(2)}, u32[]{:S(2)}) collective-permute-start(bf16[2,256,256]{2,1,0:T(8,128)(2,1)S(1)} %pad_maximum_fusion), channel_id=1, source_target_pairs={{0,4},{2,6},{4,0},{6,2},{8,12},{10,14},{12,8},{14,10},{1,5},{3,7},... | collective-permute-start | bytes 786440 | tf_op jit(solution)/shard_map/ppermute | solution.py:23
  39.9 0.1 shard_map.130
  40.0 15.5 %all_to_all.30.spread = bf16[16,32,256]{2,1,0:T(8,128)(2,1)S(1)} all-to-all(bf16[16,32,256]{2,1,0:T(8,128)(2,1)S(1)} %get-tuple-element.53), channel_id=1, replica_groups=mesh['seq_0'=4,'seq_1'=4,'z'=8,'core'=2] {'seq_0','seq_1'}, dimensions={0} | all-to-all | bytes 524288 | tf_op jit(solution)/shard_map/all_to_all | solution.py:19
  55.6 4.6 %shard_map.131 = bf16[16,40,128]{2,1,0:T(8,128)(2,1)S(1)} custom-call(s32[1]{0:T(128)} %bitcast.3.shard, s32[2]{0:T(128)S(1)} %copy-done, bf16[16,32,256]{2,1,0:T(8,128)(2,1)S(1)} %all_to_all.30.spread, bf16[256,4096]{1,0:T(8,128)(2,1)S(1)} %shard_map.129.early, bf16[2,256,4096]{2,1,0:T(8,128)(2,1)} %keys_far.1, bf16[2,256,4096]{2,1,0:T(8,128)(2,1)} %values_far.1), custom_call_target="tpu_custom_call" | custom-call | tf_op jit(solution)/shard_map/pallas_call | solution.py:44
  60.2 0.8 collective-permute-start.2
  61.1 11.1 %all_to_all.31.packed = bf16[16,40,128]{2,1,0:T(8,128)(2,1)S(1)} all-to-all(bf16[16,40,128]{2,1,0:T(8,128)(2,1)S(1)} %shard_map.131), channel_id=1, replica_groups=mesh['seq_0'=4,'seq_1'=4,'z'=8,'core'=2] {'seq_0','seq_1'}, dimensions={0} | all-to-all | bytes 327680 | tf_op jit(solution)/shard_map/all_to_all | solution.py:19
  72.1 1.0 %shard_map.132 = bf16[16,16,256]{2,1,0:T(8,128)(2,1)S(1)} custom-call(f32[16,256]{1,0:T(8,128)S(1)} %get-tuple-element.50.query, f32[16,256]{1,0:T(8,128)S(1)} %get-tuple-element.51.key, f32[16,256]{1,0:T(8,128)S(1)} %get-tuple-element.52.value, bf16[16,128]{1,0:T(8,128)(2,1)S(1)} %bitcast.21, bf16[16,40,128]{2,1,0:T(8,128)(2,1)S(1)} %all_to_all.31.packed), custom_call_target="tpu_custom_call" | custom-call | tf_op jit(solution)/shard_map/pallas_call | solution.py:44
  73.2 0.1 collective-permute-start.3
  73.3 11.0 %all_to_all.32.blocks = bf16[16,16,256]{2,1,0:T(8,128)(2,1)S(1)} all-to-all(bf16[16,16,256]{2,1,0:T(8,128)(2,1)S(1)} %shard_map.132), channel_id=1, replica_groups=mesh['seq_0'=4,'seq_1'=4,'z'=8,'core'=2] {'seq_0','seq_1'}, dimensions={0} | all-to-all | bytes 262144 | tf_op jit(solution)/shard_map/all_to_all | solution.py:19
  84.4 1.1 %shard_map.133 = f32[16,16,256]{2,1,0:T(8,128)S(1)} custom-call(s32[16]{0:T(128)S(1)} %pad_add_fusion.places, bf16[16,16,256]{2,1,0:T(8,128)(2,1)S(1)} %all_to_all.32.blocks, bf16[8,256,256]{2,1,0:T(8,128)(2,1)S(1)} %constant_dynamic-update-slice_fusion.2.mine, bf16[8,256,256]{2,1,0:T(8,128)(2,1)S(1)} %collective-permute-done.3.other, ...), custom_call_target="tpu_custom_call" | custom-call | tf_op jit(solution)/shard_map/pallas_call | solution.py:44
  85.5 11.8 %all_to_all.33.parts = f32[16,16,256]{2,1,0:T(8,128)S(1)} all-to-all(f32[16,16,256]{2,1,0:T(8,128)S(1)} %shard_map.133), channel_id=1, replica_groups=mesh['seq_0'=4,'seq_1'=4,'z'=8,'core'=2] {'seq_0','seq_1'}, dimensions={0} | all-to-all | bytes 524288 | tf_op jit(solution)/shard_map/all_to_all | solution.py:19
  97.2 0.9 shard_map.134
  (33 shorter events, 0.6 us)
Async XLA Ops:
  0.0 20.5 %copy-start.3 = (s32[2,7]{1,0:T(2,128)S(1)}, s32[2,7]{1,0:T(2,128)}, u32[]{:S(2)}) copy-start(s32[2,7]{1,0:T(2,128)} %param.13) | copy-start | bytes 172
  0.0 20.3 %copy-start = (s32[2]{0:T(128)S(1)}, s32[2]{0:T(128)}, u32[]{:S(2)}) copy-start(s32[2]{0:T(128)} %lengths) | copy-start | bytes 28
  1.4 16.0 %all-to-all-start = ((s32[16,2,7]{2,1,0:T(2,128)}), s32[16,2,7]{2,1,0:T(2,128)S(1)}, u32[]{:S(2)}, u32[]{:S(2)}) async-start(s32[16,2,7]{2,1,0:T(2,128)} %broadcast_in_dim.10), calls=%async_computation | async-start | bytes 32768 | tf_op jit(solution)/shard_map/all_to_all | solution.py:19
  9.9 19.2 %collective-permute-start = (bf16[1,256,256]{2,1,0:T(8,128)(2,1)}, bf16[1,256,256]{2,1,0:T(8,128)(2,1)S(1)}, u32[]{:S(2)}, u32[]{:S(2)}) collective-permute-start(bf16[1,256,256]{2,1,0:T(8,128)(2,1)} %bitcast.25), channel_id=1, source_target_pairs={{0,8},{2,10},{4,12},{6,14},{8,0},{10,2},{12,4},{14,6},{1,9},{3,11}... | collective-permute-start | bytes 393224 | tf_op jit(solution)/shard_map/ppermute | solution.py:23
  14.4 12.0 %copy-start.4 = (s32[8]{0:T(128)S(1)}, s32[8]{0:T(128)}, u32[]{:S(2)}) copy-start(s32[8]{0:T(128)} %constant.40.clone) | copy-start | bytes 100
  20.5 16.6 %all-to-all-start.1 = ((bf16[16,16,768]{2,1,0:T(8,128)(2,1)}), bf16[16,16,768]{2,1,0:T(8,128)(2,1)S(1)}, u32[]{:S(2)}, u32[]{:S(2)}) async-start(bf16[16,16,768]{2,1,0:T(8,128)(2,1)} %bitcast.23), calls=%async_computation.1 | async-start | bytes 786432 | tf_op jit(solution)/shard_map/all_to_all | solution.py:19
  27.4 1.7 %copy-start.1 = (bf16[16,4096]{1,0:T(8,128)(2,1)S(1)}, bf16[16,4096]{1,0:T(8,128)(2,1)}, u32[]{:S(2)}) copy-start(bf16[16,4096]{1,0:T(8,128)(2,1)} %param.24) | copy-start | bytes 393220
  27.4 1.8 %copy-start.2 = (bf16[256,256]{1,0:T(8,128)(2,1)S(1)}, bf16[256,256]{1,0:T(8,128)(2,1)}, u32[]{:S(2)}) copy-start(bf16[256,256]{1,0:T(8,128)(2,1)} %param.20) | copy-start | bytes 393220
  37.2 23.0 %collective-permute-start.1 = (bf16[2,256,256]{2,1,0:T(8,128)(2,1)S(1)}, bf16[2,256,256]{2,1,0:T(8,128)(2,1)S(1)}, u32[]{:S(2)}, u32[]{:S(2)}) collective-permute-start(bf16[2,256,256]{2,1,0:T(8,128)(2,1)S(1)} %pad_maximum_fusion), channel_id=1, source_target_pairs={{0,4},{2,6},{4,0},{6,2},{8,12},{10,14},{12,8},{14,10},{1,5},{3,7},... | collective-permute-start | bytes 786440 | tf_op jit(solution)/shard_map/ppermute | solution.py:23
  60.2 12.9 %collective-permute-start.2 = (bf16[4,256,256]{2,1,0:T(8,128)(2,1)S(1)}, bf16[4,256,256]{2,1,0:T(8,128)(2,1)S(1)}, u32[]{:S(2)}, u32[]{:S(2)}) collective-permute-start(bf16[4,256,256]{2,1,0:T(8,128)(2,1)S(1)} %constant_dynamic-update-slice_fusion), channel_id=1, source_target_pairs={{0,2},{2,0},{4,6},{6,4},{8,10},{10,8},{12,14},{14,12},{1,3},{3,1},... | collective-permute-start | bytes 1572872 | tf_op jit(solution)/shard_map/ppermute | solution.py:23
  73.2 11.1 %collective-permute-start.3 = (bf16[8,256,256]{2,1,0:T(8,128)(2,1)S(1)}, bf16[8,256,256]{2,1,0:T(8,128)(2,1)S(1)}, u32[]{:S(2)}, u32[]{:S(2)}) collective-permute-start(bf16[8,256,256]{2,1,0:T(8,128)(2,1)S(1)} %constant_dynamic-update-slice_fusion.2.mine), channel_id=1, source_target_pairs={{0,1},{1,0},{2,3},{3,2},{4,5},{5,4},{6,7},{7,6},{8,9},{9,8},{10,11... | collective-permute-start | bytes 3145736 | tf_op jit(solution)/shard_map/ppermute | solution.py:23

commit v8 on v7

--- a/solution.py
+++ b/solution.py
@@ -167,7 +167,7 @@
         table[at] = (part * lax.rsqrt(mean_square + 1e-05) * row).astype(jnp.bfloat16)
 
 
-def project_kernel(acts, table, w_query, w_key, w_value, terms):
+def project_kernel(core, acts, table, w_query, w_key, w_value, mine, others, terms):
     bins, cols = table.shape[0], w_query.shape[1]
     count = acts.shape[1]
     by_bin = lax.broadcasted_iota(jnp.int32, (bins, count), 0)
@@ -178,6 +178,11 @@
     for k, w in enumerate((w_query, w_key, w_value)):
         out = jnp.dot(normed, w[...], preferred_element_type=jnp.float32)
         terms[:, k * cols : (k + 1) * cols] = out.astype(jnp.bfloat16)
+    rows = 16
+    for z in range(count // rows // 2):
+        to = slice(z * rows, (z + 1) * rows)
+        mine[to] = terms[pl.ds(pl.multiple_of((2 * z + core[0]) * rows, rows), rows)]
+        others[to] = terms[pl.ds(pl.multiple_of((2 * z + 1 - core[0]) * rows, rows), rows)]
 
 
 def fetch_kernel(keys_far, keys, sem):
@@ -292,6 +297,7 @@
     core = lax.axis_index("core")
     seqs = lax.axis_size(SEQ)
     groups = lax.axis_size(GRP)
+    depth = lax.axis_size("z")
     robots, true_steps = actions.shape
     steps = 8
     rows = robots * steps
@@ -305,7 +311,7 @@
     array = jax.ShapeDtypeStruct
 
     blocks = w_out[None]
-    arrived = from_partner(blocks, "z", 4)
+    far_block = from_partner(blocks, "z", 4)
     zs = [0, 4]
     zs = zs + [m ^ 2 for m in zs]
     zs = zs + [m ^ 1 for m in zs]
@@ -314,13 +320,11 @@
     acts = exchange(acts, GRP).reshape(groups * robots, true_steps)
     pad_steps = ((0, 0), (0, steps - true_steps))
     acts = jnp.pad(acts, pad_steps).reshape(1, groups * rows)
-    table = call(
+    normalize = lambda *operands: call(
         table_kernel,
         array((bins, feats), jnp.bfloat16),
         [in_smem()] + [far()] * 2,
-        g[None],
-        embed,
-        attn_gain.reshape(-1, HEAD_DIM),
+        *operands,
         scratch=[
             pltpu.VMEM((bins, width), jnp.bfloat16),
             pltpu.VMEM((width // HEAD_DIM, HEAD_DIM), f32),
@@ -328,21 +332,26 @@
         ],
         limit=56,
     )
-    terms = call(
+    table = normalize(g[None], embed, attn_gain.reshape(-1, HEAD_DIM))
+    terms, sent = call(
         project_kernel,
-        array((groups * rows, 3 * cols), jnp.bfloat16),
-        [in_vmem()] * 5,
+        (array((depth * rows, 3 * cols), jnp.bfloat16),) * 2,
+        [in_smem()] + [in_vmem()] * 5,
+        core[None],
         acts,
         table,
         w_query,
         w_key,
         w_value,
+        scratch=[pltpu.VMEM((groups * rows, 3 * cols), jnp.bfloat16)],
         limit=56,
     )
+    arrived = from_partner(sent, "core", 1).astype(f32)
+    terms = (terms.astype(f32) + arrived).astype(jnp.bfloat16)
     terms, lengths, final_gain, head, shard, actions, key_cache = fenced(
         terms, lengths, final_gain, head, s[None], actions, key_cache
     )
-    sums = exchange(terms.reshape(groups, rows, 3 * cols), GRP)
+    sums = exchange(terms.reshape(depth, rows, 3 * cols), "z")
 
     places = (lengths[:, None] + jnp.arange(steps, dtype=jnp.int32)[None, :]).astype(f32)
     half = HEAD_DIM // 2
@@ -354,20 +363,21 @@
     own = (own[:, None] == jnp.arange(bins, dtype=jnp.int32)[None, :]).astype(jnp.bfloat16)
     own_embed = lax.dynamic_slice(embed, (0, s * cols), (bins, cols))
     inputs = jnp.dot(own, own_embed, preferred_element_type=f32)
-    early = call(
+    fetch = lambda cache: call(
         fetch_kernel,
         array(key_cache.shape[1:], key_cache.dtype),
         [far()],
-        key_cache,
+        cache,
         scratch=[pltpu.SemaphoreType.DMA(())],
         limit=50,
     )
+    early = fetch(key_cache)
     own_gain = lax.dynamic_slice(final_gain, (s * cols,), (cols,))[None]
     head_parts = jnp.swapaxes(head.reshape(own_bins, seqs, cols), 0, 1)
     z, core = fenced(z, core, terms)[:2]
     order = (z ^ jnp.array(zs, jnp.int32)) * lax.axis_size("core")
     order = jnp.concatenate([order + core, order + 1 - core])
-    blocks = jnp.concatenate([blocks, arrived], axis=0)
+    blocks = jnp.concatenate([blocks, far_block], axis=0)
     (sums, cosine, sine, inputs, own_gain, head_parts, order, shard, blocks, early) = fenced(
         sums, cosine, sine, inputs, own_gain, head_parts, order, shard, blocks, early
     )

time: 99.2 us -> 98.6 us (level)
  starting transfers between devices: 21.5 us -> 17.2 us
  waiting for transfers between devices: 7.96 us -> 10.6 us
  other arithmetic: 0.38 us -> 2.04 us
    all_to_all x2, starting transfers between devices: 13.4 us -> 9.06 us  [exchange(): return lax.all_to_all(pieces, axis, split_axis=0, concat_axis=0, tiled=True)]
    convert_element_type x0 -> x1, other arithmetic: none -> 1.66 us  [on_device(): terms = (terms.astype(f32) + arrived).astype(jnp.bfloat16)]
    ppermute x4 -> x5, waiting for transfers between devices: 0.01 us -> 1.49 us  [from_partner(): lax.ppermute(x, axis, [(i, i ^ k) for i in range(lax.axis_size(axis))])]
    all_to_all x2, waiting for transfers between devices: 7.95 us -> 9.11 us  [exchange(): return lax.all_to_all(pieces, axis, split_axis=0, concat_axis=0, tiled=True)]
    ppermute x4 -> x5, starting transfers between devices: 8.14 us -> 8.09 us  [from_partner(): lax.ppermute(x, axis, [(i, i ^ k) for i in range(lax.axis_size(axis))])]
  transfers between devices with their start and end apart: 6 -> 7, of which waited for: 1 -> 3; matrix products, arithmetic and copies ran while one was open for 3% -> 4% of each run, Pallas kernels for 13% -> 13%
where the time goes in v8:
time: 98.6 us; the launch traced here: 98 us
  blocking collectives  49.4 us (50%)
  starting transfers between devices  17.2 us (17%)
  Pallas kernels  14.5 us (15%)
  waiting for transfers between devices  10.6 us (11%)
  local copies, waits for them, and re-layouts  3.05 us (3%)
  other arithmetic  2.04 us (2%)
  matrix products  1.09 us (1%)
    all_to_all x4, blocking collectives, exchange(): return lax.all_to_all(pieces, axis, split_axis=0, concat_axis=0, tiled=True)  49.4 us
    pallas_call x8, Pallas kernels, call(): pl.pallas_call(kernel, out_shape=out, in_specs=specs, out_specs=outs, scr...  14.5 us
    all_to_all x2, waiting for transfers between devices, exchange(): return lax.all_to_all(pieces, axis, split_axis=0, concat_axis=0, tiled=True)  9.11 us
    all_to_all x2, starting transfers between devices, exchange(): return lax.all_to_all(pieces, axis, split_axis=0, concat_axis=0, tiled=True)  9.06 us
    ppermute x5, starting transfers between devices, from_partner(): lax.ppermute(x, axis, [(i, i ^ k) for i in range(lax.axis_size(axis))])  8.09 us
  transfers between devices with their start and end apart: 7, of which 3 were waited for; matrix products, arithmetic and copies ran while one was open for 4% of the time, Pallas kernels for 13%

profile of v8, /device:TPU:32, one launch (start us, length us, event | category | flops | bytes accessed | tf_op | source)
XLA Modules:
  0.0 98.0 jit_solution(1021849627941629980)
XLA Ops:
  0.0 6.3 %collective-permute-start.1 = (bf16[1,256,256]{2,1,0:T(8,128)(2,1)}, bf16[1,256,256]{2,1,0:T(8,128)(2,1)S(1)}, u32[]{:S(2)}, u32[]{:S(2)}) collective-permute-start(bf16[1,256,256]{2,1,0:T(8,128)(2,1)} %bitcast.25), channel_id=1, source_target_pairs={{0,8},{2,10},{4,12},{6,14},{8,0},{10,2},{12,4},{14,6},{1,9},{3,11}... | collective-permute-start | bytes 393224 | tf_op jit(solution)/shard_map/ppermute | solution.py:23
  6.3 1.3 %broadcast_in_dim.26 = s32[16,2,7]{2,1,0:T(2,128)} broadcast(s32[2,7]{1,0:T(2,128)} %param.13), dimensions={1,2} | broadcast | bytes 952 | tf_op jit(solution)/shard_map/broadcast_in_dim | solution.py:319
  7.6 4.3 %all-to-all-start = ((s32[16,2,7]{2,1,0:T(2,128)}), s32[16,2,7]{2,1,0:T(2,128)S(1)}, u32[]{:S(2)}, u32[]{:S(2)}) async-start(s32[16,2,7]{2,1,0:T(2,128)} %broadcast_in_dim.26), calls=%async_computation | async-start | bytes 32768 | tf_op jit(solution)/shard_map/all_to_all | solution.py:19
  11.9 2.9 %shard_map.127.table = bf16[256,256]{1,0:T(8,128)(2,1)} custom-call(s32[1]{0:T(128)} %bitcast.2.group, bf16[256,4096]{1,0:T(8,128)(2,1)} %embed_far.1, f32[32,128]{1,0:T(8,128)} %bitcast.28), custom_call_target="tpu_custom_call" | custom-call | tf_op jit(solution)/shard_map/pallas_call | solution.py:44
  14.8 3.4 %all-to-all-done = s32[16,2,7]{2,1,0:T(2,128)S(1)} async-done(((s32[16,2,7]{2,1,0:T(2,128)}), s32[16,2,7]{2,1,0:T(2,128)S(1)}, u32[]{:S(2)}, u32[]{:S(2)}) %all-to-all-start) | async-done | bytes 928 | tf_op jit(solution)/shard_map/all_to_all | solution.py:19
  18.2 0.7 reshape.45.acts
  18.8 2.3 %shard_map.128 = (bf16[128,768]{1,0:T(8,128)(2,1)}, bf16[128,768]{1,0:T(8,128)(2,1)}) custom-call(s32[1]{0:T(128)} %bitcast.core, s32[1,256]{1,0:T(1,128)} %reshape.45.acts, bf16[256,256]{1,0:T(8,128)(2,1)} %shard_map.127.table, bf16[256,256]{1,0:T(8,128)(2,1)} %w_query.1, bf16[256,256]{1,0:T(8,128)(2,1)} %w_key.1, bf16[256,256]{1,0:T(8,128)(2,1)} %w_value.1), custom_call_target="tpu_custom_call" | custom-call | tf_op jit(solution)/shard_map/pallas_call | solution.py:44
  21.3 1.5 %collective-permute-done = bf16[128,768]{1,0:T(8,128)(2,1)S(1)} collective-permute-done((bf16[128,768]{1,0:T(8,128)(2,1)}, bf16[128,768]{1,0:T(8,128)(2,1)S(1)}, u32[]{:S(2)}, u32[]{:S(2)}) %collective-permute-start) | collective-permute-done | bytes 196640 | tf_op jit(solution)/shard_map/ppermute | solution.py:23
  22.8 1.7 %add_convert_fusion = bf16[128,768]{1,0:T(8,128)(2,1)} fusion(bf16[128,768]{1,0:T(8,128)(2,1)S(1)} %collective-permute-done, bf16[128,768]{1,0:T(8,128)(2,1)} %get-tuple-element.37), kind=kLoop, calls=%fused_computation | loop fusion | flops 393216 | bytes 589824 | tf_op jit(solution)/shard_map/convert_element_type | solution.py:350
  24.6 4.8 %all-to-all-start.1 = ((bf16[8,16,768]{2,1,0:T(8,128)(2,1)}), bf16[8,16,768]{2,1,0:T(8,128)(2,1)S(1)}, u32[]{:S(2)}, u32[]{:S(2)}) async-start(bf16[8,16,768]{2,1,0:T(8,128)(2,1)} %bitcast.5), calls=%async_computation.1 | async-start | bytes 393216 | tf_op jit(solution)/shard_map/all_to_all | solution.py:19
  29.7 1.6 %shard_map.129.early = bf16[256,4096]{1,0:T(8,128)(2,1)S(1)} custom-call(bf16[2,256,4096]{2,1,0:T(8,128)(2,1)} %keys_far.1), custom_call_target="tpu_custom_call" | custom-call | tf_op jit(solution)/shard_map/pallas_call | solution.py:44
  31.4 0.8 dynamic_slice.7
  32.2 1.1 %fusion.inputs = f32[16,256]{1,0:T(8,128)S(1)} fusion(bf16[256,4096]{1,0:T(8,128)(2,1)} %embed_far.1, s32[]{:T(128)S(6)} %select_n.4, s32[16]{0:T(128)S(1)} %eq.15), kind=kOutput, calls=%fused_computation.3 | convolution fusion | flops 2101248 | bytes 147524 | tf_op jit(solution)/shard_map/dot_general | solution.py:365
  33.3 5.7 %all-to-all-done.1.sums = bf16[8,16,768]{2,1,0:T(8,128)(2,1)S(1)} async-done(((bf16[8,16,768]{2,1,0:T(8,128)(2,1)}), bf16[8,16,768]{2,1,0:T(8,128)(2,1)S(1)}, u32[]{:S(2)}, u32[]{:S(2)}) %all-to-all-start.1) | async-done | bytes 196640 | tf_op jit(solution)/shard_map/all_to_all | solution.py:19
  39.0 0.3 collective-permute-start.2
  39.4 15.5 %all_to_all.30.spread = bf16[16,32,256]{2,1,0:T(8,128)(2,1)S(1)} all-to-all(bf16[16,32,256]{2,1,0:T(8,128)(2,1)S(1)} %get-tuple-element.57), channel_id=1, replica_groups=mesh['seq_0'=4,'seq_1'=4,'z'=8,'core'=2] {'seq_0','seq_1'}, dimensions={0} | all-to-all | bytes 524288 | tf_op jit(solution)/shard_map/all_to_all | solution.py:19
  55.0 4.6 %shard_map.131 = bf16[16,40,128]{2,1,0:T(8,128)(2,1)S(1)} custom-call(s32[1]{0:T(128)} %bitcast.4.shard, s32[2]{0:T(128)S(1)} %copy-done, bf16[16,32,256]{2,1,0:T(8,128)(2,1)S(1)} %all_to_all.30.spread, bf16[256,4096]{1,0:T(8,128)(2,1)S(1)} %shard_map.129.early, bf16[2,256,4096]{2,1,0:T(8,128)(2,1)} %keys_far.1, bf16[2,256,4096]{2,1,0:T(8,128)(2,1)} %values_far.1), custom_call_target="tpu_custom_call" | custom-call | tf_op jit(solution)/shard_map/pallas_call | solution.py:44
  59.6 1.3 %collective-permute-start.3 = (bf16[4,256,256]{2,1,0:T(8,128)(2,1)S(1)}, bf16[4,256,256]{2,1,0:T(8,128)(2,1)S(1)}, u32[]{:S(2)}, u32[]{:S(2)}) collective-permute-start(bf16[4,256,256]{2,1,0:T(8,128)(2,1)S(1)} %constant_dynamic-update-slice_fusion), channel_id=1, source_target_pairs={{0,2},{2,0},{4,6},{6,4},{8,10},{10,8},{12,14},{14,12},{1,3},{3,1},... | collective-permute-start | bytes 1572872 | tf_op jit(solution)/shard_map/ppermute | solution.py:23
  60.9 11.1 %all_to_all.31.packed = bf16[16,40,128]{2,1,0:T(8,128)(2,1)S(1)} all-to-all(bf16[16,40,128]{2,1,0:T(8,128)(2,1)S(1)} %shard_map.131), channel_id=1, replica_groups=mesh['seq_0'=4,'seq_1'=4,'z'=8,'core'=2] {'seq_0','seq_1'}, dimensions={0} | all-to-all | bytes 327680 | tf_op jit(solution)/shard_map/all_to_all | solution.py:19
  72.0 1.0 %shard_map.132 = bf16[16,16,256]{2,1,0:T(8,128)(2,1)S(1)} custom-call(f32[16,256]{1,0:T(8,128)S(1)} %get-tuple-element.54.query, f32[16,256]{1,0:T(8,128)S(1)} %get-tuple-element.55.key, f32[16,256]{1,0:T(8,128)S(1)} %get-tuple-element.56.value, bf16[16,128]{1,0:T(8,128)(2,1)S(1)} %bitcast.22, bf16[16,40,128]{2,1,0:T(8,128)(2,1)S(1)} %all_to_all.31.packed), custom_call_target="tpu_custom_call" | custom-call | tf_op jit(solution)/shard_map/pallas_call | solution.py:44
  73.2 11.0 %all_to_all.32.blocks = bf16[16,16,256]{2,1,0:T(8,128)(2,1)S(1)} all-to-all(bf16[16,16,256]{2,1,0:T(8,128)(2,1)S(1)} %shard_map.132), channel_id=1, replica_groups=mesh['seq_0'=4,'seq_1'=4,'z'=8,'core'=2] {'seq_0','seq_1'}, dimensions={0} | all-to-all | bytes 262144 | tf_op jit(solution)/shard_map/all_to_all | solution.py:19
  84.2 1.1 %shard_map.133 = f32[16,16,256]{2,1,0:T(8,128)S(1)} custom-call(s32[16]{0:T(128)S(1)} %pad_add_fusion.places, bf16[16,16,256]{2,1,0:T(8,128)(2,1)S(1)} %all_to_all.32.blocks, bf16[8,256,256]{2,1,0:T(8,128)(2,1)S(1)} %constant_dynamic-update-slice_fusion.2.mine, bf16[8,256,256]{2,1,0:T(8,128)(2,1)S(1)} %collective-permute-done.4.other, ...), custom_call_target="tpu_custom_call" | custom-call | tf_op jit(solution)/shard_map/pallas_call | solution.py:44
  85.3 11.8 %all_to_all.33.parts = f32[16,16,256]{2,1,0:T(8,128)S(1)} all-to-all(f32[16,16,256]{2,1,0:T(8,128)S(1)} %shard_map.133), channel_id=1, replica_groups=mesh['seq_0'=4,'seq_1'=4,'z'=8,'core'=2] {'seq_0','seq_1'}, dimensions={0} | all-to-all | bytes 524288 | tf_op jit(solution)/shard_map/all_to_all | solution.py:19
  97.1 0.9 shard_map.134
  (36 shorter events, 1.0 us)
Async XLA Ops:
  0.0 21.3 %copy-start.2 = (bf16[256,256]{1,0:T(8,128)(2,1)S(1)}, bf16[256,256]{1,0:T(8,128)(2,1)}, u32[]{:S(2)}) copy-start(bf16[256,256]{1,0:T(8,128)(2,1)} %param.20) | copy-start | bytes 393220
  0.0 24.4 %copy-start = (s32[2]{0:T(128)S(1)}, s32[2]{0:T(128)}, u32[]{:S(2)}) copy-start(s32[2]{0:T(128)} %lengths) | copy-start | bytes 28
  0.0 21.3 %collective-permute-start.1 = (bf16[1,256,256]{2,1,0:T(8,128)(2,1)}, bf16[1,256,256]{2,1,0:T(8,128)(2,1)S(1)}, u32[]{:S(2)}, u32[]{:S(2)}) collective-permute-start(bf16[1,256,256]{2,1,0:T(8,128)(2,1)} %bitcast.25), channel_id=1, source_target_pairs={{0,8},{2,10},{4,12},{6,14},{8,0},{10,2},{12,4},{14,6},{1,9},{3,11}... | collective-permute-start | bytes 393224 | tf_op jit(solution)/shard_map/ppermute | solution.py:23
  7.6 10.6 %all-to-all-start = ((s32[16,2,7]{2,1,0:T(2,128)}), s32[16,2,7]{2,1,0:T(2,128)S(1)}, u32[]{:S(2)}, u32[]{:S(2)}) async-start(s32[16,2,7]{2,1,0:T(2,128)} %broadcast_in_dim.26), calls=%async_computation | async-start | bytes 32768 | tf_op jit(solution)/shard_map/all_to_all | solution.py:19
  11.9 17.6 %copy-start.4 = (s32[8]{0:T(128)S(1)}, s32[8]{0:T(128)}, u32[]{:S(2)}) copy-start(s32[8]{0:T(128)} %constant.40.clone) | copy-start | bytes 100
  11.9 17.7 %copy-start.3 = (s32[2,7]{1,0:T(2,128)S(1)}, s32[2,7]{1,0:T(2,128)}, u32[]{:S(2)}) copy-start(s32[2,7]{1,0:T(2,128)} %param.13) | copy-start | bytes 172
  21.1 1.7 %collective-permute-start = (bf16[128,768]{1,0:T(8,128)(2,1)}, bf16[128,768]{1,0:T(8,128)(2,1)S(1)}, u32[]{:S(2)}, u32[]{:S(2)}) collective-permute-start(bf16[128,768]{1,0:T(8,128)(2,1)} %get-tuple-element.38), channel_id=1, source_target_pairs={{0,1},{1,0},{2,3},{3,2},{4,5},{5,4},{6,7},{7,6},{8,9},{9,8},{10,11... | collective-permute-start | bytes 589832 | tf_op jit(solution)/shard_map/ppermute | solution.py:23
  24.6 14.4 %all-to-all-start.1 = ((bf16[8,16,768]{2,1,0:T(8,128)(2,1)}), bf16[8,16,768]{2,1,0:T(8,128)(2,1)S(1)}, u32[]{:S(2)}, u32[]{:S(2)}) async-start(bf16[8,16,768]{2,1,0:T(8,128)(2,1)} %bitcast.5), calls=%async_computation.1 | async-start | bytes 393216 | tf_op jit(solution)/shard_map/all_to_all | solution.py:19
  29.7 1.6 %copy-start.1 = (bf16[16,4096]{1,0:T(8,128)(2,1)S(1)}, bf16[16,4096]{1,0:T(8,128)(2,1)}, u32[]{:S(2)}) copy-start(bf16[16,4096]{1,0:T(8,128)(2,1)} %param.24) | copy-start | bytes 393220
  39.0 20.6 %collective-permute-start.2 = (bf16[2,256,256]{2,1,0:T(8,128)(2,1)S(1)}, bf16[2,256,256]{2,1,0:T(8,128)(2,1)S(1)}, u32[]{:S(2)}, u32[]{:S(2)}) collective-permute-start(bf16[2,256,256]{2,1,0:T(8,128)(2,1)S(1)} %pad_maximum_fusion), channel_id=1, source_target_pairs={{0,4},{2,6},{4,0},{6,2},{8,12},{10,14},{12,8},{14,10},{1,5},{3,7},... | collective-permute-start | bytes 786440 | tf_op jit(solution)/shard_map/ppermute | solution.py:23
  59.6 13.4 %collective-permute-start.3 = (bf16[4,256,256]{2,1,0:T(8,128)(2,1)S(1)}, bf16[4,256,256]{2,1,0:T(8,128)(2,1)S(1)}, u32[]{:S(2)}, u32[]{:S(2)}) collective-permute-start(bf16[4,256,256]{2,1,0:T(8,128)(2,1)S(1)} %constant_dynamic-update-slice_fusion), channel_id=1, source_target_pairs={{0,2},{2,0},{4,6},{6,4},{8,10},{10,8},{12,14},{14,12},{1,3},{3,1},... | collective-permute-start | bytes 1572872 | tf_op jit(solution)/shard_map/ppermute | solution.py:23
  73.1 11.1 %collective-permute-start.4 = (bf16[8,256,256]{2,1,0:T(8,128)(2,1)S(1)}, bf16[8,256,256]{2,1,0:T(8,128)(2,1)S(1)}, u32[]{:S(2)}, u32[]{:S(2)}) collective-permute-start(bf16[8,256,256]{2,1,0:T(8,128)(2,1)S(1)} %constant_dynamic-update-slice_fusion.2.mine), channel_id=1, source_target_pairs={{0,1},{1,0},{2,3},{3,2},{4,5},{5,4},{6,7},{7,6},{8,9},{9,8},{10,11... | collective-permute-start | bytes 3145736 | tf_op jit(solution)/shard_map/ppermute | solution.py:23

commit v9 on v8

--- a/solution.py
+++ b/solution.py
@@ -167,17 +167,16 @@
         table[at] = (part * lax.rsqrt(mean_square + 1e-05) * row).astype(jnp.bfloat16)
 
 
-def project_kernel(core, acts, table, w_query, w_key, w_value, mine, others, terms):
-    bins, cols = table.shape[0], w_query.shape[1]
+def project_kernel(core, acts, table, weights, mine, others, terms):
+    bins = table.shape[0]
     count = acts.shape[1]
     by_bin = lax.broadcasted_iota(jnp.int32, (bins, count), 0)
     hot = jnp.where(by_bin == acts[...], 1.0, 0.0).astype(jnp.bfloat16)
     normed = lax.dot_general(
         hot, table[...], (((0,), (0,)), ((), ())), preferred_element_type=jnp.float32
     ).astype(jnp.bfloat16)
-    for k, w in enumerate((w_query, w_key, w_value)):
-        out = jnp.dot(normed, w[...], preferred_element_type=jnp.float32)
-        terms[:, k * cols : (k + 1) * cols] = out.astype(jnp.bfloat16)
+    out = jnp.dot(normed, weights[...], preferred_element_type=jnp.float32)
+    terms[...] = out.astype(jnp.bfloat16)
     rows = 16
     for z in range(count // rows // 2):
         to = slice(z * rows, (z + 1) * rows)
@@ -316,6 +315,8 @@
     zs = zs + [m ^ 2 for m in zs]
     zs = zs + [m ^ 1 for m in zs]
 
+    weights = jnp.concatenate([w_query, w_key, w_value], axis=1)
+
     acts = jnp.broadcast_to(actions[None], (groups, robots, true_steps))
     acts = exchange(acts, GRP).reshape(groups * robots, true_steps)
     pad_steps = ((0, 0), (0, steps - true_steps))
@@ -330,21 +331,19 @@
             pltpu.VMEM((width // HEAD_DIM, HEAD_DIM), f32),
             pltpu.SemaphoreType.DMA((5,)),
         ],
-        limit=56,
+        limit=53,
     )
     table = normalize(g[None], embed, attn_gain.reshape(-1, HEAD_DIM))
     terms, sent = call(
         project_kernel,
         (array((depth * rows, 3 * cols), jnp.bfloat16),) * 2,
-        [in_smem()] + [in_vmem()] * 5,
+        [in_smem()] + [in_vmem()] * 3,
         core[None],
         acts,
         table,
-        w_query,
-        w_key,
-        w_value,
+        weights,
         scratch=[pltpu.VMEM((groups * rows, 3 * cols), jnp.bfloat16)],
-        limit=56,
+        limit=12,
     )
     arrived = from_partner(sent, "core", 1).astype(f32)
     terms = (terms.astype(f32) + arrived).astype(jnp.bfloat16)

time: 98.6 us -> 98.4 us (level)
  starting transfers between devices: 17.2 us -> 21.1 us
  Pallas kernels: 14.5 us -> 11.8 us
  waiting for transfers between devices: 10.6 us -> 8.81 us
    all_to_all x2, starting transfers between devices: 9.06 us -> 14.9 us  [exchange(): return lax.all_to_all(pieces, axis, split_axis=0, concat_axis=0, tiled=True)]
    all_to_all x2, waiting for transfers between devices: 9.11 us -> 5.28 us  [exchange(): return lax.all_to_all(pieces, axis, split_axis=0, concat_axis=0, tiled=True)]
    pallas_call x8, Pallas kernels: 14.5 us -> 11.8 us  [call(): pl.pallas_call(kernel, out_shape=out, in_specs=specs, out_specs=outs, scr...]
    ppermute x5, waiting for transfers between devices: 1.49 us -> 3.53 us  [from_partner(): lax.ppermute(x, axis, [(i, i ^ k) for i in range(lax.axis_size(axis))])]
    ppermute x5, starting transfers between devices: 8.09 us -> 6.21 us  [from_partner(): lax.ppermute(x, axis, [(i, i ^ k) for i in range(lax.axis_size(axis))])]
    concatenate x0 -> x1, other arithmetic: none -> 1.06 us  [on_device(): weights = jnp.concatenate([w_query, w_key, w_value], axis=1)]
  transfers between devices with their start and end apart: 7 -> 7, of which waited for: 3 -> 2; matrix products, arithmetic and copies ran while one was open for 4% -> 4% of each run, Pallas kernels for 13% -> 10%
where the time goes in v9:
time: 98.4 us; the launch traced here: 97.8 us
  blocking collectives  49.4 us (50%)
  starting transfers between devices  21.1 us (21%)
  Pallas kernels  11.8 us (12%)
  waiting for transfers between devices  8.81 us (9%)
  local copies, waits for them, and re-layouts  3.22 us (3%)
  other arithmetic  2.17 us (2%)
  matrix products  1.09 us (1%)
    all_to_all x4, blocking collectives, exchange(): return lax.all_to_all(pieces, axis, split_axis=0, concat_axis=0, tiled=True)  49.4 us
    all_to_all x2, starting transfers between devices, exchange(): return lax.all_to_all(pieces, axis, split_axis=0, concat_axis=0, tiled=True)  14.9 us
    pallas_call x8, Pallas kernels, call(): pl.pallas_call(kernel, out_shape=out, in_specs=specs, out_specs=outs, scr...  11.8 us
    ppermute x5, starting transfers between devices, from_partner(): lax.ppermute(x, axis, [(i, i ^ k) for i in range(lax.axis_size(axis))])  6.21 us
    all_to_all x2, waiting for transfers between devices, exchange(): return lax.all_to_all(pieces, axis, split_axis=0, concat_axis=0, tiled=True)  5.28 us
    ppermute x5, waiting for transfers between devices, from_partner(): lax.ppermute(x, axis, [(i, i ^ k) for i in range(lax.axis_size(axis))])  3.53 us
  transfers between devices with their start and end apart: 7, of which 2 were waited for; matrix products, arithmetic and copies ran while one was open for 4% of the time, Pallas kernels for 10%

profile of v9, /device:TPU:32, one launch (start us, length us, event | category | flops | bytes accessed | tf_op | source)
XLA Modules:
  0.0 97.8 jit_solution(2776320444905763671)
XLA Ops:
  0.0 1.3 %broadcast_in_dim.26 = s32[16,2,7]{2,1,0:T(2,128)} broadcast(s32[2,7]{1,0:T(2,128)} %param.13), dimensions={1,2} | broadcast | bytes 952 | tf_op jit(solution)/shard_map/broadcast_in_dim | solution.py:320
  1.3 8.6 %all-to-all-start = ((s32[16,2,7]{2,1,0:T(2,128)}), s32[16,2,7]{2,1,0:T(2,128)S(1)}, u32[]{:S(2)}, u32[]{:S(2)}) async-start(s32[16,2,7]{2,1,0:T(2,128)} %broadcast_in_dim.26), calls=%async_computation | async-start | bytes 32768 | tf_op jit(solution)/shard_map/all_to_all | solution.py:19
  9.9 4.5 %collective-permute-start.1 = (bf16[1,256,256]{2,1,0:T(8,128)(2,1)}, bf16[1,256,256]{2,1,0:T(8,128)(2,1)S(1)}, u32[]{:S(2)}, u32[]{:S(2)}) collective-permute-start(bf16[1,256,256]{2,1,0:T(8,128)(2,1)} %bitcast.26), channel_id=1, source_target_pairs={{0,8},{2,10},{4,12},{6,14},{8,0},{10,2},{12,4},{14,6},{1,9},{3,11}... | collective-permute-start | bytes 393224 | tf_op jit(solution)/shard_map/ppermute | solution.py:23
  14.4 1.1 %pad_maximum_fusion.weights = bf16[256,768]{1,0:T(8,128)(2,1)S(1)} fusion(bf16[256,256]{1,0:T(8,128)(2,1)} %param.19, bf16[256,256]{1,0:T(8,128)(2,1)} %param.18, bf16[256,256]{1,0:T(8,128)(2,1)} %param.17), kind=kLoop, calls=%fused_computation | loop fusion | flops 1179648 | bytes 786432 | tf_op jit(solution)/shard_map/concatenate | solution.py:318
  15.5 0.7 copy-done
  16.2 1.9 %shard_map.127.table = bf16[256,256]{1,0:T(8,128)(2,1)S(1)} custom-call(s32[1]{0:T(128)} %bitcast.2.group, bf16[256,4096]{1,0:T(8,128)(2,1)} %embed_far.1, f32[32,128]{1,0:T(8,128)S(1)} %bitcast.22), custom_call_target="tpu_custom_call" | custom-call | tf_op jit(solution)/shard_map/pallas_call | solution.py:44
  18.2 0.5 shard_map.128
  18.8 3.5 %collective-permute-done.1 = bf16[1,256,256]{2,1,0:T(8,128)(2,1)S(1)} collective-permute-done((bf16[1,256,256]{2,1,0:T(8,128)(2,1)}, bf16[1,256,256]{2,1,0:T(8,128)(2,1)S(1)}, u32[]{:S(2)}, u32[]{:S(2)}) %collective-permute-start.1) | collective-permute-done | bytes 131104 | tf_op jit(solution)/shard_map/ppermute | solution.py:23
  22.4 0.7 add_convert_fusion
  23.3 6.3 %all-to-all-start.1 = ((bf16[8,16,768]{2,1,0:T(8,128)(2,1)}), bf16[8,16,768]{2,1,0:T(8,128)(2,1)S(1)}, u32[]{:S(2)}, u32[]{:S(2)}) async-start(bf16[8,16,768]{2,1,0:T(8,128)(2,1)} %bitcast.5), calls=%async_computation.1 | async-start | bytes 393216 | tf_op jit(solution)/shard_map/all_to_all | solution.py:19
  29.9 1.6 %shard_map.129.early = bf16[256,4096]{1,0:T(8,128)(2,1)S(1)} custom-call(bf16[2,256,4096]{2,1,0:T(8,128)(2,1)} %keys_far.1), custom_call_target="tpu_custom_call" | custom-call | tf_op jit(solution)/shard_map/pallas_call | solution.py:44
  31.6 0.8 dynamic_slice.7
  32.4 1.1 %fusion.inputs = f32[16,256]{1,0:T(8,128)S(1)} fusion(bf16[256,4096]{1,0:T(8,128)(2,1)} %embed_far.1, s32[]{:T(128)S(6)} %select_n.4, s32[16]{0:T(128)S(1)} %eq.15), kind=kOutput, calls=%fused_computation.4 | convolution fusion | flops 2101248 | bytes 147524 | tf_op jit(solution)/shard_map/dot_general | solution.py:364
  33.5 5.3 %all-to-all-done.1.sums = bf16[8,16,768]{2,1,0:T(8,128)(2,1)S(1)} async-done(((bf16[8,16,768]{2,1,0:T(8,128)(2,1)}), bf16[8,16,768]{2,1,0:T(8,128)(2,1)S(1)}, u32[]{:S(2)}, u32[]{:S(2)}) %all-to-all-start.1) | async-done | bytes 196640 | tf_op jit(solution)/shard_map/all_to_all | solution.py:19
  38.8 0.4 collective-permute-start.2
  39.3 15.5 %all_to_all.30.spread = bf16[16,32,256]{2,1,0:T(8,128)(2,1)S(1)} all-to-all(bf16[16,32,256]{2,1,0:T(8,128)(2,1)S(1)} %get-tuple-element.57), channel_id=1, replica_groups=mesh['seq_0'=4,'seq_1'=4,'z'=8,'core'=2] {'seq_0','seq_1'}, dimensions={0} | all-to-all | bytes 524288 | tf_op jit(solution)/shard_map/all_to_all | solution.py:19
  54.8 4.6 %shard_map.131 = bf16[16,40,128]{2,1,0:T(8,128)(2,1)S(1)} custom-call(s32[1]{0:T(128)} %bitcast.4.shard, s32[2]{0:T(128)S(1)} %copy-done.1, bf16[16,32,256]{2,1,0:T(8,128)(2,1)S(1)} %all_to_all.30.spread, bf16[256,4096]{1,0:T(8,128)(2,1)S(1)} %shard_map.129.early, bf16[2,256,4096]{2,1,0:T(8,128)(2,1)} %keys_far.1, bf16[2,256,4096]{2,1,0:T(8,128)(2,1)} %values_far.1), custom_call_target="tpu_custom_call" | custom-call | tf_op jit(solution)/shard_map/pallas_call | solution.py:44
  59.5 1.1 %collective-permute-start.3 = (bf16[4,256,256]{2,1,0:T(8,128)(2,1)S(1)}, bf16[4,256,256]{2,1,0:T(8,128)(2,1)S(1)}, u32[]{:S(2)}, u32[]{:S(2)}) collective-permute-start(bf16[4,256,256]{2,1,0:T(8,128)(2,1)S(1)} %constant_dynamic-update-slice_fusion), channel_id=1, source_target_pairs={{0,2},{2,0},{4,6},{6,4},{8,10},{10,8},{12,14},{14,12},{1,3},{3,1},... | collective-permute-start | bytes 1572872 | tf_op jit(solution)/shard_map/ppermute | solution.py:23
  60.6 11.1 %all_to_all.31.packed = bf16[16,40,128]{2,1,0:T(8,128)(2,1)S(1)} all-to-all(bf16[16,40,128]{2,1,0:T(8,128)(2,1)S(1)} %shard_map.131), channel_id=1, replica_groups=mesh['seq_0'=4,'seq_1'=4,'z'=8,'core'=2] {'seq_0','seq_1'}, dimensions={0} | all-to-all | bytes 327680 | tf_op jit(solution)/shard_map/all_to_all | solution.py:19
  71.7 1.0 %shard_map.132 = bf16[16,16,256]{2,1,0:T(8,128)(2,1)S(1)} custom-call(f32[16,256]{1,0:T(8,128)S(1)} %get-tuple-element.54.query, f32[16,256]{1,0:T(8,128)S(1)} %get-tuple-element.55.key, f32[16,256]{1,0:T(8,128)S(1)} %get-tuple-element.56.value, bf16[16,128]{1,0:T(8,128)(2,1)S(1)} %bitcast.23, bf16[16,40,128]{2,1,0:T(8,128)(2,1)S(1)} %all_to_all.31.packed), custom_call_target="tpu_custom_call" | custom-call | tf_op jit(solution)/shard_map/pallas_call | solution.py:44
  72.9 11.0 %all_to_all.32.blocks = bf16[16,16,256]{2,1,0:T(8,128)(2,1)S(1)} all-to-all(bf16[16,16,256]{2,1,0:T(8,128)(2,1)S(1)} %shard_map.132), channel_id=1, replica_groups=mesh['seq_0'=4,'seq_1'=4,'z'=8,'core'=2] {'seq_0','seq_1'}, dimensions={0} | all-to-all | bytes 262144 | tf_op jit(solution)/shard_map/all_to_all | solution.py:19
  83.9 1.1 %shard_map.133 = f32[16,16,256]{2,1,0:T(8,128)S(1)} custom-call(s32[16]{0:T(128)S(1)} %pad_add_fusion.places, bf16[16,16,256]{2,1,0:T(8,128)(2,1)S(1)} %all_to_all.32.blocks, bf16[8,256,256]{2,1,0:T(8,128)(2,1)S(1)} %constant_dynamic-update-slice_fusion.2.mine, bf16[8,256,256]{2,1,0:T(8,128)(2,1)S(1)} %collective-permute-done.4.other, ...), custom_call_target="tpu_custom_call" | custom-call | tf_op jit(solution)/shard_map/pallas_call | solution.py:44
  85.0 11.8 %all_to_all.33.parts = f32[16,16,256]{2,1,0:T(8,128)S(1)} all-to-all(f32[16,16,256]{2,1,0:T(8,128)S(1)} %shard_map.133), channel_id=1, replica_groups=mesh['seq_0'=4,'seq_1'=4,'z'=8,'core'=2] {'seq_0','seq_1'}, dimensions={0} | all-to-all | bytes 524288 | tf_op jit(solution)/shard_map/all_to_all | solution.py:19
  96.8 0.9 shard_map.134
  (39 shorter events, 1.1 us)
Async XLA Ops:
  0.0 22.4 %copy-start.3 = (bf16[256,256]{1,0:T(8,128)(2,1)S(1)}, bf16[256,256]{1,0:T(8,128)(2,1)}, u32[]{:S(2)}) copy-start(bf16[256,256]{1,0:T(8,128)(2,1)} %param.20) | copy-start | bytes 393220
  1.3 16.8 %all-to-all-start = ((s32[16,2,7]{2,1,0:T(2,128)}), s32[16,2,7]{2,1,0:T(2,128)S(1)}, u32[]{:S(2)}, u32[]{:S(2)}) async-start(s32[16,2,7]{2,1,0:T(2,128)} %broadcast_in_dim.26), calls=%async_computation | async-start | bytes 32768 | tf_op jit(solution)/shard_map/all_to_all | solution.py:19
  9.9 12.4 %collective-permute-start.1 = (bf16[1,256,256]{2,1,0:T(8,128)(2,1)}, bf16[1,256,256]{2,1,0:T(8,128)(2,1)S(1)}, u32[]{:S(2)}, u32[]{:S(2)}) collective-permute-start(bf16[1,256,256]{2,1,0:T(8,128)(2,1)} %bitcast.26), channel_id=1, source_target_pairs={{0,8},{2,10},{4,12},{6,14},{8,0},{10,2},{12,4},{14,6},{1,9},{3,11}... | collective-permute-start | bytes 393224 | tf_op jit(solution)/shard_map/ppermute | solution.py:23
  15.4 7.7 %copy-start.1 = (s32[2]{0:T(128)S(1)}, s32[2]{0:T(128)}, u32[]{:S(2)}) copy-start(s32[2]{0:T(128)} %lengths) | copy-start | bytes 28
  15.5 0.7 copy-start
  16.2 13.5 %copy-start.5 = (s32[8]{0:T(128)S(1)}, s32[8]{0:T(128)}, u32[]{:S(2)}) copy-start(s32[8]{0:T(128)} %constant.40.clone) | copy-start | bytes 100
  16.2 13.6 %copy-start.4 = (s32[2,7]{1,0:T(2,128)S(1)}, s32[2,7]{1,0:T(2,128)}, u32[]{:S(2)}) copy-start(s32[2,7]{1,0:T(2,128)} %param.13) | copy-start | bytes 172
  18.7 3.7 %collective-permute-start = (bf16[128,768]{1,0:T(8,128)(2,1)S(1)}, bf16[128,768]{1,0:T(8,128)(2,1)S(1)}, u32[]{:S(2)}, u32[]{:S(2)}) collective-permute-start(bf16[128,768]{1,0:T(8,128)(2,1)S(1)} %get-tuple-element.38), channel_id=1, source_target_pairs={{0,1},{1,0},{2,3},{3,2},{4,5},{5,4},{6,7},{7,6},{8,9},{9,8},{10,11... | collective-permute-start | bytes 589832 | tf_op jit(solution)/shard_map/ppermute | solution.py:23
  23.3 15.5 %all-to-all-start.1 = ((bf16[8,16,768]{2,1,0:T(8,128)(2,1)}), bf16[8,16,768]{2,1,0:T(8,128)(2,1)S(1)}, u32[]{:S(2)}, u32[]{:S(2)}) async-start(bf16[8,16,768]{2,1,0:T(8,128)(2,1)} %bitcast.5), calls=%async_computation.1 | async-start | bytes 393216 | tf_op jit(solution)/shard_map/all_to_all | solution.py:19
  29.9 1.6 %copy-start.2 = (bf16[16,4096]{1,0:T(8,128)(2,1)S(1)}, bf16[16,4096]{1,0:T(8,128)(2,1)}, u32[]{:S(2)}) copy-start(bf16[16,4096]{1,0:T(8,128)(2,1)} %param.24) | copy-start | bytes 393220
  38.8 20.7 %collective-permute-start.2 = (bf16[2,256,256]{2,1,0:T(8,128)(2,1)S(1)}, bf16[2,256,256]{2,1,0:T(8,128)(2,1)S(1)}, u32[]{:S(2)}, u32[]{:S(2)}) collective-permute-start(bf16[2,256,256]{2,1,0:T(8,128)(2,1)S(1)} %pad_maximum_fusion.1), channel_id=1, source_target_pairs={{0,4},{2,6},{4,0},{6,2},{8,12},{10,14},{12,8},{14,10},{1,5},{3,7},... | collective-permute-start | bytes 786440 | tf_op jit(solution)/shard_map/ppermute | solution.py:23
  59.5 13.2 %collective-permute-start.3 = (bf16[4,256,256]{2,1,0:T(8,128)(2,1)S(1)}, bf16[4,256,256]{2,1,0:T(8,128)(2,1)S(1)}, u32[]{:S(2)}, u32[]{:S(2)}) collective-permute-start(bf16[4,256,256]{2,1,0:T(8,128)(2,1)S(1)} %constant_dynamic-update-slice_fusion), channel_id=1, source_target_pairs={{0,2},{2,0},{4,6},{6,4},{8,10},{10,8},{12,14},{14,12},{1,3},{3,1},... | collective-permute-start | bytes 1572872 | tf_op jit(solution)/shard_map/ppermute | solution.py:23
  72.8 11.1 %collective-permute-start.4 = (bf16[8,256,256]{2,1,0:T(8,128)(2,1)S(1)}, bf16[8,256,256]{2,1,0:T(8,128)(2,1)S(1)}, u32[]{:S(2)}, u32[]{:S(2)}) collective-permute-start(bf16[8,256,256]{2,1,0:T(8,128)(2,1)S(1)} %constant_dynamic-update-slice_fusion.2.mine), channel_id=1, source_target_pairs={{0,1},{1,0},{2,3},{3,2},{4,5},{5,4},{6,7},{7,6},{8,9},{9,8},{10,11... | collective-permute-start | bytes 3145736 | tf_op jit(solution)/shard_map/ppermute | solution.py:23
